TPU v7x, 256 devices: a whole 4x4x8 slice. The times are simulated.
256 devices in a mesh: gx: 8 (over z), gy: 8 (over y, core), gz: 4 (over x).
Axes of the slice: x: 4, y: 4, z: 8, core: 2. Of those that a mesh axis runs over, the one named last changes fastest.
Arguments:
- iterate: float32 [64, 128, 512], P('gx', 'gy', 'gz'), may hold values from -6 to 6
- source: float32 [64, 128, 512], P('gx', 'gy', 'gz'), may hold values from -6 to 6
- reaction: float32 [64, 128, 512], P('gx', 'gy', 'gz'), may hold values from 0.05 to 1
- trial_powers: int32 [4], replicated, may hold values from 0 to 5
Outputs:
- newton_dir: float32 [64, 128, 512], P('gx', 'gy', 'gz')
- remnant: float32 [64, 128, 512], P('gx', 'gy', 'gz')
- layer_energies: float32 [4, 64], P(None, 'gx')
- energies: float32 [4], replicated
Inputs may be any that keep to these rules, and one draw needn't show every extreme that they name: `trial_powers`: trial k takes the step length 2 to the power minus entry k.
All inputs are finite; a program needn't handle non-finite values.
Results may differ from a plain program's by a relative error of at most 0.0003.
Values sent between devices are 32-bit elements; how exact they have to be, the bound alone decides.
No kernel may reach another device: no remote copies, remote signals or barrier semaphores. Data moves between devices by JAX's collectives and lax.ppermute only.
A program may use at most 128 MiB of HBM per device.

v0:
```python
import jax
import jax.numpy as jnp
from jax import lax
from jax.experimental import pallas as pl
from jax.experimental.pallas import tpu as pltpu
from jax.sharding import Mesh
from jax.sharding import PartitionSpec as P

ITERS = 4
TRIALS = 4
ALL = ("gx", "gy_0", "gy_1", "gz")
GY = ("gy_0", "gy_1")
NGX, NGY, NGZ = 8, 8, 4
NDEV = 256
NZB = 32
NX, NY, NZ = 64, 128, 512
M = 12
B = 16
NB = 40
F32 = jnp.float32
INTERPRET = False

THETA = 1.15
DELTA = 0.85
SIGMA = THETA / DELTA
RHO0 = 1.0 / SIGMA
RHO1 = 1.0 / (2.0 * SIGMA - RHO0)
RHO2 = 1.0 / (2.0 * SIGMA - RHO1)
C1U = RHO1 * RHO0
C1R = 2.0 * RHO1 / DELTA
C2U = RHO2 * RHO1
C2R = 2.0 * RHO2 / DELTA


def roll(v, shift, axis):
    return pltpu.roll(v, shift % v.shape[axis], axis)


def up_z(v, s=1):
    return roll(v, -s, 0)


def dn_z(v, s=1):
    return roll(v, s, 0)


def up_x(v, s=1):
    return roll(v, -s, 1)


def dn_x(v, s=1):
    return roll(v, s, 1)


def ziota():
    return lax.broadcasted_iota(jnp.int32, (NB, 128), 0)


def xiota():
    return lax.broadcasted_iota(jnp.int32, (NB, 128), 1)


def even(iota, s):
    return (iota // s) % 2 == 0


def sum_z(v, s):
    return v + jnp.where(even(ziota(), s), up_z(v, s), dn_z(v, s))


def sum_x(v, s):
    return v + jnp.where(even(xiota(), s), up_x(v, s), dn_x(v, s))


def odd_z(v, s):
    return jnp.where(even(ziota(), s), up_z(v, s), v)


def odd_x(v, s):
    return jnp.where(even(xiota(), s), up_x(v, s), v)


class Level:
    def __init__(self, wx, wy, wz, c, dinv, s):
        self.wx, self.wy, self.wz, self.c, self.dinv, self.s = wx, wy, wz, c, dinv, s

    def y_flux(self, y, low, high):
        return self.wy[y] * (high - low)

    def apply(self, y, u, high, flux_low):
        s = self.s
        flux_y = self.wy[y] * (high - u)
        flux_x = self.wx[y] * (up_x(u, s) - u)
        flux_z = self.wz[y] * (up_z(u, s) - u)
        image = self.c[y] * u - ((flux_x - dn_x(flux_x, s)) + (flux_y - flux_low) + (flux_z - dn_z(flux_z, s)))
        return image, flux_y


def sweep(level, lo, hi, field, store):
    first = field(lo)
    flux = level.y_flux(lo - 1, field(lo - 1), first)

    def row(y, carry):
        u, flux_low = carry
        high = field(y + 1)
        image, flux_y = level.apply(y, u, high, flux_low)
        store(y, u, image)
        return high, flux_y

    lax.fori_loop(lo, hi, row, (first, flux))


def smooth_down(level, lo, hi, r, r1, u1, x, finish):
    def start(y):
        return level.dinv[y] * r[y] / THETA

    def first(y, u, image):
        rest = r[y] - image
        r1[y] = rest
        after = C1U * u + C1R * (level.dinv[y] * rest)
        u1[y] = after
        x[y] = u + after

    sweep(level, lo, hi, start, first)
    sweep(level, lo + 1, hi - 1, lambda y: u1[y], lambda y, u, image: finish(y, r1[y] - image))


def smooth_up(level, lo, hi, e, r2, r3, u, x, finish):
    def first(y, own, image):
        rest = r2[y] - image
        r3[y] = rest
        u[y] = level.dinv[y] * rest / THETA

    sweep(level, lo, hi, e, first)

    def second(y, own, image):
        rest = r3[y] - image
        after = C1U * own + C1R * (level.dinv[y] * rest)
        finish(y, (x[y] + e(y)) + (own + after))

    sweep(level, lo + 1, hi - 1, lambda y: u[y], second)


def down(fine, mid, r, r1, u1, x, r2, b1, r1m, u1m, xm, r2m, b2):
    def keep(y, rest):
        r2[y] = rest

    smooth_down(fine, 3, 37, r, r1, u1, x, keep)

    def restrict(y, carry):
        b1[y] = sum_x(sum_z(r2[2 * y] + r2[2 * y + 1], 1), 1)
        return carry

    lax.fori_loop(2, 18, restrict, 0)

    def keep_mid(y, rest):
        r2m[y] = rest

    smooth_down(mid, 3, 17, b1, r1m, u1m, xm, keep_mid)
    for k in range(4):
        b2[k] = sum_x(sum_z(r2m[2 * k + 6] + r2m[2 * k + 7], 2), 2)


def setup_kernel(pos, it, src, rea, wx, wy, wz, c, dinv, wx1, wy1, wz1, c1, dinv1, r, x, r2, xm, r2m, pay, r1, u1, b1, r1m, u1m):
    gy, zb = pos[0], pos[1]
    zg = ziota() + (zb * B - M)
    lane = xiota()
    inside_zx = (zg >= 0) & (zg < NZ) & (lane < NX)

    def weight(g):
        square = g * g
        root = jnp.sqrt(1.0 + square)
        return (1.0 + 2.0 * square) / root, g * root

    def row(y, carry):
        flow_low, wy_low, wym_low = carry
        yg = gy * B - M + y
        here, high = it[y], it[y + 1]
        w_x, p_x = weight(up_x(here) - here)
        w_y, p_y = weight(high - here)
        w_z, p_z = weight(up_z(here) - here)
        inside = inside_zx & (yg >= 0) & (yg < NY)
        rest = src[y] - rea[y] * here + ((p_x - dn_x(p_x)) + (p_y - flow_low) + (p_z - dn_z(p_z)))
        r[y] = jnp.where(inside, rest, 0.0)
        outer = rea[y] + jnp.where(lane == 0, dn_x(w_x), 0.0) + jnp.where(lane == NX - 1, w_x, 0.0)
        outer = outer + jnp.where(zg == 0, dn_z(w_z), 0.0) + jnp.where(zg == NZ - 1, w_z, 0.0)
        outer = outer + jnp.where(yg == 0, wy_low, 0.0) + jnp.where(yg == NY - 1, w_y, 0.0)
        outer = jnp.where(inside, outer, 0.0)
        m_x = jnp.where(inside & (lane < NX - 1), w_x, 0.0)
        m_y = jnp.where(inside & (yg < NY - 1), w_y, 0.0)
        m_z = jnp.where(inside & (zg < NZ - 1), w_z, 0.0)
        wx[y], wy[y], wz[y], c[y] = m_x, m_y, m_z, outer
        diagonal = outer + m_x + dn_x(m_x) + m_y + wym_low + m_z + dn_z(m_z)
        good = diagonal > 0.0
        dinv[y] = jnp.where(good, 1.0 / jnp.where(good, diagonal, 1.0), 0.0)
        return p_y, w_y, m_y

    zero = jnp.zeros((NB, 128), F32)
    lax.fori_loop(0, NB - 1, row, (zero, zero, zero))
    for ref in (wx, wy, wz, c, dinv, r):
        ref[NB - 1] = zero

    def row1(y, low):
        a, b = 2 * y, 2 * y + 1
        m_x = sum_z(odd_x(wx[a] + wx[b], 1), 1)
        m_y = sum_x(sum_z(wy[b], 1), 1)
        m_z = sum_x(odd_z(wz[a] + wz[b], 1), 1)
        m_c = sum_x(sum_z(c[a] + c[b], 1), 1)
        wx1[y], wy1[y], wz1[y], c1[y] = m_x, m_y, m_z, m_c
        diagonal = m_c + m_x + dn_x(m_x, 2) + m_y + low + m_z + dn_z(m_z, 2)
        good = diagonal > 0.0
        dinv1[y] = jnp.where(good, 1.0 / jnp.where(good, diagonal, 1.0), 0.0)
        return m_y

    lax.fori_loop(0, NB // 2, row1, zero)
    fine = Level(wx, wy, wz, c, dinv, 1)
    mid = Level(wx1, wy1, wz1, c1, dinv1, 2)

    class Part:
        def __setitem__(self, k, value):
            pay[k] = value

    down(fine, mid, r, r1, u1, x, r2, b1, r1m, u1m, xm, r2m, Part())
    for k in range(4):
        a, b = 2 * k + 6, 2 * k + 7
        pay[4 + k] = sum_z(odd_x(wx1[a] + wx1[b], 2), 2)
        pay[8 + k] = sum_x(sum_z(wy1[b], 2), 2)
        pay[12 + k] = sum_x(odd_z(wz1[a] + wz1[b], 2), 2)
        pay[16 + k] = sum_x(sum_z(c1[a] + c1[b], 2), 2)


def lane_ids():
    return lax.broadcasted_iota(jnp.int32, (16, NDEV), 1)


def next_z(v):
    return jnp.where(lane_ids() < 224, roll(v, -32, 1), roll(v, 223, 1))


def prev_z(v):
    lanes = lane_ids()
    return jnp.where(lanes >= 32, roll(v, 32, 1), jnp.where(lanes == 0, 0.0, roll(v, -223, 1)))


def next_y(v):
    return roll(v, -4, 1)


def prev_y(v):
    return roll(v, 4, 1)


def coarse_apply(n, s, u, wx, wy, wz, c):
    flux_y = [[None] * n for _ in range(n)]
    flux_z = [[None] * n for _ in range(n)]
    for y in range(n):
        for z in range(n):
            here = u[y][z]
            high_y = u[y + 1][z] if y + 1 < n else next_y(u[0][z])
            high_z = u[y][z + 1] if z + 1 < n else next_z(u[y][0])
            flux_y[y][z] = wy(y, z) * (high_y - here)
            flux_z[y][z] = wz(y, z) * (high_z - here)
    image = [[None] * n for _ in range(n)]
    for y in range(n):
        for z in range(n):
            here = u[y][z]
            flux_x = wx(y, z) * (roll(here, -s, 0) - here)
            low_y = flux_y[y - 1][z] if y else prev_y(flux_y[n - 1][z])
            low_z = flux_z[y][z - 1] if z else prev_z(flux_z[y][n - 1])
            image[y][z] = c(y, z) * here - (
                (flux_x - roll(flux_x, s, 0)) + (flux_y[y][z] - low_y) + (flux_z[y][z] - low_z)
            )
    return image


def planes(n, f):
    return [[f(y, z) for z in range(n)] for y in range(n)]


def pair_x(v):
    iota = lax.broadcasted_iota(jnp.int32, (16, NDEV), 0)
    return v + jnp.where(even(iota, 1), roll(v, -1, 0), roll(v, 1, 0))


def odd_pair_x(v):
    iota = lax.broadcasted_iota(jnp.int32, (16, NDEV), 0)
    return jnp.where(even(iota, 1), roll(v, -1, 0), v)


def inverse_diagonal(n, s, wx, wy, wz, c):
    def one(y, z):
        low_y = wy(y - 1, z) if y else prev_y(wy(n - 1, z))
        low_z = wz(y, z - 1) if z else prev_z(wz(y, n - 1))
        diagonal = c(y, z) + wx(y, z) + roll(wx(y, z), s, 0) + wy(y, z) + low_y + wz(y, z) + low_z
        return 1.0 / diagonal

    return planes(n, one)


def coefficients_kernel(got, k2, k3):
    for f in range(4):
        k2[f] = got[f].T

    def field(f):
        return lambda y, z: k2[f, pl.ds((y * 4 + z) * 16, 16), :]

    wx, wy, wz, c = (field(f) for f in range(4))
    inverse = inverse_diagonal(4, 1, wx, wy, wz, c)
    for y in range(4):
        for z in range(4):
            k2[4, pl.ds((y * 4 + z) * 16, 16), :] = inverse[y][z]
    for y in range(2):
        for z in range(2):
            a, b, e, f = (2 * y, 2 * z), (2 * y, 2 * z + 1), (2 * y + 1, 2 * z), (2 * y + 1, 2 * z + 1)
            at = pl.ds((y * 2 + z) * 16, 16)
            k3[0, at, :] = odd_pair_x((wx(*a) + wx(*b)) + (wx(*e) + wx(*f)))
            k3[1, at, :] = pair_x(wy(*e) + wy(*f))
            k3[2, at, :] = pair_x(wz(*b) + wz(*f))
            k3[3, at, :] = pair_x((c(*a) + c(*b)) + (c(*e) + c(*f)))

    def field3(f):
        return lambda y, z: k3[f, pl.ds((y * 2 + z) * 16, 16), :]

    inverse = inverse_diagonal(2, 2, *(field3(f) for f in range(4)))
    for y in range(2):
        for z in range(2):
            k3[4, pl.ds((y * 2 + z) * 16, 16), :] = inverse[y][z]


def combine(n, f, *lists):
    return planes(n, lambda y, z: f(*(a[y][z] for a in lists)))


def coarse_solve(got, k2, k3, b2t):
    b2t[...] = got.T

    def field(ref, n, f):
        return lambda y, z: ref[f, pl.ds((y * n + z) * 16, 16), :]

    a2 = tuple(field(k2, 4, f) for f in range(4))
    dinv = planes(4, field(k2, 4, 4))
    a3 = tuple(field(k3, 2, f) for f in range(4))
    dinv3 = planes(2, field(k3, 2, 4))
    r = planes(4, lambda y, z: b2t[pl.ds((y * 4 + z) * 16, 16), :])
    u = combine(4, lambda d, b: d * b / THETA, dinv, r)
    r = combine(4, lambda a, b: a - b, r, coarse_apply(4, 1, u, *a2))
    u1 = combine(4, lambda u, d, r: C1U * u + C1R * (d * r), u, dinv, r)
    x = combine(4, lambda a, b: a + b, u, u1)
    r = combine(4, lambda a, b: a - b, r, coarse_apply(4, 1, u1, *a2))
    r3 = planes(
        2,
        lambda y, z: pair_x(
            (r[2 * y][2 * z] + r[2 * y][2 * z + 1]) + (r[2 * y + 1][2 * z] + r[2 * y + 1][2 * z + 1])
        ),
    )
    u = combine(2, lambda d, b: d * b / THETA, dinv3, r3)
    x3 = u
    for cu, cr in ((C1U, C1R), (C2U, C2R)):
        r3 = combine(2, lambda a, b: a - b, r3, coarse_apply(2, 2, u, *a3))
        u = combine(2, lambda u, d, r: cu * u + cr * (d * r), u, dinv3, r3)
        x3 = combine(2, lambda a, b: a + b, x3, u)
    e = planes(4, lambda y, z: x3[y // 2][z // 2])
    x = combine(4, lambda a, b: a + b, x, e)
    r = combine(4, lambda a, b: a - b, r, coarse_apply(4, 1, e, *a2))
    u = combine(4, lambda d, b: d * b / THETA, dinv, r)
    r = combine(4, lambda a, b: a - b, r, coarse_apply(4, 1, u, *a2))
    u1 = combine(4, lambda u, d, r: C1U * u + C1R * (d * r), u, dinv, r)
    return combine(4, lambda x, a, b: x + (a + b), x, u, u1)


def place_coarse(pos, x2, e2):
    gy, zb = pos[0], pos[1]
    lanes = lane_ids()
    picked = {}
    for dy in (-1, 0, 1):
        for dz in (-1, 0, 1):
            at_y = jnp.clip(gy + dy, 0, NGY - 1)
            at_z = jnp.clip(zb + dz, 0, NZB - 1)
            picked[dy, dz] = lanes == ((at_z % NGX) * NGY + at_y) * NGZ + at_z // NGX
    spread = lax.broadcasted_iota(jnp.int32, (16, 128), 1) // 4 == lax.broadcasted_iota(jnp.int32, (16, 128), 0)
    rows = ziota() // 4
    for y2 in range(1, 9):
        dy, y = (y2 - 3) // 4, (y2 - 3) % 4
        plane = jnp.zeros((NB, 128), F32)
        for z2 in range(1, 9):
            dz, z = (z2 - 3) // 4, (z2 - 3) % 4
            column = jnp.sum(jnp.where(picked[dy, dz], x2[y][z], 0.0), axis=1, keepdims=True)
            line = jnp.sum(jnp.where(spread, column, 0.0), axis=0, keepdims=True)
            plane = jnp.where(rows == z2, line, plane)
        e2[y2] = plane


def up_kernel(pos, got, k2, k3, wx, wy, wz, c, dinv, wx1, wy1, wz1, c1, dinv1, x, r2, xm, r2m, out, b2t, e2, r3m, um, x1, r3, u):
    place_coarse(pos, coarse_solve(got[...], k2, k3, b2t), e2)
    fine = Level(wx, wy, wz, c, dinv, 1)
    mid = Level(wx1, wy1, wz1, c1, dinv1, 2)

    def keep(y, value):
        x1[y] = value

    smooth_up(mid, 4, 16, lambda y: e2[y // 2], r2m, r3m, um, xm, keep)

    def result(y, value):
        out[y - M] = dn_z(value, -M)[:B]

    smooth_up(fine, 11, 29, lambda y: x1[y // 2], r2, r3, u, x, result)


def image_kernel(z, r, wx, wy, wz, c, w, dots):
    fine = Level(wx, wy, wz, c, None, 1)

    def keep(y, u, image):
        w[y] = image

    sweep(fine, 2, 38, lambda y: z[y], keep)
    own = (ziota() >= M) & (ziota() < M + B)

    def row(y, carry):
        a, b = carry
        here = jnp.where(own, z[y], 0.0)
        return a + r[y] * here, b + here * w[y]

    zero = jnp.zeros((NB, 128), F32)
    a, b = lax.fori_loop(M, M + B, row, (zero, zero))
    lane = lax.broadcasted_iota(jnp.int32, (8, 128), 1)
    dots[...] = jnp.where(lane == 0, jnp.sum(a), jnp.where(lane == 1, jnp.sum(b), 0.0))


def step_sizes(got, old, scal, first):
    total = jnp.sum(got[...], axis=0, keepdims=True)
    lane = lax.broadcasted_iota(jnp.int32, (1, 128), 1)

    def pick(v, k):
        return jnp.sum(jnp.where(lane == k, v, 0.0))

    one = jnp.ones((1, 128), F32)
    gamma, delta = pick(total, 0) * one, pick(total, 1) * one
    if first:
        beta = jnp.zeros((1, 128), F32)
        alpha = gamma / delta
    else:
        was = old[0:1]
        gamma_old, alpha_old = pick(was, 0) * one, pick(was, 1) * one
        beta = gamma / gamma_old
        alpha = gamma / (delta - beta * gamma / alpha_old)
    if scal is not None:
        scal[...] = jnp.broadcast_to(jnp.where(lane == 0, gamma, alpha), (8, 128))
    return alpha, beta


def update_kernel(first, got, old, z, w, r, q, p, d, wx, wy, wz, c, dinv, wx1, wy1, wz1, c1, dinv1,
                  scal, r_o, q_o, p_o, d_o, x, r2, xm, r2m, pay, r1, u1, b1, r1m, u1m):
    alpha, beta = step_sizes(got, old, scal, first)

    def row(y, carry):
        q_y = w[y] if first else w[y] + beta * q[y]
        q_o[y] = q_y
        r_o[y] = r[y] - alpha * q_y
        return carry

    lax.fori_loop(2, 38, row, 0)

    def row_d(y, carry):
        p_y = z[y] if first else z[y] + beta * p[y]
        p_o[y] = p_y
        d_o[y] = alpha * p_y if first else d[y] + alpha * p_y
        return carry

    lax.fori_loop(M - 1, M + B + 1, row_d, 0)
    fine = Level(wx, wy, wz, c, dinv, 1)
    mid = Level(wx1, wy1, wz1, c1, dinv1, 2)
    down(fine, mid, r_o, r1, u1, x, r2, b1, r1m, u1m, xm, r2m, pay)


def finish_kernel(pos, steps, got, old, z, w, r, q, p, d, it, src, rea, d_out, r_out, layers, d_all):
    alpha, beta = step_sizes(got, old, None, False)
    gy, zb = pos[0], pos[1]

    def row_d(y, carry):
        d_all[y] = d[y] + alpha * (z[y] + beta * p[y])
        return carry

    lax.fori_loop(M - 1, M + B + 1, row_d, 0)

    def row(y, carry):
        r_out[y - M] = dn_z(r[y] - alpha * (w[y] + beta * q[y]), -M)[:B]
        d_out[y - M] = dn_z(d_all[y], -M)[:B]
        return carry

    lax.fori_loop(M, M + B, row, 0)
    zi = ziota()
    own = (zi >= M) & (zi < M + B)
    own_z = own | ((zi == M + B) & (zb == NZB - 1))
    lane = lax.broadcasted_iota(jnp.int32, (1, 128), 1)

    def energy(g):
        square = 1.0 + g * g
        return (square * jnp.sqrt(square) - 1.0) / 3.0

    zero = jnp.zeros((NB, 128), F32)
    for k in range(TRIALS):
        step = steps[k]

        def trial(y):
            return it[y] + step * d_all[y]

        def row(y, carry):
            low, acc_x, acc = carry
            v = trial(y)
            acc_x = acc_x + jnp.where(own, energy(v - dn_x(v)), 0.0)
            part = energy(v - low) + (0.5 * rea[y] * v * v - src[y] * v)
            acc = acc + jnp.where(own, part, 0.0) + jnp.where(own_z, energy(v - dn_z(v)), 0.0)
            return v, acc_x, acc

        v, acc_x, acc = lax.fori_loop(M, M + B, row, (trial(M - 1), zero, zero))
        last = own & (gy == NGY - 1)
        acc = acc + jnp.where(last, energy(trial(M + B) - v), 0.0)
        sum_of_x = jnp.sum(acc_x, axis=0, keepdims=True)
        top = jnp.where(lane == NX - 1, jnp.broadcast_to(roll(jnp.broadcast_to(sum_of_x, (8, 128)), -1, 1)[0:1], (1, 128)), 0.0)
        layers[k] = jnp.broadcast_to(sum_of_x + top + jnp.sum(acc, axis=0, keepdims=True), (8, 128))


VM = pl.BlockSpec(memory_space=pltpu.VMEM)
SM = pl.BlockSpec(memory_space=pltpu.SMEM)


def call(kernel, n_scalar, outs, scratch, name):
    def run(*args):
        return pl.pallas_call(
            kernel,
            in_specs=[SM] * n_scalar + [VM] * (len(args) - n_scalar),
            out_specs=[VM] * len(outs),
            out_shape=[jax.ShapeDtypeStruct(s, F32) for s in outs],
            scratch_shapes=[pltpu.VMEM(s, F32) for s in scratch],
            interpret=INTERPRET,
            name=name,
        )(*args)

    return run


FINE = (NB, NB, 128)
MID = (NB // 2, NB, 128)
DOWN_SCRATCH = [FINE, FINE, MID, MID, MID]


def shift_pairs(dy, dz):
    pairs = []
    for gy in range(NGY):
        for zb in range(NZB):
            ty, tz = gy + dy, zb + dz
            if 0 <= ty < NGY and 0 <= tz < NZB:
                source = ((zb % NGX) * NGY + gy) * NGZ + zb // NGX
                target = ((tz % NGX) * NGY + ty) * NGZ + tz // NGX
                pairs.append((source, target))
    return pairs


def exchange(own):
    ax = own.ndim - 2
    low = lax.ppermute(lax.slice_in_dim(own, B - M, B, axis=ax), ALL, shift_pairs(0, 1))
    high = lax.ppermute(lax.slice_in_dim(own, 0, M, axis=ax), ALL, shift_pairs(0, -1))
    own = jnp.concatenate([low, own, high], axis=ax)
    ax = own.ndim - 3
    low = lax.ppermute(lax.slice_in_dim(own, B - M, B, axis=ax), ALL, shift_pairs(1, 0))
    high = lax.ppermute(lax.slice_in_dim(own, 0, M, axis=ax), ALL, shift_pairs(-1, 0))
    return jnp.concatenate([low, own, high], axis=ax)


def to_everyone(x):
    copies = jnp.broadcast_to(x, (NDEV, *x.shape))
    return lax.all_to_all(copies, ALL, split_axis=0, concat_axis=0, tiled=True)


def compact(pay):
    kept = pay[:, M : M + B : 4, 0:NX:4]
    return kept.reshape(-1, 256)


def on_device(iterate, source, reaction, trial_powers):
    gx = lax.axis_index("gx")
    gy = lax.axis_index(GY)
    zb = lax.axis_index("gz") * NGX + gx
    pos = jnp.stack([gy, zb]).astype(jnp.int32)
    steps = jnp.exp2(-trial_powers.astype(F32))
    fields = jnp.stack([iterate, source, reaction])
    fields = fields.reshape(3, 8, 16, 8, 16).transpose(3, 1, 0, 2, 4).reshape(8, 8, 3, 256)
    fields = lax.all_to_all(fields, "gx", split_axis=0, concat_axis=0, tiled=True)
    fields = fields.reshape(NX, 3 * 256).T.reshape(3, 16, 16, NX)
    fields = exchange(jnp.pad(fields, ((0, 0), (0, 0), (0, 0), (0, 128 - NX))))
    it, src, rea = fields[0], fields[1], fields[2]
    coefs_and_rest = call(
        setup_kernel, 1, [FINE] * 5 + [MID] * 5 + [FINE] * 3 + [MID] * 2 + [(20, NB, 128)], DOWN_SCRATCH, "setup"
    )(pos, it, src, rea)
    fine, mid = coefs_and_rest[:5], coefs_and_rest[5:10]
    r, x, r2, xm, r2m, pay = coefs_and_rest[10:]
    got = to_everyone(compact(pay))
    k2, k3 = call(coefficients_kernel, 0, [(5, 256, NDEV), (5, 64, NDEV)], [], "coefficients")(
        got[:, 1:].transpose(1, 0, 2)
    )
    got = got[:, 0]
    up = call(up_kernel, 1, [(B, B, 128)], [(256, NDEV), (NB // 4, NB, 128), MID, MID, MID, FINE, FINE], "up")
    image = call(image_kernel, 0, [FINE, (8, 128)], [], "image")
    q = p = d = r
    scal = jnp.zeros((8, 128), F32)
    for i in range(ITERS):
        (z,) = up(pos, got, k2, k3, *fine, *mid, x, r2, xm, r2m)
        z = exchange(z)
        w, dots = image(z, r, *fine[:4])
        dots = to_everyone(dots[0:1])[:, 0]
        if i + 1 < ITERS:
            update = call(
                lambda *refs, first=i == 0: update_kernel(first, *refs), 0,
                [(8, 128)] + [FINE] * 6 + [MID] * 2 + [(4, NB, 128)], DOWN_SCRATCH, "update",
            )
            scal, r, q, p, d, x, r2, xm, r2m, pay = update(dots, scal, z, w, r, q, p, d, *fine, *mid)
            got = to_everyone(compact(pay))[:, 0]
    own = (B, B, 128)
    d_own, r_own, layers = call(finish_kernel, 2, [own, own, (TRIALS, 8, 128)], [FINE], "finish")(
        pos, steps, dots, scal, z, w, r, q, p, d, it, src, rea
    )
    both = jnp.stack([d_own, r_own])[..., :NX].reshape(512, NX).T
    both = lax.all_to_all(both.reshape(8, 8, 512), "gx", split_axis=0, concat_axis=0, tiled=True)
    both = both.reshape(8, 8, 2, 16, 16).transpose(2, 1, 3, 0, 4).reshape(2, 8, 16, 128)
    layers = to_everyone(layers[:, 0, :NX].reshape(2, 128)).sum(axis=0).reshape(TRIALS, NX) / (NY * NZ)
    energies = jnp.sum(layers, axis=1) / NX
    mine = lax.dynamic_slice_in_dim(layers, gx * 8, 8, axis=1)
    return both[0], both[1], mine, energies


def solution(mesh):
    torus = Mesh(mesh.devices.reshape(8, 4, 2, 4), ALL)
    placed = P("gx", GY, "gz")
    return jax.shard_map(
        on_device,
        mesh=torus,
        in_specs=(placed, placed, placed, P()),
        out_specs=(placed, placed, P(None, "gx"), P()),
        check_vma=False,
    )
```

profile of v0, /device:TPU:1, one launch (start us, length us, event | category | flops | bytes accessed | tf_op | source)
XLA Modules:
  0.0 627.3 jit_solution(9137059831515053970)
XLA Ops:
  4.1 17.8 %all_to_all.55 = f32[8,8,3,256]{3,1,2,0:T(8,128)S(1)} all-to-all(f32[8,8,3,256]{3,1,2,0:T(8,128)S(1)} %reshape.63), channel_id=1, replica_groups=mesh['gx'=8,'gy_0'=4,'gy_1'=2,'gz'=4] {'gx'}, dimensions={0} | all-to-all | bytes 393216 | tf_op jit(solution)/shard_map/all_to_all | solution.py:588
  22.1 1.9 collective-permute-start
  24.0 1.3 collective-permute-start.1
  25.4 4.3 collective-permute-done
  29.7 3.9 collective-permute-done.1
  34.9 7.0 %collective-permute-start.2 = (f32[3,12,40,128]{3,2,1,0:T(8,128)}, f32[3,12,40,128]{3,2,1,0:T(8,128)S(1)}, u32[]{:S(2)}, u32[]{:S(2)}) collective-permute-start(f32[3,12,40,128]{3,2,1,0:T(8,128)} %get-tuple-element.127), channel_id=1, source_target_pairs={{0,4},{32,36},{64,68},{96,100},{128,132},{160,164},{192,196},{224,... | collective-permute-start | bytes 2211848 | tf_op jit(solution)/shard_map/ppermute | solution.py:565
  41.9 1.9 collective-permute-start.3
  44.4 6.2 collective-permute-done.2
  50.6 4.3 collective-permute-done.3
  55.0 1.5 slice_bitcast_fusion
  56.5 30.9 %setup.1 = (f32[40,40,128]{2,1,0:T(8,128)}, f32[40,40,128]{2,1,0:T(8,128)}, f32[40,40,128]{2,1,0:T(8,128)}, f32[40,40,128]{2,1,0:T(8,128)}, f32[40,40,128]{2,1,0...) custom-call(s32[2]{0:T(128)} %pad_add_fusion.pos, ...), custom_call_target="tpu_custom_call" | custom-call | tf_op jit(solution)/shard_map/setup/pallas_call | solution.py:529
  88.9 65.7 %all_to_all.56 = f32[256,5,256]{2,1,0:T(8,128)S(1)} all-to-all(f32[256,5,256]{2,1,0:T(8,128)S(1)} %broadcast_in_dim.30), channel_id=1, replica_groups=mesh['gx'=8,'gy_0'=4,'gy_1'=2,'gz'=4] {'gx','gy_0','gy_1','gz'}, dimensions={0} | all-to-all | bytes 2621440 | tf_op jit(solution)/shard_map/all_to_all | solution.py:572
  156.1 2.9 coefficients.1
  159.8 14.8 %up.4 = f32[16,16,128]{2,1,0:T(8,128)} custom-call(s32[2]{0:T(128)} %pad_add_fusion.pos, f32[256,256]{1,0:T(8,128)} %bitcast.61, f32[5,256,256]{2,1,0:T(8,128)} %get-tuple-element.64.k2, f32[5,64,256]{2,1,0:T(8,128)} %get-tuple-element.65.k3, f32[40,40,128]{2,1,0:T(8,128)} %get-tuple-element.66.wx.refs_8_, f32[40,40,128]{2,1,0:T(8,128)} %get-tuple-element.67.wy.refs_9_, ...), custom_call_target="tpu_custom_call" | custom-call | tf_op jit(solution)/shard_map/up/pallas_call | solution.py:529
  175.6 2.6 collective-permute-start.4
  178.2 1.3 collective-permute-start.5
  179.5 1.6 collective-permute-done.4
  181.1 3.8 collective-permute-done.5
  185.9 3.3 collective-permute-start.6
  189.2 1.9 collective-permute-start.7
  192.3 4.4 collective-permute-done.7
  196.7 1.9 pad_maximum_fusion.2.z.refs_2_
  198.6 8.7 %image.4 = (f32[40,40,128]{2,1,0:T(8,128)}, f32[8,128]{1,0:T(8,128)}) custom-call(f32[40,40,128]{2,1,0:T(8,128)} %pad_maximum_fusion.2.z.refs_2_, f32[40,40,128]{2,1,0:T(8,128)} %get-tuple-element.80.r.refs_4_.refs_5_.refs_6_.refs_7_, f32[40,40,128]{2,1,0:T(8,128)} %get-tuple-element.66.wx.refs_8_, f32[40,40,128]{2,1,0:T(8,128)} %get-tuple-element.67.wy.refs_9_, ...), custom_call_target="tpu_custom_call" | custom-call | tf_op jit(solution)/shard_map/image/pallas_call | solution.py:529
  208.0 21.6 %all_to_all.57 = f32[256,1,128]{2,1,0:T(1,128)} all-to-all(f32[256,1,128]{2,1,0:T(1,128)S(1)} %broadcast_in_dim.31), channel_id=1, replica_groups=mesh['gx'=8,'gy_0'=4,'gy_1'=2,'gz'=4] {'gx','gy_0','gy_1','gz'}, dimensions={0} | all-to-all | bytes 262144 | tf_op jit(solution)/shard_map/all_to_all | solution.py:572
  230.2 22.5 %update.3 = (f32[8,128]{1,0:T(8,128)}, f32[40,40,128]{2,1,0:T(8,128)}, f32[40,40,128]{2,1,0:T(8,128)}, f32[40,40,128]{2,1,0:T(8,128)}, f32[40,40,128]{2,1,0:T(8,...) custom-call(f32[256,128]{1,0:T(8,128)} %bitcast.69, ...), custom_call_target="tpu_custom_call" | custom-call | tf_op jit(solution)/shard_map/update/pallas_call | solution.py:529
  253.9 21.1 %all_to_all.58 = f32[256,1,256]{2,1,0:T(1,128)S(1)} all-to-all(f32[256,1,256]{2,1,0:T(1,128)S(1)} %broadcast_in_dim.33), channel_id=1, replica_groups=mesh['gx'=8,'gy_0'=4,'gy_1'=2,'gz'=4] {'gx','gy_0','gy_1','gz'}, dimensions={0} | all-to-all | bytes 524288 | tf_op jit(solution)/shard_map/all_to_all | solution.py:572
  275.7 14.9 %up.5 = f32[16,16,128]{2,1,0:T(8,128)} custom-call(s32[2]{0:T(128)} %pad_add_fusion.pos, f32[256,256]{1,0:T(8,128)} %bitcast.62, f32[5,256,256]{2,1,0:T(8,128)} %get-tuple-element.64.k2, f32[5,64,256]{2,1,0:T(8,128)} %get-tuple-element.65.k3, f32[40,40,128]{2,1,0:T(8,128)} %get-tuple-element.66.wx.refs_8_, f32[40,40,128]{2,1,0:T(8,128)} %get-tuple-element.67.wy.refs_9_, ...), custom_call_target="tpu_custom_call" | custom-call | tf_op jit(solution)/shard_map/up/pallas_call | solution.py:529
  291.6 2.6 collective-permute-start.8
  294.2 1.3 collective-permute-start.9
  296.6 3.8 collective-permute-done.9
  301.5 3.7 collective-permute-start.10
  305.2 1.9 collective-permute-start.11
  308.3 4.4 collective-permute-done.11
  312.7 1.9 pad_maximum_fusion.3.z.refs_2_
  314.5 8.7 %image.5 = (f32[40,40,128]{2,1,0:T(8,128)}, f32[8,128]{1,0:T(8,128)}) custom-call(f32[40,40,128]{2,1,0:T(8,128)} %pad_maximum_fusion.3.z.refs_2_, f32[40,40,128]{2,1,0:T(8,128)} %get-tuple-element.88.r.refs_4_, f32[40,40,128]{2,1,0:T(8,128)} %get-tuple-element.66.wx.refs_8_, f32[40,40,128]{2,1,0:T(8,128)} %get-tuple-element.67.wy.refs_9_, ...), custom_call_target="tpu_custom_call" | custom-call | tf_op jit(solution)/shard_map/image/pallas_call | solution.py:529
  324.0 22.2 %all_to_all.59 = f32[256,1,128]{2,1,0:T(1,128)} all-to-all(f32[256,1,128]{2,1,0:T(1,128)S(1)} %broadcast_in_dim.34), channel_id=1, replica_groups=mesh['gx'=8,'gy_0'=4,'gy_1'=2,'gz'=4] {'gx','gy_0','gy_1','gz'}, dimensions={0} | all-to-all | bytes 262144 | tf_op jit(solution)/shard_map/all_to_all | solution.py:572
  346.2 22.5 %update.4 = (f32[8,128]{1,0:T(8,128)}, f32[40,40,128]{2,1,0:T(8,128)}, f32[40,40,128]{2,1,0:T(8,128)}, f32[40,40,128]{2,1,0:T(8,128)}, f32[40,40,128]{2,1,0:T(8,...) custom-call(f32[256,128]{1,0:T(8,128)} %bitcast.67, ...), custom_call_target="tpu_custom_call" | custom-call | tf_op jit(solution)/shard_map/update/pallas_call | solution.py:529
  369.9 20.9 %all_to_all.60 = f32[256,1,256]{2,1,0:T(1,128)S(1)} all-to-all(f32[256,1,256]{2,1,0:T(1,128)S(1)} %broadcast_in_dim.35), channel_id=1, replica_groups=mesh['gx'=8,'gy_0'=4,'gy_1'=2,'gz'=4] {'gx','gy_0','gy_1','gz'}, dimensions={0} | all-to-all | bytes 524288 | tf_op jit(solution)/shard_map/all_to_all | solution.py:572
  391.5 14.8 %up.6 = f32[16,16,128]{2,1,0:T(8,128)} custom-call(s32[2]{0:T(128)} %pad_add_fusion.pos, f32[256,256]{1,0:T(8,128)} %bitcast.63, f32[5,256,256]{2,1,0:T(8,128)} %get-tuple-element.64.k2, f32[5,64,256]{2,1,0:T(8,128)} %get-tuple-element.65.k3, f32[40,40,128]{2,1,0:T(8,128)} %get-tuple-element.66.wx.refs_8_, f32[40,40,128]{2,1,0:T(8,128)} %get-tuple-element.67.wy.refs_9_, ...), custom_call_target="tpu_custom_call" | custom-call | tf_op jit(solution)/shard_map/up/pallas_call | solution.py:529
  407.3 2.6 collective-permute-start.12
  412.4 3.8 collective-permute-done.13
  417.2 3.7 collective-permute-start.14
  420.9 1.9 collective-permute-start.15
  424.0 4.4 collective-permute-done.15
  428.4 1.9 pad_maximum_fusion.4.z.refs_2_
  430.3 8.7 %image.6 = (f32[40,40,128]{2,1,0:T(8,128)}, f32[8,128]{1,0:T(8,128)}) custom-call(f32[40,40,128]{2,1,0:T(8,128)} %pad_maximum_fusion.4.z.refs_2_, f32[40,40,128]{2,1,0:T(8,128)} %get-tuple-element.100.r.refs_4_, f32[40,40,128]{2,1,0:T(8,128)} %get-tuple-element.66.wx.refs_8_, f32[40,40,128]{2,1,0:T(8,128)} %get-tuple-element.67.wy.refs_9_, ...), custom_call_target="tpu_custom_call" | custom-call | tf_op jit(solution)/shard_map/image/pallas_call | solution.py:529
  439.7 22.2 %all_to_all.61 = f32[256,1,128]{2,1,0:T(1,128)} all-to-all(f32[256,1,128]{2,1,0:T(1,128)S(1)} %broadcast_in_dim.36), channel_id=1, replica_groups=mesh['gx'=8,'gy_0'=4,'gy_1'=2,'gz'=4] {'gx','gy_0','gy_1','gz'}, dimensions={0} | all-to-all | bytes 262144 | tf_op jit(solution)/shard_map/all_to_all | solution.py:572
  461.9 22.6 %update.5 = (f32[8,128]{1,0:T(8,128)}, f32[40,40,128]{2,1,0:T(8,128)}, f32[40,40,128]{2,1,0:T(8,128)}, f32[40,40,128]{2,1,0:T(8,128)}, f32[40,40,128]{2,1,0:T(8,...) custom-call(f32[256,128]{1,0:T(8,128)} %bitcast.68, ...), custom_call_target="tpu_custom_call" | custom-call | tf_op jit(solution)/shard_map/update/pallas_call | solution.py:529
  485.7 20.9 %all_to_all.62 = f32[256,1,256]{2,1,0:T(1,128)S(1)} all-to-all(f32[256,1,256]{2,1,0:T(1,128)S(1)} %broadcast_in_dim.37), channel_id=1, replica_groups=mesh['gx'=8,'gy_0'=4,'gy_1'=2,'gz'=4] {'gx','gy_0','gy_1','gz'}, dimensions={0} | all-to-all | bytes 524288 | tf_op jit(solution)/shard_map/all_to_all | solution.py:572
  507.4 14.8 %up.7 = f32[16,16,128]{2,1,0:T(8,128)} custom-call(s32[2]{0:T(128)} %pad_add_fusion.pos, f32[256,256]{1,0:T(8,128)} %bitcast.60, f32[5,256,256]{2,1,0:T(8,128)} %get-tuple-element.64.k2, f32[5,64,256]{2,1,0:T(8,128)} %get-tuple-element.65.k3, f32[40,40,128]{2,1,0:T(8,128)} %get-tuple-element.66.wx.refs_8_, f32[40,40,128]{2,1,0:T(8,128)} %get-tuple-element.67.wy.refs_9_, ...), custom_call_target="tpu_custom_call" | custom-call | tf_op jit(solution)/shard_map/up/pallas_call | solution.py:529
  523.2 2.6 collective-permute-start.16
  528.2 3.8 collective-permute-done.17
  533.1 3.7 collective-permute-start.18
  536.8 1.9 collective-permute-start.19
  539.9 4.4 collective-permute-done.19
  544.3 1.9 pad_maximum_fusion.5.z
  546.2 8.7 %image.7 = (f32[40,40,128]{2,1,0:T(8,128)}, f32[8,128]{1,0:T(8,128)}) custom-call(f32[40,40,128]{2,1,0:T(8,128)} %pad_maximum_fusion.5.z, f32[40,40,128]{2,1,0:T(8,128)} %get-tuple-element.112.r, f32[40,40,128]{2,1,0:T(8,128)} %get-tuple-element.66.wx.refs_8_, f32[40,40,128]{2,1,0:T(8,128)} %get-tuple-element.67.wy.refs_9_, ...), custom_call_target="tpu_custom_call" | custom-call | tf_op jit(solution)/shard_map/image/pallas_call | solution.py:529
  556.2 9.4 %all-to-all-start.8 = ((f32[256,1,128]{2,1,0:T(1,128)}), f32[256,1,128]{2,1,0:T(1,128)S(1)}, u32[]{:S(2)}, u32[]{:S(2)}) async-start(f32[256,1,128]{2,1,0:T(1,128)} %broadcast_in_dim.38), calls=%async_computation.8 | async-start | bytes 262144 | tf_op jit(solution)/shard_map/all_to_all | solution.py:572
  566.2 12.3 %all-to-all-done.8 = f32[256,1,128]{2,1,0:T(1,128)S(1)} async-done(((f32[256,1,128]{2,1,0:T(1,128)}), f32[256,1,128]{2,1,0:T(1,128)S(1)}, u32[]{:S(2)}, u32[]{:S(2)}) %all-to-all-start.8) | async-done | bytes 131104 | tf_op jit(solution)/shard_map/all_to_all | solution.py:572
  579.1 10.4 %finish.1 = (f32[16,16,128]{2,1,0:T(8,128)}, f32[16,16,128]{2,1,0:T(8,128)}, f32[4,8,128]{2,1,0:T(8,128)}) custom-call(s32[2]{0:T(128)} %pad_add_fusion.pos, f32[4]{0:T(128)} %multiply_exponential_fusion.steps, f32[256,128]{1,0:T(8,128)} %bitcast.66, f32[8,128]{1,0:T(8,128)} %get-tuple-element.114.old, f32[40,40,128]{2,1,0:T(8,128)} %pad_maximum_fusion.5.z, ...), custom_call_target="tpu_custom_call" | custom-call | tf_op jit(solution)/shard_map/finish/pallas_call | solution.py:529
  591.2 3.4 all-to-all-start.9
  595.4 7.1 %all-to-all-done.9 = f32[8,8,512]{2,1,0:T(8,128)S(1)} async-done(((f32[8,8,512]{2,1,0:T(8,128)}), f32[8,8,512]{2,1,0:T(8,128)S(1)}, u32[]{:S(2)}, u32[]{:S(2)}) %all-to-all-start.9) | async-done | bytes 131104 | tf_op jit(solution)/shard_map/all_to_all | solution.py:623
  603.3 7.0 %all-to-all-start.10 = ((f32[256,2,128]{2,1,0:T(2,128)}), f32[256,2,128]{2,1,0:T(2,128)S(1)}, u32[]{:S(2)}, u32[]{:S(2)}) async-start(f32[256,2,128]{2,1,0:T(2,128)} %broadcast_in_dim.39), calls=%async_computation.10 | async-start | bytes 524288 | tf_op jit(solution)/shard_map/all_to_all | solution.py:572
  613.0 12.6 %all-to-all-done.10 = f32[256,2,128]{2,1,0:T(2,128)S(1)} async-done(((f32[256,2,128]{2,1,0:T(2,128)}), f32[256,2,128]{2,1,0:T(2,128)S(1)}, u32[]{:S(2)}, u32[]{:S(2)}) %all-to-all-start.10) | async-done | bytes 262176 | tf_op jit(solution)/shard_map/all_to_all | solution.py:572
  (88 shorter events, 46.9 us)
Async XLA Ops:
  0.6 2.3 copy-start.1
  22.1 7.5 %collective-permute-start = (f32[3,16,12,128]{3,2,1,0:T(8,128)S(1)}, f32[3,16,12,128]{3,2,1,0:T(8,128)S(1)}, u32[]{:S(2)}, u32[]{:S(2)}) collective-permute-start(f32[3,16,12,128]{3,2,1,0:T(8,128)S(1)} %get-tuple-element.129), channel_id=1, source_target_pairs={{0,32},{32,64},{64,96},{96,128},{128,160},{160,192},{192,224},{224... | collective-permute-start | bytes 884744 | tf_op jit(solution)/shard_map/ppermute | solution.py:561
  24.0 9.5 %collective-permute-start.1 = (f32[3,16,12,128]{3,2,1,0:T(8,128)S(1)}, f32[3,16,12,128]{3,2,1,0:T(8,128)S(1)}, u32[]{:S(2)}, u32[]{:S(2)}) collective-permute-start(f32[3,16,12,128]{3,2,1,0:T(8,128)S(1)} %get-tuple-element.130), channel_id=1, source_target_pairs={{32,0},{64,32},{96,64},{128,96},{160,128},{192,160},{224,192},{1,2... | collective-permute-start | bytes 884744 | tf_op jit(solution)/shard_map/ppermute | solution.py:562
  34.9 15.7 %collective-permute-start.2 = (f32[3,12,40,128]{3,2,1,0:T(8,128)}, f32[3,12,40,128]{3,2,1,0:T(8,128)S(1)}, u32[]{:S(2)}, u32[]{:S(2)}) collective-permute-start(f32[3,12,40,128]{3,2,1,0:T(8,128)} %get-tuple-element.127), channel_id=1, source_target_pairs={{0,4},{32,36},{64,68},{96,100},{128,132},{160,164},{192,196},{224,... | collective-permute-start | bytes 2211848 | tf_op jit(solution)/shard_map/ppermute | solution.py:565
  41.9 13.0 %collective-permute-start.3 = (f32[3,12,40,128]{3,2,1,0:T(8,128)}, f32[3,12,40,128]{3,2,1,0:T(8,128)S(1)}, u32[]{:S(2)}, u32[]{:S(2)}) collective-permute-start(f32[3,12,40,128]{3,2,1,0:T(8,128)} %get-tuple-element.128), channel_id=1, source_target_pairs={{4,0},{36,32},{68,64},{100,96},{132,128},{164,160},{196,192},{228,... | collective-permute-start | bytes 2211848 | tf_op jit(solution)/shard_map/ppermute | solution.py:566
  175.6 5.5 collective-permute-start.4
  178.2 6.7 %collective-permute-start.5 = (f32[16,12,128]{2,1,0:T(8,128)S(1)}, f32[16,12,128]{2,1,0:T(8,128)S(1)}, u32[]{:S(2)}, u32[]{:S(2)}) collective-permute-start(f32[16,12,128]{2,1,0:T(8,128)S(1)} %get-tuple-element.146), channel_id=1, source_target_pairs={{32,0},{64,32},{96,64},{128,96},{160,128},{192,160},{224,192},{1,2... | collective-permute-start | bytes 294920 | tf_op jit(solution)/shard_map/ppermute | solution.py:562
  185.9 6.4 %collective-permute-start.6 = (f32[12,40,128]{2,1,0:T(8,128)S(1)}, f32[12,40,128]{2,1,0:T(8,128)S(1)}, u32[]{:S(2)}, u32[]{:S(2)}) collective-permute-start(f32[12,40,128]{2,1,0:T(8,128)S(1)} %get-tuple-element.137), channel_id=1, source_target_pairs={{0,4},{32,36},{64,68},{96,100},{128,132},{160,164},{192,196},{224,... | collective-permute-start | bytes 737288 | tf_op jit(solution)/shard_map/ppermute | solution.py:565
  189.2 7.5 %collective-permute-start.7 = (f32[12,40,128]{2,1,0:T(8,128)S(1)}, f32[12,40,128]{2,1,0:T(8,128)S(1)}, u32[]{:S(2)}, u32[]{:S(2)}) collective-permute-start(f32[12,40,128]{2,1,0:T(8,128)S(1)} %get-tuple-element.138), channel_id=1, source_target_pairs={{4,0},{36,32},{68,64},{100,96},{132,128},{164,160},{196,192},{228,... | collective-permute-start | bytes 737288 | tf_op jit(solution)/shard_map/ppermute | solution.py:566
  291.6 5.1 collective-permute-start.8
  294.2 6.3 collective-permute-start.9
  301.5 6.8 %collective-permute-start.10 = (f32[12,40,128]{2,1,0:T(8,128)S(1)}, f32[12,40,128]{2,1,0:T(8,128)S(1)}, u32[]{:S(2)}, u32[]{:S(2)}) collective-permute-start(f32[12,40,128]{2,1,0:T(8,128)S(1)} %get-tuple-element.135), channel_id=1, source_target_pairs={{0,4},{32,36},{64,68},{96,100},{128,132},{160,164},{192,196},{224,... | collective-permute-start | bytes 737288 | tf_op jit(solution)/shard_map/ppermute | solution.py:565
  305.2 7.5 %collective-permute-start.11 = (f32[12,40,128]{2,1,0:T(8,128)S(1)}, f32[12,40,128]{2,1,0:T(8,128)S(1)}, u32[]{:S(2)}, u32[]{:S(2)}) collective-permute-start(f32[12,40,128]{2,1,0:T(8,128)S(1)} %get-tuple-element.136), channel_id=1, source_target_pairs={{4,0},{36,32},{68,64},{100,96},{132,128},{164,160},{196,192},{228,... | collective-permute-start | bytes 737288 | tf_op jit(solution)/shard_map/ppermute | solution.py:566
  407.3 5.1 collective-permute-start.12
  409.9 6.3 collective-permute-start.13
  417.2 6.8 %collective-permute-start.14 = (f32[12,40,128]{2,1,0:T(8,128)S(1)}, f32[12,40,128]{2,1,0:T(8,128)S(1)}, u32[]{:S(2)}, u32[]{:S(2)}) collective-permute-start(f32[12,40,128]{2,1,0:T(8,128)S(1)} %get-tuple-element.133), channel_id=1, source_target_pairs={{0,4},{32,36},{64,68},{96,100},{128,132},{160,164},{192,196},{224,... | collective-permute-start | bytes 737288 | tf_op jit(solution)/shard_map/ppermute | solution.py:565
  420.9 7.5 %collective-permute-start.15 = (f32[12,40,128]{2,1,0:T(8,128)S(1)}, f32[12,40,128]{2,1,0:T(8,128)S(1)}, u32[]{:S(2)}, u32[]{:S(2)}) collective-permute-start(f32[12,40,128]{2,1,0:T(8,128)S(1)} %get-tuple-element.134), channel_id=1, source_target_pairs={{4,0},{36,32},{68,64},{100,96},{132,128},{164,160},{196,192},{228,... | collective-permute-start | bytes 737288 | tf_op jit(solution)/shard_map/ppermute | solution.py:566
  523.2 5.1 collective-permute-start.16
  525.8 6.3 collective-permute-start.17
  533.1 6.8 %collective-permute-start.18 = (f32[12,40,128]{2,1,0:T(8,128)S(1)}, f32[12,40,128]{2,1,0:T(8,128)S(1)}, u32[]{:S(2)}, u32[]{:S(2)}) collective-permute-start(f32[12,40,128]{2,1,0:T(8,128)S(1)} %get-tuple-element.131), channel_id=1, source_target_pairs={{0,4},{32,36},{64,68},{96,100},{128,132},{160,164},{192,196},{224,... | collective-permute-start | bytes 737288 | tf_op jit(solution)/shard_map/ppermute | solution.py:565
  536.8 7.5 %collective-permute-start.19 = (f32[12,40,128]{2,1,0:T(8,128)S(1)}, f32[12,40,128]{2,1,0:T(8,128)S(1)}, u32[]{:S(2)}, u32[]{:S(2)}) collective-permute-start(f32[12,40,128]{2,1,0:T(8,128)S(1)} %get-tuple-element.132), channel_id=1, source_target_pairs={{4,0},{36,32},{68,64},{100,96},{132,128},{164,160},{196,192},{228,... | collective-permute-start | bytes 737288 | tf_op jit(solution)/shard_map/ppermute | solution.py:566
  546.2 19.5 %copy-start.2 = (s32[4]{0:T(128)S(1)}, s32[4]{0:T(128)}, u32[]{:S(2)}) copy-start(s32[4]{0:T(128)} %param.7) | copy-start | bytes 52
  556.2 22.2 %all-to-all-start.8 = ((f32[256,1,128]{2,1,0:T(1,128)}), f32[256,1,128]{2,1,0:T(1,128)S(1)}, u32[]{:S(2)}, u32[]{:S(2)}) async-start(f32[256,1,128]{2,1,0:T(1,128)} %broadcast_in_dim.38), calls=%async_computation.8 | async-start | bytes 262144 | tf_op jit(solution)/shard_map/all_to_all | solution.py:572
  578.4 0.7 copy-start
  591.2 11.3 %all-to-all-start.9 = ((f32[8,8,512]{2,1,0:T(8,128)}), f32[8,8,512]{2,1,0:T(8,128)S(1)}, u32[]{:S(2)}, u32[]{:S(2)}) async-start(f32[8,8,512]{2,1,0:T(8,128)} %bitcast.23), calls=%async_computation.9 | async-start | bytes 262144 | tf_op jit(solution)/shard_map/all_to_all | solution.py:623
  603.3 22.4 %all-to-all-start.10 = ((f32[256,2,128]{2,1,0:T(2,128)}), f32[256,2,128]{2,1,0:T(2,128)S(1)}, u32[]{:S(2)}, u32[]{:S(2)}) async-start(f32[256,2,128]{2,1,0:T(2,128)} %broadcast_in_dim.39), calls=%async_computation.10 | async-start | bytes 524288 | tf_op jit(solution)/shard_map/all_to_all | solution.py:572
where the time goes:
time: 629 us; the launch traced here: 627 us
  blocking collectives  213 us (34%)
  Pallas kernels  206 us (33%)
  waiting for transfers between devices  93.3 us (15%)
  starting transfers between devices  69.5 us (11%)
  local copies, waits for them, and re-layouts  30.4 us (5%)
  other arithmetic  14.7 us (2%)
    pallas_call x14, Pallas kernels, run(): pl.pallas_call(kernel, in_specs=[SM] * n_scalar + [VM] * (len(args) - n_s...  206 us
    all_to_all x7, blocking collectives, to_everyone(): return lax.all_to_all(copies, ALL, split_axis=0, concat_axis=0, tiled=True)  195 us
    all_to_all x2, waiting for transfers between devices, to_everyone(): return lax.all_to_all(copies, ALL, split_axis=0, concat_axis=0, tiled=True)  24.9 us
    ppermute x5, waiting for transfers between devices, exchange(): lax.ppermute(lax.slice_in_dim(own, 0, M, axis=ax), ALL, shift_pairs(-1, 0))  21.9 us
    ppermute x5, starting transfers between devices, exchange(): lax.ppermute(lax.slice_in_dim(own, B - M, B, axis=ax), ALL, shift_pairs(1...  21.4 us
    ppermute x5, waiting for transfers between devices, exchange(): lax.ppermute(lax.slice_in_dim(own, 0, M, axis=ax), ALL, shift_pairs(0, -1))  19.2 us
    all_to_all x1, blocking collectives, on_device(): lax.all_to_all(fields, 'gx', split_axis=0, concat_axis=0, tiled=True)  17.8 us
    all_to_all x2, starting transfers between devices, to_everyone(): return lax.all_to_all(copies, ALL, split_axis=0, concat_axis=0, tiled=True)  16.4 us
  transfers between devices with their start and end apart: 23, of which 23 were waited for; matrix products, arithmetic and copies ran while one was open for 1% of the time, Pallas kernels for 0%

commit v1 on v0

--- a/solution.py
+++ b/solution.py
@@ -1,3 +1,5 @@
+import functools
+
 import jax
 import jax.numpy as jnp
 from jax import lax
@@ -19,6 +21,7 @@
 NB = 40
 F32 = jnp.float32
 INTERPRET = False
+LIMIT = 26 * 1024 * 1024
 
 THETA = 1.15
 DELTA = 0.85
@@ -96,6 +99,26 @@
         return image, flux_y
 
 
+def rows(lo, hi, body, carry, step=4):
+    def group(start, carry):
+        stores = []
+        for k in range(step):
+            carry, more = body(start + k, carry)
+            stores += more
+        for ref, at, value in stores:
+            ref[at] = value
+        return carry
+
+    count = (hi - lo) // step
+    if count:
+        carry = lax.fori_loop(0, count, lambda i, carry: group(lo + i * step, carry), carry)
+    for y in range(lo + count * step, hi):
+        carry, stores = body(y, carry)
+        for ref, at, value in stores:
+            ref[at] = value
+    return carry
+
+
 def sweep(level, lo, hi, field, store):
     first = field(lo)
     flux = level.y_flux(lo - 1, field(lo - 1), first)
@@ -104,64 +127,74 @@
         u, flux_low = carry
         high = field(y + 1)
         image, flux_y = level.apply(y, u, high, flux_low)
-        store(y, u, image)
-        return high, flux_y
-
-    lax.fori_loop(lo, hi, row, (first, flux))
-
-
-def smooth_down(level, lo, hi, r, r1, u1, x, finish):
+        return (high, flux_y), store(y, u, image)
+
+    rows(lo, hi, row, (first, flux))
+
+
+def smooth_down(level, lo, hi, r, r1, u1, x, r2):
     def start(y):
-        return level.dinv[y] * r[y] / THETA
+        return level.dinv[y] * r[y] * (1.0 / THETA)
 
     def first(y, u, image):
         rest = r[y] - image
-        r1[y] = rest
         after = C1U * u + C1R * (level.dinv[y] * rest)
-        u1[y] = after
-        x[y] = u + after
+        return [(r1, y, rest), (u1, y, after), (x, y, u + after)]
 
     sweep(level, lo, hi, start, first)
-    sweep(level, lo + 1, hi - 1, lambda y: u1[y], lambda y, u, image: finish(y, r1[y] - image))
+    sweep(level, lo + 1, hi - 1, lambda y: u1[y], lambda y, u, image: [(r2, y, r1[y] - image)])
 
 
 def smooth_up(level, lo, hi, e, r2, r3, u, x, finish):
     def first(y, own, image):
         rest = r2[y] - image
-        r3[y] = rest
-        u[y] = level.dinv[y] * rest / THETA
+        return [(r3, y, rest), (u, y, level.dinv[y] * rest * (1.0 / THETA))]
 
     sweep(level, lo, hi, e, first)
 
     def second(y, own, image):
         rest = r3[y] - image
         after = C1U * own + C1R * (level.dinv[y] * rest)
-        finish(y, (x[y] + e(y)) + (own + after))
+        return finish(y, (x[y] + e(y)) + (own + after))
 
     sweep(level, lo + 1, hi - 1, lambda y: u[y], second)
 
 
-def down(fine, mid, r, r1, u1, x, r2, b1, r1m, u1m, xm, r2m, b2):
-    def keep(y, rest):
-        r2[y] = rest
-
-    smooth_down(fine, 3, 37, r, r1, u1, x, keep)
-
-    def restrict(y, carry):
-        b1[y] = sum_x(sum_z(r2[2 * y] + r2[2 * y + 1], 1), 1)
-        return carry
-
-    lax.fori_loop(2, 18, restrict, 0)
-
-    def keep_mid(y, rest):
-        r2m[y] = rest
-
-    smooth_down(mid, 3, 17, b1, r1m, u1m, xm, keep_mid)
-    for k in range(4):
-        b2[k] = sum_x(sum_z(r2m[2 * k + 6] + r2m[2 * k + 7], 2), 2)
-
-
-def setup_kernel(pos, it, src, rea, wx, wy, wz, c, dinv, wx1, wy1, wz1, c1, dinv1, r, x, r2, xm, r2m, pay, r1, u1, b1, r1m, u1m):
+def down(fine, mid, r, x, r2, xm, r2m, r1, u1, b1, r1m, u1m):
+    smooth_down(fine, 3, 37, r, r1, u1, x, r2)
+    rows(2, 18, lambda y, c: (c, [(b1, y, sum_x(sum_z(r2[2 * y] + r2[2 * y + 1], 1), 1))]), 0)
+    smooth_down(mid, 3, 17, b1, r1m, u1m, xm, r2m)
+    return to_line([sum_x(sum_z(r2m[2 * k + 6] + r2m[2 * k + 7], 2), 2) for k in range(4)])
+
+
+def to_line(rows):
+    spread = lax.broadcasted_iota(jnp.int32, (128, 256), 1) % 16 * 4 == lax.broadcasted_iota(jnp.int32, (128, 256), 0)
+    spread = jnp.where(spread, 1.0, 0.0)
+    at = lax.broadcasted_iota(jnp.int32, (NB, 256), 1) // 16
+    z = lax.broadcasted_iota(jnp.int32, (NB, 256), 0)
+    line = jnp.zeros((1, 256), F32)
+    for y in range(4):
+        wide = jnp.dot(rows[y], spread, precision=lax.Precision.HIGHEST, preferred_element_type=F32)
+        mine = (at // 4 == y) & (z == M + 4 * (at % 4))
+        line = line + jnp.sum(jnp.where(mine, wide, 0.0), axis=0, keepdims=True)
+    return line
+
+
+def levels_of(coef, coef1):
+    return Level(*(coef.at[k] for k in range(5)), 1), Level(*(coef1.at[k] for k in range(5)), 2)
+
+
+def cycle_of(cycle, cycle1):
+    return cycle.at[0], cycle.at[1], cycle1.at[0], cycle1.at[1]
+
+
+def setup_kernel(pos, fields, coef, coef1, rq, cycle, cycle1, kept, pay, *scratch):
+    it, src, rea, r = fields.at[0], fields.at[1], fields.at[2], rq.at[0]
+    fine, mid = levels_of(coef, coef1)
+    wx, wy, wz, c, dinv = fine.wx, fine.wy, fine.wz, fine.c, fine.dinv
+    wx1, wy1, wz1, c1, dinv1 = mid.wx, mid.wy, mid.wz, mid.c, mid.dinv
+    for k in range(3):
+        kept[k] = fields[k, M - 1 : M + B + 1]
     gy, zb = pos[0], pos[1]
     zg = ziota() + (zb * B - M)
     lane = xiota()
@@ -181,7 +214,6 @@
         w_z, p_z = weight(up_z(here) - here)
         inside = inside_zx & (yg >= 0) & (yg < NY)
         rest = src[y] - rea[y] * here + ((p_x - dn_x(p_x)) + (p_y - flow_low) + (p_z - dn_z(p_z)))
-        r[y] = jnp.where(inside, rest, 0.0)
         outer = rea[y] + jnp.where(lane == 0, dn_x(w_x), 0.0) + jnp.where(lane == NX - 1, w_x, 0.0)
         outer = outer + jnp.where(zg == 0, dn_z(w_z), 0.0) + jnp.where(zg == NZ - 1, w_z, 0.0)
         outer = outer + jnp.where(yg == 0, wy_low, 0.0) + jnp.where(yg == NY - 1, w_y, 0.0)
@@ -189,14 +221,14 @@
         m_x = jnp.where(inside & (lane < NX - 1), w_x, 0.0)
         m_y = jnp.where(inside & (yg < NY - 1), w_y, 0.0)
         m_z = jnp.where(inside & (zg < NZ - 1), w_z, 0.0)
-        wx[y], wy[y], wz[y], c[y] = m_x, m_y, m_z, outer
         diagonal = outer + m_x + dn_x(m_x) + m_y + wym_low + m_z + dn_z(m_z)
         good = diagonal > 0.0
-        dinv[y] = jnp.where(good, 1.0 / jnp.where(good, diagonal, 1.0), 0.0)
-        return p_y, w_y, m_y
+        inverse = jnp.where(good, 1.0 / jnp.where(good, diagonal, 1.0), 0.0)
+        stores = [(r, y, jnp.where(inside, rest, 0.0)), (wx, y, m_x), (wy, y, m_y), (wz, y, m_z), (c, y, outer)]
+        return (p_y, w_y, m_y), stores + [(dinv, y, inverse)]
 
     zero = jnp.zeros((NB, 128), F32)
-    lax.fori_loop(0, NB - 1, row, (zero, zero, zero))
+    rows(0, NB - 1, row, (zero, zero, zero), 2)
     for ref in (wx, wy, wz, c, dinv, r):
         ref[NB - 1] = zero
 
@@ -206,27 +238,19 @@
         m_y = sum_x(sum_z(wy[b], 1), 1)
         m_z = sum_x(odd_z(wz[a] + wz[b], 1), 1)
         m_c = sum_x(sum_z(c[a] + c[b], 1), 1)
-        wx1[y], wy1[y], wz1[y], c1[y] = m_x, m_y, m_z, m_c
         diagonal = m_c + m_x + dn_x(m_x, 2) + m_y + low + m_z + dn_z(m_z, 2)
         good = diagonal > 0.0
-        dinv1[y] = jnp.where(good, 1.0 / jnp.where(good, diagonal, 1.0), 0.0)
-        return m_y
-
-    lax.fori_loop(0, NB // 2, row1, zero)
-    fine = Level(wx, wy, wz, c, dinv, 1)
-    mid = Level(wx1, wy1, wz1, c1, dinv1, 2)
-
-    class Part:
-        def __setitem__(self, k, value):
-            pay[k] = value
-
-    down(fine, mid, r, r1, u1, x, r2, b1, r1m, u1m, xm, r2m, Part())
-    for k in range(4):
-        a, b = 2 * k + 6, 2 * k + 7
-        pay[4 + k] = sum_z(odd_x(wx1[a] + wx1[b], 2), 2)
-        pay[8 + k] = sum_x(sum_z(wy1[b], 2), 2)
-        pay[12 + k] = sum_x(odd_z(wz1[a] + wz1[b], 2), 2)
-        pay[16 + k] = sum_x(sum_z(c1[a] + c1[b], 2), 2)
+        inverse = jnp.where(good, 1.0 / jnp.where(good, diagonal, 1.0), 0.0)
+        return m_y, [(wx1, y, m_x), (wy1, y, m_y), (wz1, y, m_z), (c1, y, m_c), (dinv1, y, inverse)]
+
+    rows(0, NB // 2, row1, zero, 2)
+
+    pay[:, 0:256] = down(fine, mid, r, *cycle_of(cycle, cycle1), *scratch)
+    pair = [(2 * k + 6, 2 * k + 7) for k in range(4)]
+    pay[:, 256:512] = to_line([sum_z(odd_x(wx1[a] + wx1[b], 2), 2) for a, b in pair])
+    pay[:, 512:768] = to_line([sum_x(sum_z(wy1[b], 2), 2) for a, b in pair])
+    pay[:, 768:1024] = to_line([sum_x(odd_z(wz1[a] + wz1[b], 2), 2) for a, b in pair])
+    pay[:, 1024:1280] = to_line([sum_x(sum_z(c1[a] + c1[b], 2), 2) for a, b in pair])
 
 
 def lane_ids():
@@ -297,9 +321,9 @@
     return planes(n, one)
 
 
-def coefficients_kernel(got, k2, k3):
+def coefficients(got, k2, k3):
     for f in range(4):
-        k2[f] = got[f].T
+        k2[f] = got[:, 256 * (f + 1) : 256 * (f + 2)].T
 
     def field(f):
         return lambda y, z: k2[f, pl.ds((y * 4 + z) * 16, 16), :]
@@ -331,9 +355,7 @@
     return planes(n, lambda y, z: f(*(a[y][z] for a in lists)))
 
 
-def coarse_solve(got, k2, k3, b2t):
-    b2t[...] = got.T
-
+def coarse_solve(k2, k3, b2t):
     def field(ref, n, f):
         return lambda y, z: ref[f, pl.ds((y * n + z) * 16, 16), :]
 
@@ -390,44 +412,49 @@
         e2[y2] = plane
 
 
-def up_kernel(pos, got, k2, k3, wx, wy, wz, c, dinv, wx1, wy1, wz1, c1, dinv1, x, r2, xm, r2m, out, b2t, e2, r3m, um, x1, r3, u):
-    place_coarse(pos, coarse_solve(got[...], k2, k3, b2t), e2)
-    fine = Level(wx, wy, wz, c, dinv, 1)
-    mid = Level(wx1, wy1, wz1, c1, dinv1, 2)
-
-    def keep(y, value):
-        x1[y] = value
-
-    smooth_up(mid, 4, 16, lambda y: e2[y // 2], r2m, r3m, um, xm, keep)
+def up(pos, k2, k3, b2t, fine, mid, x, r2, xm, r2m, out, e2, r3, u, x1, r3m, um):
+    place_coarse(pos, coarse_solve(k2, k3, b2t), e2)
+    smooth_up(mid, 4, 16, lambda y: e2[y // 2], r2m, r3m, um, xm, lambda y, value: [(x1, y, value)])
 
     def result(y, value):
-        out[y - M] = dn_z(value, -M)[:B]
+        return [(out, y - M, dn_z(value, -M)[:B])]
 
     smooth_up(fine, 11, 29, lambda y: x1[y // 2], r2, r3, u, x, result)
 
 
-def image_kernel(z, r, wx, wy, wz, c, w, dots):
-    fine = Level(wx, wy, wz, c, None, 1)
-
-    def keep(y, u, image):
-        w[y] = image
-
-    sweep(fine, 2, 38, lambda y: z[y], keep)
+def first_kernel(pos, got, coef, coef1, cycle, cycle1, out, k2, k3, b2t, *scratch):
+    fine, mid = levels_of(coef, coef1)
+    coefficients(got, k2, k3)
+    b2t[...] = got[:, 0:256].T
+    up(pos, k2, k3, b2t, fine, mid, *cycle_of(cycle, cycle1), out, *scratch)
+
+
+def image_kernel(last, centre, low, high, rq, coef, coef1, z_kept, w, pay, z, *scratch):
+    fine, mid = levels_of(coef, coef1)
+    z[0:M] = low[...]
+    z[M : M + B] = centre[...]
+    z[M + B : NB] = high[...]
+    z_kept[...] = z[M - 1 : M + B + 1]
+    lo, hi = (M, M + B) if last else (2, 38)
+    sweep(fine, lo, hi, lambda y: z[y], lambda y, u, image: [(w, y, image)])
     own = (ziota() >= M) & (ziota() < M + B)
 
     def row(y, carry):
         a, b = carry
         here = jnp.where(own, z[y], 0.0)
-        return a + r[y] * here, b + here * w[y]
+        return (a + rq[0, y] * here, b + here * w[y]), []
 
     zero = jnp.zeros((NB, 128), F32)
-    a, b = lax.fori_loop(M, M + B, row, (zero, zero))
-    lane = lax.broadcasted_iota(jnp.int32, (8, 128), 1)
-    dots[...] = jnp.where(lane == 0, jnp.sum(a), jnp.where(lane == 1, jnp.sum(b), 0.0))
+    a, b = rows(M, M + B, row, (zero, zero))
+    lane = lax.broadcasted_iota(jnp.int32, (1, 128), 1)
+    pay[:, 0:128] = jnp.where(lane == 0, jnp.sum(a), jnp.where(lane == 1, jnp.sum(b), 0.0))
+    if not last:
+        cycle, cycle1 = scratch[:2]
+        pay[:, 128:384] = down(fine, mid, w, *cycle_of(cycle, cycle1), *scratch[2:])
 
 
 def step_sizes(got, old, scal, first):
-    total = jnp.sum(got[...], axis=0, keepdims=True)
+    total = jnp.sum(got[:, 0:128], axis=0, keepdims=True)
     lane = lax.broadcasted_iota(jnp.int32, (1, 128), 1)
 
     def pick(v, k):
@@ -448,46 +475,46 @@
     return alpha, beta
 
 
-def update_kernel(first, got, old, z, w, r, q, p, d, wx, wy, wz, c, dinv, wx1, wy1, wz1, c1, dinv1,
-                  scal, r_o, q_o, p_o, d_o, x, r2, xm, r2m, pay, r1, u1, b1, r1m, u1m):
+def step_kernel(first, pos, got, old, z, w, b2_was, rq, *refs):
+    pd, refs = (None, refs) if first else (refs[0], refs[1:])
+    coef, coef1, k2, k3, scal, rq_o, pd_o, out, pay, b2q, b2t, cycle, cycle1, e2, *scratch = refs
+    fine, mid = levels_of(coef, coef1)
     alpha, beta = step_sizes(got, old, scal, first)
 
     def row(y, carry):
-        q_y = w[y] if first else w[y] + beta * q[y]
-        q_o[y] = q_y
-        r_o[y] = r[y] - alpha * q_y
-        return carry
-
-    lax.fori_loop(2, 38, row, 0)
+        q = w[y] if first else w[y] + beta * rq[1, y]
+        return carry, [(rq_o, (1, y), q), (rq_o, (0, y), rq[0, y] - alpha * q)]
+
+    rows(2, 38, row, 0)
 
     def row_d(y, carry):
-        p_y = z[y] if first else z[y] + beta * p[y]
-        p_o[y] = p_y
-        d_o[y] = alpha * p_y if first else d[y] + alpha * p_y
-        return carry
-
-    lax.fori_loop(M - 1, M + B + 1, row_d, 0)
-    fine = Level(wx, wy, wz, c, dinv, 1)
-    mid = Level(wx1, wy1, wz1, c1, dinv1, 2)
-    down(fine, mid, r_o, r1, u1, x, r2, b1, r1m, u1m, xm, r2m, pay)
-
-
-def finish_kernel(pos, steps, got, old, z, w, r, q, p, d, it, src, rea, d_out, r_out, layers, d_all):
+        p = z[y] if first else z[y] + beta * pd[0, y]
+        return carry, [(pd_o, (0, y), p), (pd_o, (1, y), alpha * p if first else pd[1, y] + alpha * p)]
+
+    rows(0, B + 2, row_d, 0)
+    x, r2, xm, r2m = cycle_of(cycle, cycle1)
+    pay[...] = down(fine, mid, rq_o.at[0], x, r2, xm, r2m, *scratch)
+    alpha2 = jnp.concatenate([alpha, alpha], axis=1)
+    if first:
+        b2q[...] = got[:, 128:384].T
+        b2t[...] = b2_was[...] - alpha2 * b2q[...]
+    else:
+        beta2 = jnp.concatenate([beta, beta], axis=1)
+        b2q[...] = got[:, 128:384].T + beta2 * b2_was[...]
+        b2t[...] = got[:, 384:640].T - alpha2 * b2q[...]
+    up(pos, k2, k3, b2t, fine, mid, x, r2, xm, r2m, out, e2, *scratch)
+
+
+def finish_kernel(pos, steps, got, old, z, w, rq, pd, kept, d_out, r_out, layers, d_all):
     alpha, beta = step_sizes(got, old, None, False)
     gy, zb = pos[0], pos[1]
-
-    def row_d(y, carry):
-        d_all[y] = d[y] + alpha * (z[y] + beta * p[y])
-        return carry
-
-    lax.fori_loop(M - 1, M + B + 1, row_d, 0)
+    rows(0, B + 2, lambda y, c: (c, [(d_all, y, pd[1, y] + alpha * (z[y] + beta * pd[0, y]))]), 0)
 
     def row(y, carry):
-        r_out[y - M] = dn_z(r[y] - alpha * (w[y] + beta * q[y]), -M)[:B]
-        d_out[y - M] = dn_z(d_all[y], -M)[:B]
-        return carry
-
-    lax.fori_loop(M, M + B, row, 0)
+        r = rq[0, y + M] - alpha * (w[y + M] + beta * rq[1, y + M])
+        return carry, [(r_out, y, dn_z(r, -M)[:B]), (d_out, y, dn_z(d_all[y + 1], -M)[:B])]
+
+    rows(0, B, row, 0)
     zi = ziota()
     own = (zi >= M) & (zi < M + B)
     own_z = own | ((zi == M + B) & (zb == NZB - 1))
@@ -502,19 +529,19 @@
         step = steps[k]
 
         def trial(y):
-            return it[y] + step * d_all[y]
+            return kept[0, y] + step * d_all[y]
 
         def row(y, carry):
             low, acc_x, acc = carry
             v = trial(y)
             acc_x = acc_x + jnp.where(own, energy(v - dn_x(v)), 0.0)
-            part = energy(v - low) + (0.5 * rea[y] * v * v - src[y] * v)
+            part = energy(v - low) + (0.5 * kept[2, y] * v * v - kept[1, y] * v)
             acc = acc + jnp.where(own, part, 0.0) + jnp.where(own_z, energy(v - dn_z(v)), 0.0)
-            return v, acc_x, acc
-
-        v, acc_x, acc = lax.fori_loop(M, M + B, row, (trial(M - 1), zero, zero))
+            return (v, acc_x, acc), []
+
+        v, acc_x, acc = rows(1, B + 1, row, (trial(0), zero, zero), 2)
         last = own & (gy == NGY - 1)
-        acc = acc + jnp.where(last, energy(trial(M + B) - v), 0.0)
+        acc = acc + jnp.where(last, energy(trial(B + 1) - v), 0.0)
         sum_of_x = jnp.sum(acc_x, axis=0, keepdims=True)
         top = jnp.where(lane == NX - 1, jnp.broadcast_to(roll(jnp.broadcast_to(sum_of_x, (8, 128)), -1, 1)[0:1], (1, 128)), 0.0)
         layers[k] = jnp.broadcast_to(sum_of_x + top + jnp.sum(acc, axis=0, keepdims=True), (8, 128))
@@ -524,7 +551,7 @@
 SM = pl.BlockSpec(memory_space=pltpu.SMEM)
 
 
-def call(kernel, n_scalar, outs, scratch, name):
+def call(kernel, n_scalar, outs, scratch, name, aliases={}):
     def run(*args):
         return pl.pallas_call(
             kernel,
@@ -532,6 +559,8 @@
             out_specs=[VM] * len(outs),
             out_shape=[jax.ShapeDtypeStruct(s, F32) for s in outs],
             scratch_shapes=[pltpu.VMEM(s, F32) for s in scratch],
+            input_output_aliases=aliases,
+            compiler_params=pltpu.CompilerParams(vmem_limit_bytes=LIMIT),
             interpret=INTERPRET,
             name=name,
         )(*args)
@@ -541,7 +570,12 @@
 
 FINE = (NB, NB, 128)
 MID = (NB // 2, NB, 128)
-DOWN_SCRATCH = [FINE, FINE, MID, MID, MID]
+KEPT = (B + 2, NB, 128)
+SCRATCH = [FINE, FINE, MID, MID, MID]
+CYCLE = [(2, *FINE), (2, *MID)]
+COEFS = [(5, *FINE), (5, *MID)]
+COARSE = (NB // 4, NB, 128)
+PLANES = (256, NDEV)
 
 
 def shift_pairs(dy, dz):
@@ -556,15 +590,16 @@
     return pairs
 
 
-def exchange(own):
-    ax = own.ndim - 2
-    low = lax.ppermute(lax.slice_in_dim(own, B - M, B, axis=ax), ALL, shift_pairs(0, 1))
-    high = lax.ppermute(lax.slice_in_dim(own, 0, M, axis=ax), ALL, shift_pairs(0, -1))
-    own = jnp.concatenate([low, own, high], axis=ax)
-    ax = own.ndim - 3
-    low = lax.ppermute(lax.slice_in_dim(own, B - M, B, axis=ax), ALL, shift_pairs(1, 0))
-    high = lax.ppermute(lax.slice_in_dim(own, 0, M, axis=ax), ALL, shift_pairs(-1, 0))
-    return jnp.concatenate([low, own, high], axis=ax)
+def exchange_z(own):
+    low = lax.ppermute(own, ALL, shift_pairs(0, 1))
+    high = lax.ppermute(own, ALL, shift_pairs(0, -1))
+    return jnp.concatenate([low[..., B - M :, :], own, high[..., :M, :]], axis=-2)
+
+
+def exchange_y(own):
+    low = lax.ppermute(own[..., B - M :, :, :], ALL, shift_pairs(1, 0))
+    high = lax.ppermute(own[..., :M, :, :], ALL, shift_pairs(-1, 0))
+    return low, high
 
 
 def to_everyone(x):
@@ -572,9 +607,13 @@
     return lax.all_to_all(copies, ALL, split_axis=0, concat_axis=0, tiled=True)
 
 
-def compact(pay):
-    kept = pay[:, M : M + B : 4, 0:NX:4]
-    return kept.reshape(-1, 256)
+def to_everyone_by_axes(line):
+    n = line.shape[1]
+    copies = jnp.broadcast_to(line, (NGX, 1, n))
+    got = lax.all_to_all(copies, "gx", split_axis=0, concat_axis=0, tiled=True)
+    copies = jnp.broadcast_to(got.reshape(NGX, n), (NDEV // NGX, NGX, n))
+    got = lax.all_to_all(copies, (*GY, "gz"), split_axis=0, concat_axis=0, tiled=True)
+    return got.transpose(1, 0, 2).reshape(NDEV, n)
 
 
 def on_device(iterate, source, reaction, trial_powers):
@@ -587,42 +626,45 @@
     fields = fields.reshape(3, 8, 16, 8, 16).transpose(3, 1, 0, 2, 4).reshape(8, 8, 3, 256)
     fields = lax.all_to_all(fields, "gx", split_axis=0, concat_axis=0, tiled=True)
     fields = fields.reshape(NX, 3 * 256).T.reshape(3, 16, 16, NX)
-    fields = exchange(jnp.pad(fields, ((0, 0), (0, 0), (0, 0), (0, 128 - NX))))
-    it, src, rea = fields[0], fields[1], fields[2]
-    coefs_and_rest = call(
-        setup_kernel, 1, [FINE] * 5 + [MID] * 5 + [FINE] * 3 + [MID] * 2 + [(20, NB, 128)], DOWN_SCRATCH, "setup"
-    )(pos, it, src, rea)
-    fine, mid = coefs_and_rest[:5], coefs_and_rest[5:10]
-    r, x, r2, xm, r2m, pay = coefs_and_rest[10:]
-    got = to_everyone(compact(pay))
-    k2, k3 = call(coefficients_kernel, 0, [(5, 256, NDEV), (5, 64, NDEV)], [], "coefficients")(
-        got[:, 1:].transpose(1, 0, 2)
-    )
-    got = got[:, 0]
-    up = call(up_kernel, 1, [(B, B, 128)], [(256, NDEV), (NB // 4, NB, 128), MID, MID, MID, FINE, FINE], "up")
-    image = call(image_kernel, 0, [FINE, (8, 128)], [], "image")
-    q = p = d = r
+    fields = exchange_z(jnp.pad(fields, ((0, 0), (0, 0), (0, 0), (0, 128 - NX))))
+    low, high = exchange_y(fields)
+    fields = jnp.concatenate([low, fields, high], axis=1)
+    coef, coef1, rq, cycle, cycle1, kept, pay = call(
+        setup_kernel, 1, COEFS + [(2, *FINE)] + CYCLE + [(3, *KEPT), (1, 1280)], SCRATCH, "setup"
+    )(pos, fields)
+    own = (B, B, 128)
+    z, k2, k3, b2 = call(
+        first_kernel, 1, [own, (5, 256, NDEV), (5, 64, NDEV), PLANES], [COARSE] + SCRATCH, "first"
+    )(pos, to_everyone_by_axes(pay), coef, coef1, cycle, cycle1)
     scal = jnp.zeros((8, 128), F32)
+    pd = None
     for i in range(ITERS):
-        (z,) = up(pos, got, k2, k3, *fine, *mid, x, r2, xm, r2m)
-        z = exchange(z)
-        w, dots = image(z, r, *fine[:4])
-        dots = to_everyone(dots[0:1])[:, 0]
-        if i + 1 < ITERS:
-            update = call(
-                lambda *refs, first=i == 0: update_kernel(first, *refs), 0,
-                [(8, 128)] + [FINE] * 6 + [MID] * 2 + [(4, NB, 128)], DOWN_SCRATCH, "update",
-            )
-            scal, r, q, p, d, x, r2, xm, r2m, pay = update(dots, scal, z, w, r, q, p, d, *fine, *mid)
-            got = to_everyone(compact(pay))[:, 0]
-    own = (B, B, 128)
-    d_own, r_own, layers = call(finish_kernel, 2, [own, own, (TRIALS, 8, 128)], [FINE], "finish")(
-        pos, steps, dots, scal, z, w, r, q, p, d, it, src, rea
+        first, last = i == 0, i + 1 == ITERS
+        centre = exchange_z(z)
+        low, high = exchange_y(centre)
+        z, w, line = call(
+            functools.partial(image_kernel, last), 0, [KEPT, FINE, (1, 128 if last else 384)],
+            [FINE] + ([] if last else CYCLE + SCRATCH), "image",
+        )(centre, low, high, rq, coef, coef1)
+        if last:
+            break
+        if not first:
+            line = jnp.concatenate([line, pay], axis=1)
+        got = to_everyone(line)[:, 0]
+        state = (rq,) if first else (rq, pd)
+        scal, rq, pd, z, pay, b2 = call(
+            functools.partial(step_kernel, first), 1,
+            [(8, 128), (2, *FINE), (2, *KEPT), own, (1, 256), PLANES], [PLANES] + CYCLE + [COARSE] + SCRATCH, "step",
+            {6: 1} if first else {6: 1, 7: 2},
+        )(pos, got, scal, z, w, b2, *state, coef, coef1, k2, k3)
+    dots = to_everyone(line)[:, 0]
+    d_own, r_own, layers = call(finish_kernel, 2, [own, own, (TRIALS, 8, 128)], [KEPT], "finish")(
+        pos, steps, dots, scal, z, w, rq, pd, kept
     )
     both = jnp.stack([d_own, r_own])[..., :NX].reshape(512, NX).T
     both = lax.all_to_all(both.reshape(8, 8, 512), "gx", split_axis=0, concat_axis=0, tiled=True)
     both = both.reshape(8, 8, 2, 16, 16).transpose(2, 1, 3, 0, 4).reshape(2, 8, 16, 128)
-    layers = to_everyone(layers[:, 0, :NX].reshape(2, 128)).sum(axis=0).reshape(TRIALS, NX) / (NY * NZ)
+    layers = to_everyone(layers[:, 0, :NX].reshape(1, 256)).sum(axis=0).reshape(TRIALS, NX) / (NY * NZ)
     energies = jnp.sum(layers, axis=1) / NX
     mine = lax.dynamic_slice_in_dim(layers, gx * 8, 8, axis=1)
     return both[0], both[1], mine, energies

time: 629 us -> 425 us (0.68)
  Pallas kernels: 206 us -> 76 us
  blocking collectives: 213 us -> 148 us
  other arithmetic: 14.7 us -> 1.7 us
    pallas_call x14 -> x10, Pallas kernels: 206 us -> 76 us  [run(): pl.pallas_call(kernel, in_specs=[SM] * n_scalar + [VM] * (len(args) - n_s...]
    all_to_all x7 -> x3, blocking collectives: 195 us -> 89.1 us  [to_everyone(): return lax.all_to_all(copies, ALL, split_axis=0, concat_axis=0, tiled=True)]
    all_to_all x0 -> x2, blocking collectives: none -> 41 us  [the longest x1 27.2 us: to_everyone_by_axes(): lax.all_to_all(copies, (*GY, 'gz'), split_axis=0, concat_axis=0, tiled=True)]
    unnamed x11 -> x64, local copies, waits for them, and re-layouts: 4.74 us -> 20 us
    slice x21 -> x11, local copies, waits for them, and re-layouts: 13.3 us -> 1.24 us  [the longest x1 1 us: exchange_y(): low = lax.ppermute(own[..., B - M:, :, :], ALL, shift_pairs(1, 0))]
    concatenate x10 -> x8, other arithmetic: 11.6 us -> 0.47 us  [the longest x5 0.26 us: exchange_z(): jnp.concatenate([low[..., B - M:, :], own, high[..., :M, :]], axis=-2)]
where the time goes in v1:
time: 425 us; the launch traced here: 423 us
  blocking collectives  148 us (35%)
  waiting for transfers between devices  93.7 us (22%)
  Pallas kernels  76 us (18%)
  starting transfers between devices  71.7 us (17%)
  local copies, waits for them, and re-layouts  31.1 us (7%)
    all_to_all x3, blocking collectives, to_everyone(): return lax.all_to_all(copies, ALL, split_axis=0, concat_axis=0, tiled=True)  89.1 us
    pallas_call x10, Pallas kernels, run(): pl.pallas_call(kernel, in_specs=[SM] * n_scalar + [VM] * (len(args) - n_s...  76 us
    all_to_all x1, blocking collectives, to_everyone_by_axes(): lax.all_to_all(copies, (*GY, 'gz'), split_axis=0, concat_axis=0, tiled=True)  27.2 us
    all_to_all x2, waiting for transfers between devices, to_everyone(): return lax.all_to_all(copies, ALL, split_axis=0, concat_axis=0, tiled=True)  25.4 us
    ppermute x5, starting transfers between devices, exchange_y(): low = lax.ppermute(own[..., B - M:, :, :], ALL, shift_pairs(1, 0))  24 us
    ppermute x5, waiting for transfers between devices, exchange_y(): high = lax.ppermute(own[..., :M, :, :], ALL, shift_pairs(-1, 0))  21.7 us
    unnamed x64, local copies, waits for them, and re-layouts  20 us
    ppermute x5, waiting for transfers between devices, exchange_z(): high = lax.ppermute(own, ALL, shift_pairs(0, -1))  19.1 us
  transfers between devices with their start and end apart: 23, of which 23 were waited for; matrix products, arithmetic and copies ran while one was open for 1% of the time, Pallas kernels for 0%

profile of v1, /device:TPU:1, one launch (start us, length us, event | category | flops | bytes accessed | tf_op | source)
XLA Modules:
  0.0 423.5 jit_solution(17415410029405913458)
XLA Ops:
  3.3 17.8 %all_to_all.45 = f32[8,8,3,256]{3,1,2,0:T(8,128)S(1)} all-to-all(f32[8,8,3,256]{3,1,2,0:T(8,128)S(1)} %reshape.56), channel_id=1, replica_groups=mesh['gx'=8,'gy_0'=4,'gy_1'=2,'gz'=4] {'gx'}, dimensions={0} | all-to-all | bytes 393216 | tf_op jit(solution)/shard_map/all_to_all | solution.py:627
  21.3 1.9 collective-permute-start
  23.2 1.3 collective-permute-start.1
  24.5 4.4 %collective-permute-done = f32[3,16,16,128]{3,2,1,0:T(8,128)S(1)} collective-permute-done((f32[3,16,16,128]{3,2,1,0:T(8,128)S(1)}, f32[3,16,16,128]{3,2,1,0:T(8,128)S(1)}, u32[]{:S(2)}, u32[]{:S(2)}) %collective-permute-start) | collective-permute-done | bytes 393248 | tf_op jit(solution)/shard_map/ppermute | solution.py:594
  28.9 3.8 collective-permute-done.1
  33.8 7.0 %collective-permute-start.2 = (f32[3,12,40,128]{3,2,1,0:T(8,128)}, f32[3,12,40,128]{3,2,1,0:T(8,128)S(1)}, u32[]{:S(2)}, u32[]{:S(2)}) collective-permute-start(f32[3,12,40,128]{3,2,1,0:T(8,128)} %get-tuple-element.90), channel_id=1, source_target_pairs={{0,4},{32,36},{64,68},{96,100},{128,132},{160,164},{192,196},{224,... | collective-permute-start | bytes 2211848 | tf_op jit(solution)/shard_map/ppermute | solution.py:600
  40.8 1.9 collective-permute-start.3
  42.8 6.7 %collective-permute-done.2 = f32[3,12,40,128]{3,2,1,0:T(8,128)S(1)} collective-permute-done((f32[3,12,40,128]{3,2,1,0:T(8,128)}, f32[3,12,40,128]{3,2,1,0:T(8,128)S(1)}, u32[]{:S(2)}, u32[]{:S(2)}) %collective-permute-start.2) | collective-permute-done | bytes 737312 | tf_op jit(solution)/shard_map/ppermute | solution.py:600
  49.5 4.1 collective-permute-done.3
  53.8 12.9 %setup.1 = (f32[5,40,40,128]{3,2,1,0:T(8,128)S(1)}, f32[5,20,40,128]{3,2,1,0:T(8,128)S(1)}, f32[2,40,40,128]{3,2,1,0:T(8,128)S(1)}, f32[2,40,40,128]{3,2,1,0:T(8...) custom-call(s32[2]{0:T(128)S(1)} %pad_add_fusion.pos, ...), custom_call_target="tpu_custom_call" | custom-call | tf_op jit(solution)/shard_map/setup/pallas_call | solution.py:556
  66.6 1.9 copy-done
  68.6 1.2 copy-done.4
  69.8 1.2 copy-done.13
  73.0 13.8 %all_to_all.46 = f32[8,1,1280]{2,1,0:T(1,128)S(1)} all-to-all(f32[8,1,1280]{2,1,0:T(1,128)S(1)} %broadcast_in_dim.24), channel_id=1, replica_groups=mesh['gx'=8,'gy_0'=4,'gy_1'=2,'gz'=4] {'gx'}, dimensions={0} | all-to-all | bytes 81920 | tf_op jit(solution)/shard_map/all_to_all | solution.py:613
  86.9 27.2 %all_to_all.47 = f32[32,8,1280]{2,1,0:T(8,128)S(1)} all-to-all(f32[32,8,1280]{2,1,0:T(8,128)S(1)} %broadcast_in_dim.25), channel_id=1, replica_groups=mesh['gx'=8,'gy_0'=4,'gy_1'=2,'gz'=4] {'gy_0','gy_1','gz'}, dimensions={0} | all-to-all | bytes 2621440 | tf_op jit(solution)/shard_map/all_to_all | solution.py:615
  115.2 5.3 %first.1 = (f32[16,16,128]{2,1,0:T(8,128)S(1)}, f32[5,256,256]{2,1,0:T(8,128)S(1)}, f32[5,64,256]{2,1,0:T(8,128)S(1)}, f32[256,256]{1,0:T(8,128)S(1)}) custom-call(s32[2]{0:T(128)S(1)} %pad_add_fusion.pos, f32[256,1280]{1,0:T(8,128)S(1)} %bitcast.44, f32[5,40,40,128]{3,2,1,0:T(8,128)S(1)} %copy-done.1, ...), custom_call_target="tpu_custom_call" | custom-call | tf_op jit(solution)/shard_map/first/pallas_call | solution.py:556
  121.9 2.4 collective-permute-start.4
  124.2 1.3 collective-permute-start.5
  125.5 1.3 collective-permute-done.4
  126.8 3.8 collective-permute-done.5
  130.8 3.5 collective-permute-start.6
  134.3 1.9 collective-permute-start.7
  136.2 1.2 collective-permute-done.6.low
  137.4 4.4 %collective-permute-done.7.high = f32[12,40,128]{2,1,0:T(8,128)S(1)} collective-permute-done((f32[12,40,128]{2,1,0:T(8,128)S(1)}, f32[12,40,128]{2,1,0:T(8,128)S(1)}, u32[]{:S(2)}, u32[]{:S(2)}) %collective-permute-start.7) | collective-permute-done | bytes 245792 | tf_op jit(solution)/shard_map/ppermute | solution.py:601
  141.8 6.9 %image.4 = (f32[18,40,128]{2,1,0:T(8,128)S(1)}, f32[40,40,128]{2,1,0:T(8,128)S(1)}, f32[1,384]{1,0:T(1,128)S(1)}) custom-call(f32[16,40,128]{2,1,0:T(8,128)S(1)} %pad_maximum_fusion.2.centre, f32[12,40,128]{2,1,0:T(8,128)S(1)} %collective-permute-done.6.low, f32[12,40,128]{2,1,0:T(8,128)S(1)} %collective-permute-done.7.high, ...), custom_call_target="tpu_custom_call" | custom-call | tf_op jit(solution)/shard_map/image/pallas_call | solution.py:556
  150.6 26.8 %all_to_all.48 = f32[256,1,384]{2,1,0:T(1,128)S(1)} all-to-all(f32[256,1,384]{2,1,0:T(1,128)S(1)} %broadcast_in_dim.26), channel_id=1, replica_groups=mesh['gx'=8,'gy_0'=4,'gy_1'=2,'gz'=4] {'gx','gy_0','gy_1','gz'}, dimensions={0} | all-to-all | bytes 786432 | tf_op jit(solution)/shard_map/all_to_all | solution.py:607
  177.5 2.2 copy-done.2
  179.6 1.1 copy-done.22
  182.7 10.2 %step.3 = (f32[8,128]{1,0:T(8,128)S(1)}, f32[2,40,40,128]{3,2,1,0:T(8,128)S(1)}, f32[2,18,40,128]{3,2,1,0:T(8,128)S(1)}, f32[16,16,128]{2,1,0:T(8,128)S(1)}, f32...) custom-call(s32[2]{0:T(128)S(1)} %pad_add_fusion.pos, f32[256,384]{1,0:T(8,128)S(1)} %bitcast.47, ...), custom_call_target="tpu_custom_call", output_to_operand_aliasing={{1}: (6, {})} | custom-call | tf_op jit(solution)/shard_map/step/pallas_call | solution.py:556
  192.9 2.6 collective-permute-start.8
  195.5 1.3 collective-permute-start.9
  197.4 3.8 collective-permute-done.9
  201.3 4.9 %collective-permute-start.10 = (f32[12,40,128]{2,1,0:T(8,128)S(1)}, f32[12,40,128]{2,1,0:T(8,128)S(1)}, u32[]{:S(2)}, u32[]{:S(2)}) collective-permute-start(f32[12,40,128]{2,1,0:T(8,128)S(1)} %get-tuple-element.97), channel_id=1, source_target_pairs={{0,4},{32,36},{64,68},{96,100},{128,132},{160,164},{192,196},{224,... | collective-permute-start | bytes 737288 | tf_op jit(solution)/shard_map/ppermute | solution.py:600
  206.2 1.9 collective-permute-start.11
  208.1 1.2 collective-permute-done.10.low
  209.3 4.4 %collective-permute-done.11.high = f32[12,40,128]{2,1,0:T(8,128)S(1)} collective-permute-done((f32[12,40,128]{2,1,0:T(8,128)S(1)}, f32[12,40,128]{2,1,0:T(8,128)S(1)}, u32[]{:S(2)}, u32[]{:S(2)}) %collective-permute-start.11) | collective-permute-done | bytes 245792 | tf_op jit(solution)/shard_map/ppermute | solution.py:601
  213.7 6.9 %image.5 = (f32[18,40,128]{2,1,0:T(8,128)S(1)}, f32[40,40,128]{2,1,0:T(8,128)S(1)}, f32[1,384]{1,0:T(1,128)S(1)}) custom-call(f32[16,40,128]{2,1,0:T(8,128)S(1)} %pad_maximum_fusion.3.centre, f32[12,40,128]{2,1,0:T(8,128)S(1)} %collective-permute-done.10.low, f32[12,40,128]{2,1,0:T(8,128)S(1)} %collective-permute-done.11.high, ...), custom_call_target="tpu_custom_call" | custom-call | tf_op jit(solution)/shard_map/image/pallas_call | solution.py:556
  221.0 31.3 %all_to_all.49 = f32[256,1,640]{2,1,0:T(1,128)S(1)} all-to-all(f32[256,1,640]{2,1,0:T(1,128)S(1)} %broadcast_in_dim.28), channel_id=1, replica_groups=mesh['gx'=8,'gy_0'=4,'gy_1'=2,'gz'=4] {'gx','gy_0','gy_1','gz'}, dimensions={0} | all-to-all | bytes 1310720 | tf_op jit(solution)/shard_map/all_to_all | solution.py:607
  252.3 10.4 %step.4 = (f32[8,128]{1,0:T(8,128)S(1)}, f32[2,40,40,128]{3,2,1,0:T(8,128)S(1)}, f32[2,18,40,128]{3,2,1,0:T(8,128)S(1)}, f32[16,16,128]{2,1,0:T(8,128)S(1)}, f32...) custom-call(s32[2]{0:T(128)S(1)} %pad_add_fusion.pos, ...), custom_call_target="tpu_custom_call", output_to_operand_aliasing={{1}: (6, {}), {2}: (7, {})} | custom-call | tf_op jit(solution)/shard_map/step/pallas_call | solution.py:556
  262.7 2.9 collective-permute-start.12
  265.6 1.3 collective-permute-start.13
  268.0 3.8 collective-permute-done.13
  271.9 4.3 %collective-permute-start.14 = (f32[12,40,128]{2,1,0:T(8,128)S(1)}, f32[12,40,128]{2,1,0:T(8,128)S(1)}, u32[]{:S(2)}, u32[]{:S(2)}) collective-permute-start(f32[12,40,128]{2,1,0:T(8,128)S(1)} %get-tuple-element.95), channel_id=1, source_target_pairs={{0,4},{32,36},{64,68},{96,100},{128,132},{160,164},{192,196},{224,... | collective-permute-start | bytes 737288 | tf_op jit(solution)/shard_map/ppermute | solution.py:600
  276.2 2.1 collective-permute-start.15
  279.3 4.4 %collective-permute-done.15.high = f32[12,40,128]{2,1,0:T(8,128)S(1)} collective-permute-done((f32[12,40,128]{2,1,0:T(8,128)S(1)}, f32[12,40,128]{2,1,0:T(8,128)S(1)}, u32[]{:S(2)}, u32[]{:S(2)}) %collective-permute-start.15) | collective-permute-done | bytes 245792 | tf_op jit(solution)/shard_map/ppermute | solution.py:601
  283.7 6.9 %image.6 = (f32[18,40,128]{2,1,0:T(8,128)S(1)}, f32[40,40,128]{2,1,0:T(8,128)S(1)}, f32[1,384]{1,0:T(1,128)S(1)}) custom-call(f32[16,40,128]{2,1,0:T(8,128)S(1)} %pad_maximum_fusion.4.centre, f32[12,40,128]{2,1,0:T(8,128)S(1)} %collective-permute-done.14.low, f32[12,40,128]{2,1,0:T(8,128)S(1)} %collective-permute-done.15.high, ...), custom_call_target="tpu_custom_call" | custom-call | tf_op jit(solution)/shard_map/image/pallas_call | solution.py:556
  291.0 31.0 %all_to_all.50 = f32[256,1,640]{2,1,0:T(1,128)S(1)} all-to-all(f32[256,1,640]{2,1,0:T(1,128)S(1)} %broadcast_in_dim.29), channel_id=1, replica_groups=mesh['gx'=8,'gy_0'=4,'gy_1'=2,'gz'=4] {'gx','gy_0','gy_1','gz'}, dimensions={0} | all-to-all | bytes 1310720 | tf_op jit(solution)/shard_map/all_to_all | solution.py:607
  322.1 11.2 %step.5 = (f32[8,128]{1,0:T(8,128)S(1)}, f32[2,40,40,128]{3,2,1,0:T(8,128)S(1)}, f32[2,18,40,128]{3,2,1,0:T(8,128)S(1)}, f32[16,16,128]{2,1,0:T(8,128)S(1)}, f32[1,256]{1,0:T(1,128)}, /*index=5*/f32[256,256]{1,0:T(8,128)}) custom-call(s32[2]{0:T(128)S(1)} %pad_add_fusion.pos, f32[256,640]{1,0:T(8,128)S(1)} %bitcast.45, ...), custom_call_target="tpu_custom_call", output_to_operand_aliasing={{1}: (6, {}), {2}: (7, {})} | custom-call | tf_op jit(solution)/shard_map/step/pallas_call | solution.py:556
  333.2 2.9 collective-permute-start.16
  336.1 1.3 collective-permute-start.17
  338.5 3.8 collective-permute-done.17
  342.4 4.3 %collective-permute-start.18 = (f32[12,40,128]{2,1,0:T(8,128)S(1)}, f32[12,40,128]{2,1,0:T(8,128)S(1)}, u32[]{:S(2)}, u32[]{:S(2)}) collective-permute-start(f32[12,40,128]{2,1,0:T(8,128)S(1)} %get-tuple-element.93), channel_id=1, source_target_pairs={{0,4},{32,36},{64,68},{96,100},{128,132},{160,164},{192,196},{224,... | collective-permute-start | bytes 737288 | tf_op jit(solution)/shard_map/ppermute | solution.py:600
  346.7 1.9 collective-permute-start.19
  348.7 1.2 collective-permute-done.18.low
  349.9 4.4 %collective-permute-done.19.high = f32[12,40,128]{2,1,0:T(8,128)S(1)} collective-permute-done((f32[12,40,128]{2,1,0:T(8,128)S(1)}, f32[12,40,128]{2,1,0:T(8,128)S(1)}, u32[]{:S(2)}, u32[]{:S(2)}) %collective-permute-start.19) | collective-permute-done | bytes 245792 | tf_op jit(solution)/shard_map/ppermute | solution.py:601
  356.8 8.6 %all-to-all-start.6 = ((f32[256,1,128]{2,1,0:T(1,128)}), f32[256,1,128]{2,1,0:T(1,128)S(1)}, u32[]{:S(2)}, u32[]{:S(2)}) async-start(f32[256,1,128]{2,1,0:T(1,128)} %broadcast_in_dim.30), calls=%async_computation.6 | async-start | bytes 262144 | tf_op jit(solution)/shard_map/all_to_all | solution.py:607
  365.4 12.8 %all-to-all-done.6 = f32[256,1,128]{2,1,0:T(1,128)S(1)} async-done(((f32[256,1,128]{2,1,0:T(1,128)}), f32[256,1,128]{2,1,0:T(1,128)S(1)}, u32[]{:S(2)}, u32[]{:S(2)}) %all-to-all-start.6) | async-done | bytes 131104 | tf_op jit(solution)/shard_map/all_to_all | solution.py:607
  378.2 1.4 copy-done.8
  380.8 1.1 copy-done.18
  381.9 4.6 %finish.1 = (f32[16,16,128]{2,1,0:T(8,128)S(1)}, f32[16,16,128]{2,1,0:T(8,128)S(1)}, f32[4,8,128]{2,1,0:T(8,128)S(1)}) custom-call(s32[2]{0:T(128)S(1)} %pad_add_fusion.pos, f32[4]{0:T(128)S(1)} %multiply_exponential_fusion.steps, f32[256,128]{1,0:T(8,128)S(1)} %bitcast.48, f32[8,128]{1,0:T(8,128)S(1)} %get-tuple-element.80.old, ...), custom_call_target="tpu_custom_call" | custom-call | tf_op jit(solution)/shard_map/finish/pallas_call | solution.py:556
  387.3 3.4 all-to-all-start.7
  390.8 7.8 %all-to-all-done.7 = f32[8,8,512]{2,1,0:T(8,128)S(1)} async-done(((f32[8,8,512]{2,1,0:T(8,128)}), f32[8,8,512]{2,1,0:T(8,128)S(1)}, u32[]{:S(2)}, u32[]{:S(2)}) %all-to-all-start.7) | async-done | bytes 131104 | tf_op jit(solution)/shard_map/all_to_all | solution.py:665
  399.4 7.0 %all-to-all-start.8 = ((f32[256,1,256]{2,1,0:T(1,128)}), f32[256,1,256]{2,1,0:T(1,128)S(1)}, u32[]{:S(2)}, u32[]{:S(2)}) async-start(f32[256,1,256]{2,1,0:T(1,128)} %broadcast_in_dim.31), calls=%async_computation.8 | async-start | bytes 524288 | tf_op jit(solution)/shard_map/all_to_all | solution.py:607
  409.2 12.6 %all-to-all-done.8 = f32[256,1,256]{2,1,0:T(1,128)S(1)} async-done(((f32[256,1,256]{2,1,0:T(1,128)}), f32[256,1,256]{2,1,0:T(1,128)S(1)}, u32[]{:S(2)}, u32[]{:S(2)}) %all-to-all-start.8) | async-done | bytes 262176 | tf_op jit(solution)/shard_map/all_to_all | solution.py:607
  (119 shorter events, 27.5 us)
Async XLA Ops:
  0.6 1.2 copy-start.27
  0.6 1.5 copy-start.28
  21.3 7.5 %collective-permute-start = (f32[3,16,16,128]{3,2,1,0:T(8,128)S(1)}, f32[3,16,16,128]{3,2,1,0:T(8,128)S(1)}, u32[]{:S(2)}, u32[]{:S(2)}) collective-permute-start(f32[3,16,16,128]{3,2,1,0:T(8,128)S(1)} %pad.4), channel_id=1, source_target_pairs={{0,32},{32,64},{64,96},{96,128},{128,160},{160,192},{192,224},{224... | collective-permute-start | bytes 1179656 | tf_op jit(solution)/shard_map/ppermute | solution.py:594
  23.2 9.5 %collective-permute-start.1 = (f32[3,16,16,128]{3,2,1,0:T(8,128)S(1)}, f32[3,16,16,128]{3,2,1,0:T(8,128)S(1)}, u32[]{:S(2)}, u32[]{:S(2)}) collective-permute-start(f32[3,16,16,128]{3,2,1,0:T(8,128)S(1)} %pad.4), channel_id=1, source_target_pairs={{32,0},{64,32},{96,64},{128,96},{160,128},{192,160},{224,192},{1,2... | collective-permute-start | bytes 1179656 | tf_op jit(solution)/shard_map/ppermute | solution.py:595
  33.8 15.7 %collective-permute-start.2 = (f32[3,12,40,128]{3,2,1,0:T(8,128)}, f32[3,12,40,128]{3,2,1,0:T(8,128)S(1)}, u32[]{:S(2)}, u32[]{:S(2)}) collective-permute-start(f32[3,12,40,128]{3,2,1,0:T(8,128)} %get-tuple-element.90), channel_id=1, source_target_pairs={{0,4},{32,36},{64,68},{96,100},{128,132},{160,164},{192,196},{224,... | collective-permute-start | bytes 2211848 | tf_op jit(solution)/shard_map/ppermute | solution.py:600
  40.8 12.8 %collective-permute-start.3 = (f32[3,12,40,128]{3,2,1,0:T(8,128)S(1)}, f32[3,12,40,128]{3,2,1,0:T(8,128)S(1)}, u32[]{:S(2)}, u32[]{:S(2)}) collective-permute-start(f32[3,12,40,128]{3,2,1,0:T(8,128)S(1)} %get-tuple-element.91), channel_id=1, source_target_pairs={{4,0},{36,32},{68,64},{100,96},{132,128},{164,160},{196,192},{228,... | collective-permute-start | bytes 2211848 | tf_op jit(solution)/shard_map/ppermute | solution.py:601
  66.6 1.9 copy-start
  68.6 1.2 copy-start.4
  69.8 1.2 copy-start.13
  71.0 1.1 copy-start.15
  72.0 0.9 copy-start.19
  86.8 27.7 %copy-start.14 = (f32[2,40,40,128]{3,2,1,0:T(8,128)S(1)}, f32[2,40,40,128]{3,2,1,0:T(8,128)}, u32[]{:S(2)}) copy-start(f32[2,40,40,128]{3,2,1,0:T(8,128)} %copy-done.13) | copy-start | bytes 4915204
  86.8 27.6 %copy-start.1 = (f32[5,40,40,128]{3,2,1,0:T(8,128)S(1)}, f32[5,40,40,128]{3,2,1,0:T(8,128)}, u32[]{:S(2)}) copy-start(f32[5,40,40,128]{3,2,1,0:T(8,128)} %copy-done) | copy-start | bytes 12288004
  114.0 1.1 copy-start.20
  120.5 0.7 copy-start.11
  121.2 0.7 copy-start.25
  121.9 19.9 %copy-start.5 = (f32[2,40,40,128]{3,2,1,0:T(8,128)S(1)}, f32[2,40,40,128]{3,2,1,0:T(8,128)}, u32[]{:S(2)}) copy-start(f32[2,40,40,128]{3,2,1,0:T(8,128)} %copy-done.4) | copy-start | bytes 4915204
  121.9 5.0 %collective-permute-start.4 = (f32[16,16,128]{2,1,0:T(8,128)S(1)}, f32[16,16,128]{2,1,0:T(8,128)S(1)}, u32[]{:S(2)}, u32[]{:S(2)}) collective-permute-start(f32[16,16,128]{2,1,0:T(8,128)S(1)} %get-tuple-element.51), channel_id=1, source_target_pairs={{0,32},{32,64},{64,96},{96,128},{128,160},{160,192},{192,224},{224... | collective-permute-start | bytes 393224 | tf_op jit(solution)/shard_map/ppermute | solution.py:594
  124.2 6.4 %collective-permute-start.5 = (f32[16,16,128]{2,1,0:T(8,128)S(1)}, f32[16,16,128]{2,1,0:T(8,128)S(1)}, u32[]{:S(2)}, u32[]{:S(2)}) collective-permute-start(f32[16,16,128]{2,1,0:T(8,128)S(1)} %get-tuple-element.51), channel_id=1, source_target_pairs={{32,0},{64,32},{96,64},{128,96},{160,128},{192,160},{224,192},{1,2... | collective-permute-start | bytes 393224 | tf_op jit(solution)/shard_map/ppermute | solution.py:595
  130.8 6.6 %collective-permute-start.6 = (f32[12,40,128]{2,1,0:T(8,128)S(1)}, f32[12,40,128]{2,1,0:T(8,128)S(1)}, u32[]{:S(2)}, u32[]{:S(2)}) collective-permute-start(f32[12,40,128]{2,1,0:T(8,128)S(1)} %get-tuple-element.99), channel_id=1, source_target_pairs={{0,4},{32,36},{64,68},{96,100},{128,132},{160,164},{192,196},{224,... | collective-permute-start | bytes 737288 | tf_op jit(solution)/shard_map/ppermute | solution.py:600
  134.3 7.5 %collective-permute-start.7 = (f32[12,40,128]{2,1,0:T(8,128)S(1)}, f32[12,40,128]{2,1,0:T(8,128)S(1)}, u32[]{:S(2)}, u32[]{:S(2)}) collective-permute-start(f32[12,40,128]{2,1,0:T(8,128)S(1)} %get-tuple-element.98), channel_id=1, source_target_pairs={{4,0},{36,32},{68,64},{100,96},{132,128},{164,160},{196,192},{228,... | collective-permute-start | bytes 737288 | tf_op jit(solution)/shard_map/ppermute | solution.py:601
  148.7 0.9 copy-start.21
  149.7 0.7 copy-start.23
  150.4 27.1 %copy-start.6 = (f32[2,40,40,128]{3,2,1,0:T(8,128)S(1)}, f32[2,40,40,128]{3,2,1,0:T(8,128)}, u32[]{:S(2)}) copy-start(f32[2,40,40,128]{3,2,1,0:T(8,128)} %copy-done.4) | copy-start | bytes 4915204
  150.4 27.1 %copy-start.12 = (f32[5,64,256]{2,1,0:T(8,128)S(1)}, f32[5,64,256]{2,1,0:T(8,128)}, u32[]{:S(2)}) copy-start(f32[5,64,256]{2,1,0:T(8,128)} %copy-done.11) | copy-start | bytes 983044
  177.5 2.2 copy-start.2
  179.6 1.1 copy-start.22
  180.8 1.0 copy-start.24
  181.8 0.9 copy-start.26
  182.7 31.0 %copy-start.3 = (f32[5,40,40,128]{3,2,1,0:T(8,128)S(1)}, f32[5,40,40,128]{3,2,1,0:T(8,128)}, u32[]{:S(2)}) copy-start(f32[5,40,40,128]{3,2,1,0:T(8,128)} %copy-done) | copy-start | bytes 12288004
  192.9 4.5 %collective-permute-start.8 = (f32[16,16,128]{2,1,0:T(8,128)S(1)}, f32[16,16,128]{2,1,0:T(8,128)S(1)}, u32[]{:S(2)}, u32[]{:S(2)}) collective-permute-start(f32[16,16,128]{2,1,0:T(8,128)S(1)} %get-tuple-element.59), channel_id=1, source_target_pairs={{0,32},{32,64},{64,96},{96,128},{128,160},{160,192},{192,224},{224... | collective-permute-start | bytes 393224 | tf_op jit(solution)/shard_map/ppermute | solution.py:594
  195.5 5.7 %collective-permute-start.9 = (f32[16,16,128]{2,1,0:T(8,128)S(1)}, f32[16,16,128]{2,1,0:T(8,128)S(1)}, u32[]{:S(2)}, u32[]{:S(2)}) collective-permute-start(f32[16,16,128]{2,1,0:T(8,128)S(1)} %get-tuple-element.59), channel_id=1, source_target_pairs={{32,0},{64,32},{96,64},{128,96},{160,128},{192,160},{224,192},{1,2... | collective-permute-start | bytes 393224 | tf_op jit(solution)/shard_map/ppermute | solution.py:595
  201.3 8.0 %collective-permute-start.10 = (f32[12,40,128]{2,1,0:T(8,128)S(1)}, f32[12,40,128]{2,1,0:T(8,128)S(1)}, u32[]{:S(2)}, u32[]{:S(2)}) collective-permute-start(f32[12,40,128]{2,1,0:T(8,128)S(1)} %get-tuple-element.97), channel_id=1, source_target_pairs={{0,4},{32,36},{64,68},{96,100},{128,132},{160,164},{192,196},{224,... | collective-permute-start | bytes 737288 | tf_op jit(solution)/shard_map/ppermute | solution.py:600
  206.2 7.5 %collective-permute-start.11 = (f32[12,40,128]{2,1,0:T(8,128)S(1)}, f32[12,40,128]{2,1,0:T(8,128)S(1)}, u32[]{:S(2)}, u32[]{:S(2)}) collective-permute-start(f32[12,40,128]{2,1,0:T(8,128)S(1)} %get-tuple-element.96), channel_id=1, source_target_pairs={{4,0},{36,32},{68,64},{100,96},{132,128},{164,160},{196,192},{228,... | collective-permute-start | bytes 737288 | tf_op jit(solution)/shard_map/ppermute | solution.py:601
  262.7 5.3 %collective-permute-start.12 = (f32[16,16,128]{2,1,0:T(8,128)S(1)}, f32[16,16,128]{2,1,0:T(8,128)S(1)}, u32[]{:S(2)}, u32[]{:S(2)}) collective-permute-start(f32[16,16,128]{2,1,0:T(8,128)S(1)} %get-tuple-element.68), channel_id=1, source_target_pairs={{0,32},{32,64},{64,96},{96,128},{128,160},{160,192},{192,224},{224... | collective-permute-start | bytes 393224 | tf_op jit(solution)/shard_map/ppermute | solution.py:594
  265.6 6.3 %collective-permute-start.13 = (f32[16,16,128]{2,1,0:T(8,128)S(1)}, f32[16,16,128]{2,1,0:T(8,128)S(1)}, u32[]{:S(2)}, u32[]{:S(2)}) collective-permute-start(f32[16,16,128]{2,1,0:T(8,128)S(1)} %get-tuple-element.68), channel_id=1, source_target_pairs={{32,0},{64,32},{96,64},{128,96},{160,128},{192,160},{224,192},{1,2... | collective-permute-start | bytes 393224 | tf_op jit(solution)/shard_map/ppermute | solution.py:595
  271.9 7.4 %collective-permute-start.14 = (f32[12,40,128]{2,1,0:T(8,128)S(1)}, f32[12,40,128]{2,1,0:T(8,128)S(1)}, u32[]{:S(2)}, u32[]{:S(2)}) collective-permute-start(f32[12,40,128]{2,1,0:T(8,128)S(1)} %get-tuple-element.95), channel_id=1, source_target_pairs={{0,4},{32,36},{64,68},{96,100},{128,132},{160,164},{192,196},{224,... | collective-permute-start | bytes 737288 | tf_op jit(solution)/shard_map/ppermute | solution.py:600
  276.2 7.5 %collective-permute-start.15 = (f32[12,40,128]{2,1,0:T(8,128)S(1)}, f32[12,40,128]{2,1,0:T(8,128)S(1)}, u32[]{:S(2)}, u32[]{:S(2)}) collective-permute-start(f32[12,40,128]{2,1,0:T(8,128)S(1)} %get-tuple-element.94), channel_id=1, source_target_pairs={{4,0},{36,32},{68,64},{100,96},{132,128},{164,160},{196,192},{228,... | collective-permute-start | bytes 737288 | tf_op jit(solution)/shard_map/ppermute | solution.py:601
  333.2 22.0 %copy-start.7 = (f32[2,40,40,128]{3,2,1,0:T(8,128)}, f32[2,40,40,128]{3,2,1,0:T(8,128)S(1)}, u32[]{:S(2)}) copy-start(f32[2,40,40,128]{3,2,1,0:T(8,128)S(1)} %get-tuple-element.78.rq) | copy-start | bytes 4915204
  333.2 22.0 %copy-start.9 = (f32[2,18,40,128]{3,2,1,0:T(8,128)}, f32[2,18,40,128]{3,2,1,0:T(8,128)S(1)}, u32[]{:S(2)}) copy-start(f32[2,18,40,128]{3,2,1,0:T(8,128)S(1)} %get-tuple-element.83.pd) | copy-start | bytes 2211844
  333.2 5.3 %collective-permute-start.16 = (f32[16,16,128]{2,1,0:T(8,128)S(1)}, f32[16,16,128]{2,1,0:T(8,128)S(1)}, u32[]{:S(2)}, u32[]{:S(2)}) collective-permute-start(f32[16,16,128]{2,1,0:T(8,128)S(1)} %get-tuple-element.77), channel_id=1, source_target_pairs={{0,32},{32,64},{64,96},{96,128},{128,160},{160,192},{192,224},{224... | collective-permute-start | bytes 393224 | tf_op jit(solution)/shard_map/ppermute | solution.py:594
  336.1 6.3 %collective-permute-start.17 = (f32[16,16,128]{2,1,0:T(8,128)S(1)}, f32[16,16,128]{2,1,0:T(8,128)S(1)}, u32[]{:S(2)}, u32[]{:S(2)}) collective-permute-start(f32[16,16,128]{2,1,0:T(8,128)S(1)} %get-tuple-element.77), channel_id=1, source_target_pairs={{32,0},{64,32},{96,64},{128,96},{160,128},{192,160},{224,192},{1,2... | collective-permute-start | bytes 393224 | tf_op jit(solution)/shard_map/ppermute | solution.py:595
  342.4 7.4 %collective-permute-start.18 = (f32[12,40,128]{2,1,0:T(8,128)S(1)}, f32[12,40,128]{2,1,0:T(8,128)S(1)}, u32[]{:S(2)}, u32[]{:S(2)}) collective-permute-start(f32[12,40,128]{2,1,0:T(8,128)S(1)} %get-tuple-element.93), channel_id=1, source_target_pairs={{0,4},{32,36},{64,68},{96,100},{128,132},{160,164},{192,196},{224,... | collective-permute-start | bytes 737288 | tf_op jit(solution)/shard_map/ppermute | solution.py:600
  346.7 7.5 %collective-permute-start.19 = (f32[12,40,128]{2,1,0:T(8,128)S(1)}, f32[12,40,128]{2,1,0:T(8,128)S(1)}, u32[]{:S(2)}, u32[]{:S(2)}) collective-permute-start(f32[12,40,128]{2,1,0:T(8,128)S(1)} %get-tuple-element.92), channel_id=1, source_target_pairs={{4,0},{36,32},{68,64},{100,96},{132,128},{164,160},{196,192},{228,... | collective-permute-start | bytes 737288 | tf_op jit(solution)/shard_map/ppermute | solution.py:601
  354.2 11.2 %copy-start.29 = (s32[4]{0:T(128)S(1)}, s32[4]{0:T(128)}, u32[]{:S(2)}) copy-start(s32[4]{0:T(128)} %param.7) | copy-start | bytes 52
  354.2 24.0 %copy-start.16 = (f32[3,18,40,128]{3,2,1,0:T(8,128)S(1)}, f32[3,18,40,128]{3,2,1,0:T(8,128)}, u32[]{:S(2)}) copy-start(f32[3,18,40,128]{3,2,1,0:T(8,128)} %copy-done.15) | copy-start | bytes 3317764
  355.2 0.9 copy-start.17
  356.8 21.4 %all-to-all-start.6 = ((f32[256,1,128]{2,1,0:T(1,128)}), f32[256,1,128]{2,1,0:T(1,128)S(1)}, u32[]{:S(2)}, u32[]{:S(2)}) async-start(f32[256,1,128]{2,1,0:T(1,128)} %broadcast_in_dim.30), calls=%async_computation.6 | async-start | bytes 262144 | tf_op jit(solution)/shard_map/all_to_all | solution.py:607
  378.2 1.4 copy-start.8
  379.6 1.1 copy-start.10
  380.8 1.1 copy-start.18
  387.3 11.3 %all-to-all-start.7 = ((f32[8,8,512]{2,1,0:T(8,128)}), f32[8,8,512]{2,1,0:T(8,128)S(1)}, u32[]{:S(2)}, u32[]{:S(2)}) async-start(f32[8,8,512]{2,1,0:T(8,128)} %bitcast.14), calls=%async_computation.7 | async-start | bytes 262144 | tf_op jit(solution)/shard_map/all_to_all | solution.py:665
  399.4 22.4 %all-to-all-start.8 = ((f32[256,1,256]{2,1,0:T(1,128)}), f32[256,1,256]{2,1,0:T(1,128)S(1)}, u32[]{:S(2)}, u32[]{:S(2)}) async-start(f32[256,1,256]{2,1,0:T(1,128)} %broadcast_in_dim.31), calls=%async_computation.8 | async-start | bytes 524288 | tf_op jit(solution)/shard_map/all_to_all | solution.py:607

commit v2 on v1

--- a/solution.py
+++ b/solution.py
@@ -21,6 +21,7 @@
 NB = 40
 F32 = jnp.float32
 INTERPRET = False
+H = 20
 LIMIT = 26 * 1024 * 1024
 
 THETA = 1.15
@@ -55,6 +56,10 @@
     return roll(v, s, 1)
 
 
+def swap(v):
+    return roll(v, NX, 1)
+
+
 def ziota():
     return lax.broadcasted_iota(jnp.int32, (NB, 128), 0)
 
@@ -119,7 +124,7 @@
     return carry
 
 
-def sweep(level, lo, hi, field, store):
+def sweep(level, lo, n, field, store):
     first = field(lo)
     flux = level.y_flux(lo - 1, field(lo - 1), first)
 
@@ -129,10 +134,13 @@
         image, flux_y = level.apply(y, u, high, flux_low)
         return (high, flux_y), store(y, u, image)
 
-    rows(lo, hi, row, (first, flux))
-
-
-def smooth_down(level, lo, hi, r, r1, u1, x, r2):
+    u, flux_low = rows(lo, n - 1, row, (first, flux))
+    image, _ = level.apply(n - 1, u, swap(u), flux_low)
+    for ref, at, value in store(n - 1, u, image):
+        ref[at] = value
+
+
+def smooth_down(level, lo, n, r, r1, u1, x, r2):
     def start(y):
         return level.dinv[y] * r[y] * (1.0 / THETA)
 
@@ -141,42 +149,43 @@
         after = C1U * u + C1R * (level.dinv[y] * rest)
         return [(r1, y, rest), (u1, y, after), (x, y, u + after)]
 
-    sweep(level, lo, hi, start, first)
-    sweep(level, lo + 1, hi - 1, lambda y: u1[y], lambda y, u, image: [(r2, y, r1[y] - image)])
-
-
-def smooth_up(level, lo, hi, e, r2, r3, u, x, finish):
+    sweep(level, lo, n, start, first)
+    sweep(level, lo + 1, n, lambda y: u1[y], lambda y, u, image: [(r2, y, r1[y] - image)])
+
+
+def smooth_up(level, lo, n, e, r2, r3, u, x, finish):
     def first(y, own, image):
         rest = r2[y] - image
         return [(r3, y, rest), (u, y, level.dinv[y] * rest * (1.0 / THETA))]
 
-    sweep(level, lo, hi, e, first)
+    sweep(level, lo, n, e, first)
 
     def second(y, own, image):
         rest = r3[y] - image
         after = C1U * own + C1R * (level.dinv[y] * rest)
         return finish(y, (x[y] + e(y)) + (own + after))
 
-    sweep(level, lo + 1, hi - 1, lambda y: u[y], second)
+    sweep(level, lo + 1, n, lambda y: u[y], second)
 
 
 def down(fine, mid, r, x, r2, xm, r2m, r1, u1, b1, r1m, u1m):
-    smooth_down(fine, 3, 37, r, r1, u1, x, r2)
-    rows(2, 18, lambda y, c: (c, [(b1, y, sum_x(sum_z(r2[2 * y] + r2[2 * y + 1], 1), 1))]), 0)
-    smooth_down(mid, 3, 17, b1, r1m, u1m, xm, r2m)
-    return to_line([sum_x(sum_z(r2m[2 * k + 6] + r2m[2 * k + 7], 2), 2) for k in range(4)])
-
-
-def to_line(rows):
-    spread = lax.broadcasted_iota(jnp.int32, (128, 256), 1) % 16 * 4 == lax.broadcasted_iota(jnp.int32, (128, 256), 0)
+    smooth_down(fine, 3, H, r, r1, u1, x, r2)
+    rows(2, H // 2, lambda y, c: (c, [(b1, y, sum_x(sum_z(r2[2 * y] + r2[2 * y + 1], 1), 1))]), 0)
+    smooth_down(mid, 3, H // 2, b1, r1m, u1m, xm, r2m)
+    return to_line([sum_x(sum_z(r2m[2 * k + 6] + r2m[2 * k + 7], 2), 2) for k in range(2)])
+
+
+def to_line(folded):
+    to = lax.broadcasted_iota(jnp.int32, (128, 256), 1)
+    spread = to % 16 * 4 + to // 128 * NX == lax.broadcasted_iota(jnp.int32, (128, 256), 0)
     spread = jnp.where(spread, 1.0, 0.0)
     at = lax.broadcasted_iota(jnp.int32, (NB, 256), 1) // 16
-    z = lax.broadcasted_iota(jnp.int32, (NB, 256), 0)
+    y = at // 4
+    z = lax.broadcasted_iota(jnp.int32, (NB, 256), 0) == M + 4 * (at % 4)
     line = jnp.zeros((1, 256), F32)
-    for y in range(4):
-        wide = jnp.dot(rows[y], spread, precision=lax.Precision.HIGHEST, preferred_element_type=F32)
-        mine = (at // 4 == y) & (z == M + 4 * (at % 4))
-        line = line + jnp.sum(jnp.where(mine, wide, 0.0), axis=0, keepdims=True)
+    for k in range(2):
+        wide = jnp.dot(folded[k], spread, precision=lax.Precision.HIGHEST, preferred_element_type=F32)
+        line = line + jnp.sum(jnp.where(((y == k) | (y == 3 - k)) & z, wide, 0.0), axis=0, keepdims=True)
     return line
 
 
@@ -194,43 +203,48 @@
     wx, wy, wz, c, dinv = fine.wx, fine.wy, fine.wz, fine.c, fine.dinv
     wx1, wy1, wz1, c1, dinv1 = mid.wx, mid.wy, mid.wz, mid.c, mid.dinv
     for k in range(3):
-        kept[k] = fields[k, M - 1 : M + B + 1]
+        kept[k] = fields[k, M - 1 : H]
     gy, zb = pos[0], pos[1]
     zg = ziota() + (zb * B - M)
     lane = xiota()
-    inside_zx = (zg >= 0) & (zg < NZ) & (lane < NX)
+    xg = lane % NX
+    inside_z = (zg >= 0) & (zg < NZ)
+    at_edge = ((lane < NX) & (gy == 0)) | ((lane >= NX) & (gy == NGY - 1))
 
     def weight(g):
         square = g * g
         root = jnp.sqrt(1.0 + square)
         return (1.0 + 2.0 * square) / root, g * root
 
-    def row(y, carry):
-        flow_low, wy_low, wym_low = carry
-        yg = gy * B - M + y
-        here, high = it[y], it[y + 1]
-        w_x, p_x = weight(up_x(here) - here)
+    def row(y, carry, high=None):
+        here, flow_low, wy_low, wym_low = carry
+        high = it[y + 1] if high is None else high
+        w_x, p_x = weight(jnp.where(xg == NX - 1, 0.0, up_x(here)) - here)
+        w_0, p_0 = weight(here)
         w_y, p_y = weight(high - here)
         w_z, p_z = weight(up_z(here) - here)
-        inside = inside_zx & (yg >= 0) & (yg < NY)
-        rest = src[y] - rea[y] * here + ((p_x - dn_x(p_x)) + (p_y - flow_low) + (p_z - dn_z(p_z)))
-        outer = rea[y] + jnp.where(lane == 0, dn_x(w_x), 0.0) + jnp.where(lane == NX - 1, w_x, 0.0)
+        inside = inside_z & jnp.logical_not(at_edge & (y < M))
+        low_x = jnp.where(xg == 0, p_0, dn_x(p_x))
+        rest = src[y] - rea[y] * here + ((p_x - low_x) + (p_y - flow_low) + (p_z - dn_z(p_z)))
+        outer = rea[y] + jnp.where(xg == 0, w_0, 0.0) + jnp.where(xg == NX - 1, w_x, 0.0)
         outer = outer + jnp.where(zg == 0, dn_z(w_z), 0.0) + jnp.where(zg == NZ - 1, w_z, 0.0)
-        outer = outer + jnp.where(yg == 0, wy_low, 0.0) + jnp.where(yg == NY - 1, w_y, 0.0)
+        outer = outer + jnp.where(at_edge & (y == M), wy_low, 0.0)
         outer = jnp.where(inside, outer, 0.0)
-        m_x = jnp.where(inside & (lane < NX - 1), w_x, 0.0)
-        m_y = jnp.where(inside & (yg < NY - 1), w_y, 0.0)
+        m_x = jnp.where(inside & (xg < NX - 1), w_x, 0.0)
+        m_y = jnp.where(inside, w_y, 0.0)
         m_z = jnp.where(inside & (zg < NZ - 1), w_z, 0.0)
         diagonal = outer + m_x + dn_x(m_x) + m_y + wym_low + m_z + dn_z(m_z)
         good = diagonal > 0.0
         inverse = jnp.where(good, 1.0 / jnp.where(good, diagonal, 1.0), 0.0)
         stores = [(r, y, jnp.where(inside, rest, 0.0)), (wx, y, m_x), (wy, y, m_y), (wz, y, m_z), (c, y, outer)]
-        return (p_y, w_y, m_y), stores + [(dinv, y, inverse)]
+        return (high, p_y, w_y, m_y), stores + [(dinv, y, inverse)]
 
     zero = jnp.zeros((NB, 128), F32)
-    rows(0, NB - 1, row, (zero, zero, zero), 2)
+    carry = rows(1, H - 1, row, (it[1], zero, zero, zero), 2)
+    for ref, at, value in row(H - 1, carry, swap(carry[0]))[1]:
+        ref[at] = value
     for ref in (wx, wy, wz, c, dinv, r):
-        ref[NB - 1] = zero
+        ref[0] = zero
 
     def row1(y, low):
         a, b = 2 * y, 2 * y + 1
@@ -243,12 +257,13 @@
         inverse = jnp.where(good, 1.0 / jnp.where(good, diagonal, 1.0), 0.0)
         return m_y, [(wx1, y, m_x), (wy1, y, m_y), (wz1, y, m_z), (c1, y, m_c), (dinv1, y, inverse)]
 
-    rows(0, NB // 2, row1, zero, 2)
+    rows(0, H // 2, row1, zero, 2)
 
     pay[:, 0:256] = down(fine, mid, r, *cycle_of(cycle, cycle1), *scratch)
-    pair = [(2 * k + 6, 2 * k + 7) for k in range(4)]
+    pair = [(2 * k + 6, 2 * k + 7) for k in range(2)]
     pay[:, 256:512] = to_line([sum_z(odd_x(wx1[a] + wx1[b], 2), 2) for a, b in pair])
-    pay[:, 512:768] = to_line([sum_x(sum_z(wy1[b], 2), 2) for a, b in pair])
+    half = lane < NX
+    pay[:, 512:768] = to_line([sum_x(sum_z(jnp.where(half, wy1[b], wy1[b - 2]), 2), 2) for a, b in pair])
     pay[:, 768:1024] = to_line([sum_x(odd_z(wz1[a] + wz1[b], 2), 2) for a, b in pair])
     pay[:, 1024:1280] = to_line([sum_x(sum_z(c1[a] + c1[b], 2), 2) for a, b in pair])
 
@@ -399,27 +414,31 @@
             at_y = jnp.clip(gy + dy, 0, NGY - 1)
             at_z = jnp.clip(zb + dz, 0, NZB - 1)
             picked[dy, dz] = lanes == ((at_z % NGX) * NGY + at_y) * NGZ + at_z // NGX
-    spread = lax.broadcasted_iota(jnp.int32, (16, 128), 1) // 4 == lax.broadcasted_iota(jnp.int32, (16, 128), 0)
-    rows = ziota() // 4
-    for y2 in range(1, 9):
-        dy, y = (y2 - 3) // 4, (y2 - 3) % 4
+    lane = lax.broadcasted_iota(jnp.int32, (16, 128), 1)
+    spread = lane % NX // 4 == lax.broadcasted_iota(jnp.int32, (16, 128), 0)
+    rows_z = ziota() // 4
+
+    def column(y2, z2):
+        mine = picked[(y2 - 3) // 4, (z2 - 3) // 4]
+        return jnp.sum(jnp.where(mine, x2[(y2 - 3) % 4][(z2 - 3) % 4], 0.0), axis=1, keepdims=True)
+
+    for k in range(1, 5):
         plane = jnp.zeros((NB, 128), F32)
         for z2 in range(1, 9):
-            dz, z = (z2 - 3) // 4, (z2 - 3) % 4
-            column = jnp.sum(jnp.where(picked[dy, dz], x2[y][z], 0.0), axis=1, keepdims=True)
-            line = jnp.sum(jnp.where(spread, column, 0.0), axis=0, keepdims=True)
-            plane = jnp.where(rows == z2, line, plane)
-        e2[y2] = plane
+            both = jnp.where(lane < NX, column(k, z2), column(9 - k, z2))
+            line = jnp.sum(jnp.where(spread, both, 0.0), axis=0, keepdims=True)
+            plane = jnp.where(rows_z == z2, line, plane)
+        e2[k] = plane
 
 
 def up(pos, k2, k3, b2t, fine, mid, x, r2, xm, r2m, out, e2, r3, u, x1, r3m, um):
     place_coarse(pos, coarse_solve(k2, k3, b2t), e2)
-    smooth_up(mid, 4, 16, lambda y: e2[y // 2], r2m, r3m, um, xm, lambda y, value: [(x1, y, value)])
+    smooth_up(mid, 4, H // 2, lambda y: e2[y // 2], r2m, r3m, um, xm, lambda y, value: [(x1, y, value)])
 
     def result(y, value):
         return [(out, y - M, dn_z(value, -M)[:B])]
 
-    smooth_up(fine, 11, 29, lambda y: x1[y // 2], r2, r3, u, x, result)
+    smooth_up(fine, M - 1, H, lambda y: x1[y // 2], r2, r3, u, x, result)
 
 
 def first_kernel(pos, got, coef, coef1, cycle, cycle1, out, k2, k3, b2t, *scratch):
@@ -429,14 +448,24 @@
     up(pos, k2, k3, b2t, fine, mid, *cycle_of(cycle, cycle1), out, *scratch)
 
 
-def image_kernel(last, centre, low, high, rq, coef, coef1, z_kept, w, pay, z, *scratch):
+def image_kernel(last, centre, *refs):
+    if last:
+        before, after, edge, rq, coef, coef1, z_kept, w, pay, z, *scratch = refs
+        z[M - 1] = edge[0]
+        blank = jnp.zeros((8, 128), F32)
+        for k in range(8):
+            z[M + k] = roll(jnp.concatenate([before[k], centre[k], after[k], blank], axis=0), 4, 0)
+    else:
+        low, high, rq, coef, coef1, z_kept, w, pay, z, *scratch = refs
+        half = xiota() < NX
+        z[M:H] = centre[...]
+        for k in range(4):
+            z[k] = jnp.where(half, low[k + 4], high[k + 4])
+        for k in range(4, M):
+            z[k] = swap(jnp.where(half, high[11 - k], low[11 - k]))
     fine, mid = levels_of(coef, coef1)
-    z[0:M] = low[...]
-    z[M : M + B] = centre[...]
-    z[M + B : NB] = high[...]
-    z_kept[...] = z[M - 1 : M + B + 1]
-    lo, hi = (M, M + B) if last else (2, 38)
-    sweep(fine, lo, hi, lambda y: z[y], lambda y, u, image: [(w, y, image)])
+    z_kept[...] = z[M - 1 : H]
+    sweep(fine, M if last else 2, H, lambda y: z[y], lambda y, u, image: [(w, y, image)])
     own = (ziota() >= M) & (ziota() < M + B)
 
     def row(y, carry):
@@ -445,7 +474,7 @@
         return (a + rq[0, y] * here, b + here * w[y]), []
 
     zero = jnp.zeros((NB, 128), F32)
-    a, b = rows(M, M + B, row, (zero, zero))
+    a, b = rows(M, H, row, (zero, zero))
     lane = lax.broadcasted_iota(jnp.int32, (1, 128), 1)
     pay[:, 0:128] = jnp.where(lane == 0, jnp.sum(a), jnp.where(lane == 1, jnp.sum(b), 0.0))
     if not last:
@@ -485,13 +514,13 @@
         q = w[y] if first else w[y] + beta * rq[1, y]
         return carry, [(rq_o, (1, y), q), (rq_o, (0, y), rq[0, y] - alpha * q)]
 
-    rows(2, 38, row, 0)
+    rows(2, H, row, 0)
 
     def row_d(y, carry):
         p = z[y] if first else z[y] + beta * pd[0, y]
         return carry, [(pd_o, (0, y), p), (pd_o, (1, y), alpha * p if first else pd[1, y] + alpha * p)]
 
-    rows(0, B + 2, row_d, 0)
+    rows(0, 9, row_d, 0)
     x, r2, xm, r2m = cycle_of(cycle, cycle1)
     pay[...] = down(fine, mid, rq_o.at[0], x, r2, xm, r2m, *scratch)
     alpha2 = jnp.concatenate([alpha, alpha], axis=1)
@@ -508,17 +537,19 @@
 def finish_kernel(pos, steps, got, old, z, w, rq, pd, kept, d_out, r_out, layers, d_all):
     alpha, beta = step_sizes(got, old, None, False)
     gy, zb = pos[0], pos[1]
-    rows(0, B + 2, lambda y, c: (c, [(d_all, y, pd[1, y] + alpha * (z[y] + beta * pd[0, y]))]), 0)
+    rows(0, 9, lambda y, c: (c, [(d_all, y, pd[1, y] + alpha * (z[y] + beta * pd[0, y]))]), 0)
 
     def row(y, carry):
         r = rq[0, y + M] - alpha * (w[y + M] + beta * rq[1, y + M])
         return carry, [(r_out, y, dn_z(r, -M)[:B]), (d_out, y, dn_z(d_all[y + 1], -M)[:B])]
 
-    rows(0, B, row, 0)
+    rows(0, 8, row, 0)
     zi = ziota()
     own = (zi >= M) & (zi < M + B)
     own_z = own | ((zi == M + B) & (zb == NZB - 1))
-    lane = lax.broadcasted_iota(jnp.int32, (1, 128), 1)
+    lane = xiota()
+    x = lane % NX
+    edge = own & ((lane < NX) | (gy == NGY - 1))
 
     def energy(g):
         square = 1.0 + g * g
@@ -531,20 +562,20 @@
         def trial(y):
             return kept[0, y] + step * d_all[y]
 
+        def part(y, low, acc, outer):
+            v = trial(y)
+            acc = acc + jnp.where(outer, energy(v - low), 0.0) + jnp.where(own_z, energy(v - dn_z(v)), 0.0)
+            inner = energy(v - jnp.where(x == 0, 0.0, dn_x(v))) + jnp.where(x == NX - 1, energy(v), 0.0)
+            inner = inner + (0.5 * kept[2, y] * v * v - kept[1, y] * v)
+            return v, acc + jnp.where(own, inner, 0.0)
+
         def row(y, carry):
-            low, acc_x, acc = carry
-            v = trial(y)
-            acc_x = acc_x + jnp.where(own, energy(v - dn_x(v)), 0.0)
-            part = energy(v - low) + (0.5 * kept[2, y] * v * v - kept[1, y] * v)
-            acc = acc + jnp.where(own, part, 0.0) + jnp.where(own_z, energy(v - dn_z(v)), 0.0)
-            return (v, acc_x, acc), []
-
-        v, acc_x, acc = rows(1, B + 1, row, (trial(0), zero, zero), 2)
-        last = own & (gy == NGY - 1)
-        acc = acc + jnp.where(last, energy(trial(B + 1) - v), 0.0)
-        sum_of_x = jnp.sum(acc_x, axis=0, keepdims=True)
-        top = jnp.where(lane == NX - 1, jnp.broadcast_to(roll(jnp.broadcast_to(sum_of_x, (8, 128)), -1, 1)[0:1], (1, 128)), 0.0)
-        layers[k] = jnp.broadcast_to(sum_of_x + top + jnp.sum(acc, axis=0, keepdims=True), (8, 128))
+            return part(y, *carry, own), []
+
+        v, acc = rows(2, 9, row, part(1, trial(0), zero, edge), 2)
+        acc = acc + jnp.where(own & (lane < NX), energy(swap(v) - v), 0.0)
+        total = jnp.broadcast_to(jnp.sum(acc, axis=0, keepdims=True), (8, 128))
+        layers[k] = total + swap(total)
 
 
 VM = pl.BlockSpec(memory_space=pltpu.VMEM)
@@ -568,13 +599,13 @@
     return run
 
 
-FINE = (NB, NB, 128)
-MID = (NB // 2, NB, 128)
-KEPT = (B + 2, NB, 128)
+FINE = (H, NB, 128)
+MID = (H // 2, NB, 128)
+KEPT = (9, NB, 128)
 SCRATCH = [FINE, FINE, MID, MID, MID]
 CYCLE = [(2, *FINE), (2, *MID)]
 COEFS = [(5, *FINE), (5, *MID)]
-COARSE = (NB // 4, NB, 128)
+COARSE = (H // 4, NB, 128)
 PLANES = (256, NDEV)
 
 
@@ -597,9 +628,21 @@
 
 
 def exchange_y(own):
-    low = lax.ppermute(own[..., B - M :, :, :], ALL, shift_pairs(1, 0))
-    high = lax.ppermute(own[..., :M, :, :], ALL, shift_pairs(-1, 0))
-    return low, high
+    return lax.ppermute(own, ALL, shift_pairs(1, 0)), lax.ppermute(own, ALL, shift_pairs(-1, 0))
+
+
+def exchange_faces(own):
+    low = lax.ppermute(own[:, 8:], ALL, shift_pairs(0, 1))
+    high = lax.ppermute(own[:, :8], ALL, shift_pairs(0, -1))
+    below, above = exchange_y(own[:1])
+    edge = jnp.concatenate([below[..., NX:], above[..., :NX]], axis=-1)
+    return own, low, high, jnp.pad(edge, ((0, 0), (M, M), (0, 0)))
+
+
+def unfold_margin(own, low, high):
+    outer = jnp.concatenate([low[..., 4:, :, :NX], high[..., 4:, :, NX:]], axis=-1)
+    inner = jnp.concatenate([low[..., ::-1, :, NX:], high[..., ::-1, :, :NX]], axis=-1)
+    return jnp.concatenate([outer, inner, own], axis=-3)
 
 
 def to_everyone(x):
@@ -621,18 +664,18 @@
     gy = lax.axis_index(GY)
     zb = lax.axis_index("gz") * NGX + gx
     pos = jnp.stack([gy, zb]).astype(jnp.int32)
-    steps = jnp.exp2(-trial_powers.astype(F32))
+    pos, steps = lax.optimization_barrier((pos, jnp.exp2(-trial_powers.astype(F32))))
     fields = jnp.stack([iterate, source, reaction])
     fields = fields.reshape(3, 8, 16, 8, 16).transpose(3, 1, 0, 2, 4).reshape(8, 8, 3, 256)
     fields = lax.all_to_all(fields, "gx", split_axis=0, concat_axis=0, tiled=True)
     fields = fields.reshape(NX, 3 * 256).T.reshape(3, 16, 16, NX)
-    fields = exchange_z(jnp.pad(fields, ((0, 0), (0, 0), (0, 0), (0, 128 - NX))))
-    low, high = exchange_y(fields)
-    fields = jnp.concatenate([low, fields, high], axis=1)
+    fields = jnp.concatenate([fields[:, :8], fields[:, :7:-1]], axis=-1)
+    fields = exchange_z(fields)
+    fields = unfold_margin(fields, *exchange_y(fields))
     coef, coef1, rq, cycle, cycle1, kept, pay = call(
         setup_kernel, 1, COEFS + [(2, *FINE)] + CYCLE + [(3, *KEPT), (1, 1280)], SCRATCH, "setup"
     )(pos, fields)
-    own = (B, B, 128)
+    own = (8, B, 128)
     z, k2, k3, b2 = call(
         first_kernel, 1, [own, (5, 256, NDEV), (5, 64, NDEV), PLANES], [COARSE] + SCRATCH, "first"
     )(pos, to_everyone_by_axes(pay), coef, coef1, cycle, cycle1)
@@ -640,12 +683,15 @@
     pd = None
     for i in range(ITERS):
         first, last = i == 0, i + 1 == ITERS
-        centre = exchange_z(z)
-        low, high = exchange_y(centre)
+        if last:
+            around = exchange_faces(z)
+        else:
+            centre = exchange_z(z)
+            around = (centre, *exchange_y(centre))
         z, w, line = call(
             functools.partial(image_kernel, last), 0, [KEPT, FINE, (1, 128 if last else 384)],
             [FINE] + ([] if last else CYCLE + SCRATCH), "image",
-        )(centre, low, high, rq, coef, coef1)
+        )(*around, rq, coef, coef1)
         if last:
             break
         if not first:
@@ -661,10 +707,14 @@
     d_own, r_own, layers = call(finish_kernel, 2, [own, own, (TRIALS, 8, 128)], [KEPT], "finish")(
         pos, steps, dots, scal, z, w, rq, pd, kept
     )
-    both = jnp.stack([d_own, r_own])[..., :NX].reshape(512, NX).T
-    both = lax.all_to_all(both.reshape(8, 8, 512), "gx", split_axis=0, concat_axis=0, tiled=True)
+    both = jnp.stack([d_own, r_own])
+    both = jnp.concatenate([both[..., :NX], both[:, ::-1, :, NX:]], axis=1).reshape(512, NX).T
+    copies = jnp.broadcast_to(layers[:, 0, :NX].reshape(1, 256), (NDEV, 1, 256))
+    copies, both = lax.optimization_barrier((copies, both.reshape(8, 8, 512)))
+    layers = lax.all_to_all(copies, ALL, split_axis=0, concat_axis=0, tiled=True)
+    both = lax.all_to_all(both, "gx", split_axis=0, concat_axis=0, tiled=True)
     both = both.reshape(8, 8, 2, 16, 16).transpose(2, 1, 3, 0, 4).reshape(2, 8, 16, 128)
-    layers = to_everyone(layers[:, 0, :NX].reshape(1, 256)).sum(axis=0).reshape(TRIALS, NX) / (NY * NZ)
+    layers = layers.sum(axis=0).reshape(TRIALS, NX) / (NY * NZ)
     energies = jnp.sum(layers, axis=1) / NX
     mine = lax.dynamic_slice_in_dim(layers, gx * 8, 8, axis=1)
     return both[0], both[1], mine, energies

time: 425 us -> 357 us (0.84)
  waiting for transfers between devices: 93.7 us -> 42 us
  blocking collectives: 148 us -> 191 us
  Pallas kernels: 76 us -> 42.4 us
  local copies, waits for them, and re-layouts: 31.1 us -> 16.6 us
  starting transfers between devices: 71.7 us -> 59.9 us
    pallas_call x10, Pallas kernels: 76 us -> 42.4 us  [run(): pl.pallas_call(kernel, in_specs=[SM] * n_scalar + [VM] * (len(args) - n_s...]
    all_to_all x3 -> x4, blocking collectives: 89.1 us -> 120 us  [to_everyone(): return lax.all_to_all(copies, ALL, split_axis=0, concat_axis=0, tiled=True)]
    all_to_all x3 -> x1, waiting for transfers between devices: 33.2 us -> 12.6 us  [on_device(): lax.all_to_all(copies, ALL, split_axis=0, concat_axis=0, tiled=True)]
    ppermute x10 -> x12, waiting for transfers between devices: 32.9 us -> 13.2 us  [the longest x5 7.66 us: exchange_y(): lax.ppermute(own, ALL, shift_pairs(-1, 0))]
    unnamed x64 -> x44, local copies, waits for them, and re-layouts: 20 us -> 7.51 us
    all_to_all x3 -> x1, starting transfers between devices: 19 us -> 7.31 us  [on_device(): lax.all_to_all(copies, ALL, split_axis=0, concat_axis=0, tiled=True)]
    all_to_all x0 -> x1, blocking collectives: none -> 10.1 us  [on_device(): both = lax.all_to_all(both, 'gx', split_axis=0, concat_axis=0, tiled=True)]
    ppermute x5 -> x4, waiting for transfers between devices: 8.55 us -> 1.32 us  [exchange_z(): low = lax.ppermute(own, ALL, shift_pairs(0, 1))]
  transfers between devices with their start and end apart: 23 -> 21, of which waited for: 23 -> 15; matrix products, arithmetic and copies ran while one was open for 1% -> 1% of each run, Pallas kernels for 0% -> 0%
where the time goes in v2:
time: 357 us; the launch traced here: 355 us
  blocking collectives  191 us (54%)
  starting transfers between devices  59.9 us (17%)
  Pallas kernels  42.4 us (12%)
  waiting for transfers between devices  42 us (12%)
  local copies, waits for them, and re-layouts  16.6 us (5%)
    all_to_all x4, blocking collectives, to_everyone(): return lax.all_to_all(copies, ALL, split_axis=0, concat_axis=0, tiled=True)  120 us
    pallas_call x10, Pallas kernels, run(): pl.pallas_call(kernel, in_specs=[SM] * n_scalar + [VM] * (len(args) - n_s...  42.4 us
    all_to_all x1, blocking collectives, to_everyone_by_axes(): lax.all_to_all(copies, (*GY, 'gz'), split_axis=0, concat_axis=0, tiled=True)  29.4 us
    ppermute x5, starting transfers between devices, exchange_y(): lax.ppermute(own, ALL, shift_pairs(-1, 0))  19.5 us
    all_to_all x1, blocking collectives, on_device(): lax.all_to_all(fields, 'gx', split_axis=0, concat_axis=0, tiled=True)  17.8 us
    ppermute x4, waiting for transfers between devices, exchange_z(): high = lax.ppermute(own, ALL, shift_pairs(0, -1))  14.9 us
    all_to_all x1, blocking collectives, to_everyone_by_axes(): got = lax.all_to_all(copies, 'gx', split_axis=0, concat_axis=0, tiled=True)  13.5 us
    ppermute x5, starting transfers between devices, exchange_y(): lax.ppermute(own, ALL, shift_pairs(1, 0))  13.2 us
  transfers between devices with their start and end apart: 21, of which 15 were waited for; matrix products, arithmetic and copies ran while one was open for 1% of the time, Pallas kernels for 0%

profile of v2, /device:TPU:1, one launch (start us, length us, event | category | flops | bytes accessed | tf_op | source)
XLA Modules:
  0.0 355.5 jit_solution(530520325448638218)
XLA Ops:
  0.6 1.1 stack.33
  3.7 17.8 %all_to_all.45 = f32[8,8,3,256]{3,1,2,0:T(8,128)S(1)} all-to-all(f32[8,8,3,256]{3,1,2,0:T(8,128)S(1)} %reshape.56), channel_id=1, replica_groups=mesh['gx'=8,'gy_0'=4,'gy_1'=2,'gz'=4] {'gx'}, dimensions={0} | all-to-all | bytes 393216 | tf_op jit(solution)/shard_map/all_to_all | solution.py:670
  21.8 1.9 collective-permute-start
  23.7 1.3 collective-permute-start.1
  25.0 1.3 collective-permute-done
  26.3 3.8 %collective-permute-done.1 = f32[3,8,16,128]{3,2,1,0:T(8,128)S(1)} collective-permute-done((f32[3,8,16,128]{3,2,1,0:T(8,128)S(1)}, f32[3,8,16,128]{3,2,1,0:T(8,128)S(1)}, u32[]{:S(2)}, u32[]{:S(2)}) %collective-permute-start.1) | collective-permute-done | bytes 196640 | tf_op jit(solution)/shard_map/ppermute | solution.py:626
  30.3 6.1 %collective-permute-start.3 = (f32[3,8,40,128]{3,2,1,0:T(8,128)S(1)}, f32[3,8,40,128]{3,2,1,0:T(8,128)S(1)}, u32[]{:S(2)}, u32[]{:S(2)}) collective-permute-start(f32[3,8,40,128]{3,2,1,0:T(8,128)S(1)} %pad_maximum_fusion), channel_id=1, source_target_pairs={{4,0},{36,32},{68,64},{100,96},{132,128},{164,160},{196,192},{228,... | collective-permute-start | bytes 1474568 | tf_op jit(solution)/shard_map/ppermute | solution.py:631
  36.4 3.1 collective-permute-start.2
  39.6 4.5 %collective-permute-done.3 = f32[3,8,40,128]{3,2,1,0:T(8,128)S(1)} collective-permute-done((f32[3,8,40,128]{3,2,1,0:T(8,128)S(1)}, f32[3,8,40,128]{3,2,1,0:T(8,128)S(1)}, u32[]{:S(2)}, u32[]{:S(2)}) %collective-permute-start.3) | collective-permute-done | bytes 491552 | tf_op jit(solution)/shard_map/ppermute | solution.py:631
  44.1 1.1 collective-permute-done.2
  46.0 6.4 %setup.1 = (f32[5,20,40,128]{3,2,1,0:T(8,128)S(1)}, f32[5,10,40,128]{3,2,1,0:T(8,128)S(1)}, f32[2,20,40,128]{3,2,1,0:T(8,128)S(1)}, f32[2,20,40,128]{3,2,1,0:T(8...) custom-call(s32[2]{0:T(128)S(1)} %pad_add_fusion.pos, ...), custom_call_target="tpu_custom_call" | custom-call | tf_op jit(solution)/shard_map/setup/pallas_call | solution.py:587
  52.4 0.9 copy-done
  53.3 0.9 copy-done.5
  54.2 0.8 copy-done.7
  55.0 0.8 copy-done.9
  55.8 13.5 %all_to_all.46 = f32[8,1,1280]{2,1,0:T(1,128)S(1)} all-to-all(f32[8,1,1280]{2,1,0:T(1,128)S(1)} %broadcast_in_dim.24), channel_id=1, replica_groups=mesh['gx'=8,'gy_0'=4,'gy_1'=2,'gz'=4] {'gx'}, dimensions={0} | all-to-all | bytes 81920 | tf_op jit(solution)/shard_map/all_to_all | solution.py:656
  69.4 29.4 %all_to_all.47 = f32[32,8,1280]{2,1,0:T(8,128)S(1)} all-to-all(f32[32,8,1280]{2,1,0:T(8,128)S(1)} %broadcast_in_dim.25), channel_id=1, replica_groups=mesh['gx'=8,'gy_0'=4,'gy_1'=2,'gz'=4] {'gy_0','gy_1','gz'}, dimensions={0} | all-to-all | bytes 2621440 | tf_op jit(solution)/shard_map/all_to_all | solution.py:658
  99.2 0.7 copy-done.6
  100.1 3.8 %first.1 = (f32[8,16,128]{2,1,0:T(8,128)S(1)}, f32[5,256,256]{2,1,0:T(8,128)S(1)}, f32[5,64,256]{2,1,0:T(8,128)S(1)}, f32[256,256]{1,0:T(8,128)S(1)}) custom-call(s32[2]{0:T(128)S(1)} %pad_add_fusion.pos, f32[256,1280]{1,0:T(8,128)S(1)} %bitcast.45, f32[5,20,40,128]{3,2,1,0:T(8,128)S(1)} %get-tuple-element.53.coef.refs_3_.refs_0_.refs_1_.refs_4_, ...), custom_call_target="tpu_custom_call" | custom-call | tf_op jit(solution)/shard_map/first/pallas_call | solution.py:587
  103.9 2.2 collective-permute-start.4
  106.1 1.3 collective-permute-start.5
  107.4 3.7 %collective-permute-done.5 = f32[8,16,128]{2,1,0:T(8,128)S(1)} collective-permute-done((f32[8,16,128]{2,1,0:T(8,128)S(1)}, f32[8,16,128]{2,1,0:T(8,128)S(1)}, u32[]{:S(2)}, u32[]{:S(2)}) %collective-permute-start.5) | collective-permute-done | bytes 65568 | tf_op jit(solution)/shard_map/ppermute | solution.py:626
  111.1 3.6 %collective-permute-start.7 = (f32[8,40,128]{2,1,0:T(8,128)S(1)}, f32[8,40,128]{2,1,0:T(8,128)S(1)}, u32[]{:S(2)}, u32[]{:S(2)}) collective-permute-start(f32[8,40,128]{2,1,0:T(8,128)S(1)} %pad_maximum_fusion.3.centre), channel_id=1, source_target_pairs={{4,0},{36,32},{68,64},{100,96},{132,128},{164,160},{196,192},{228,... | collective-permute-start | bytes 491528 | tf_op jit(solution)/shard_map/ppermute | solution.py:631
  114.7 2.2 collective-permute-start.6
  116.8 1.1 collective-permute-done.7.refs_1_
  117.9 1.2 collective-permute-done.6.refs_0_
  119.1 3.5 image.4
  122.7 0.7 copy-done.11
  124.4 28.8 %all_to_all.48 = f32[256,1,384]{2,1,0:T(1,128)S(1)} all-to-all(f32[256,1,384]{2,1,0:T(1,128)S(1)} %broadcast_in_dim.26), channel_id=1, replica_groups=mesh['gx'=8,'gy_0'=4,'gy_1'=2,'gz'=4] {'gx','gy_0','gy_1','gz'}, dimensions={0} | all-to-all | bytes 786432 | tf_op jit(solution)/shard_map/all_to_all | solution.py:650
  153.2 1.3 copy-done.4
  154.6 5.8 %step.3 = (f32[8,128]{1,0:T(8,128)S(1)}, f32[2,20,40,128]{3,2,1,0:T(8,128)S(1)}, f32[2,9,40,128]{3,2,1,0:T(8,128)S(1)}, f32[8,16,128]{2,1,0:T(8,128)S(1)}, f32[1,256]{1,0:T(1,128)S(1)}, /*index=5*/f32[256,256]{1,0:T(8,128)S(1)}) custom-call(s32[2]{0:T(128)S(1)} %pad_add_fusion.pos, f32[256,384]{1,0:T(8,128)S(1)} %bitcast.48, ...), custom_call_target="tpu_custom_call", output_to_operand_aliasing={{1}: (6, {})} | custom-call | tf_op jit(solution)/shard_map/step/pallas_call | solution.py:587
  160.4 2.6 collective-permute-start.8
  163.0 1.3 collective-permute-start.9
  164.3 3.7 %collective-permute-done.9 = f32[8,16,128]{2,1,0:T(8,128)S(1)} collective-permute-done((f32[8,16,128]{2,1,0:T(8,128)S(1)}, f32[8,16,128]{2,1,0:T(8,128)S(1)}, u32[]{:S(2)}, u32[]{:S(2)}) %collective-permute-start.9) | collective-permute-done | bytes 65568 | tf_op jit(solution)/shard_map/ppermute | solution.py:626
  168.0 4.1 %collective-permute-start.11 = (f32[8,40,128]{2,1,0:T(8,128)S(1)}, f32[8,40,128]{2,1,0:T(8,128)S(1)}, u32[]{:S(2)}, u32[]{:S(2)}) collective-permute-start(f32[8,40,128]{2,1,0:T(8,128)S(1)} %pad_maximum_fusion.4.centre), channel_id=1, source_target_pairs={{4,0},{36,32},{68,64},{100,96},{132,128},{164,160},{196,192},{228,... | collective-permute-start | bytes 491528 | tf_op jit(solution)/shard_map/ppermute | solution.py:631
  172.2 2.0 collective-permute-start.10
  174.1 1.1 collective-permute-done.11.refs_1_
  175.2 1.2 collective-permute-done.10.refs_0_
  176.4 3.5 image.5
  180.3 34.4 %all_to_all.49 = f32[256,1,640]{2,1,0:T(1,128)S(1)} all-to-all(f32[256,1,640]{2,1,0:T(1,128)S(1)} %broadcast_in_dim.28), channel_id=1, replica_groups=mesh['gx'=8,'gy_0'=4,'gy_1'=2,'gz'=4] {'gx','gy_0','gy_1','gz'}, dimensions={0} | all-to-all | bytes 1310720 | tf_op jit(solution)/shard_map/all_to_all | solution.py:650
  214.8 6.0 %step.4 = (f32[8,128]{1,0:T(8,128)S(1)}, f32[2,20,40,128]{3,2,1,0:T(8,128)S(1)}, f32[2,9,40,128]{3,2,1,0:T(8,128)S(1)}, f32[8,16,128]{2,1,0:T(8,128)S(1)}, f32[1,256]{1,0:T(1,128)S(1)}, /*index=5*/f32[256,256]{1,0:T(8,128)S(1)}) custom-call(s32[2]{0:T(128)S(1)} %pad_add_fusion.pos, ...), custom_call_target="tpu_custom_call", output_to_operand_aliasing={{1}: (6, {}), {2}: (7, {})} | custom-call | tf_op jit(solution)/shard_map/step/pallas_call | solution.py:587
  220.8 2.9 collective-permute-start.12
  223.7 1.3 collective-permute-start.13
  225.0 3.7 %collective-permute-done.13 = f32[8,16,128]{2,1,0:T(8,128)S(1)} collective-permute-done((f32[8,16,128]{2,1,0:T(8,128)S(1)}, f32[8,16,128]{2,1,0:T(8,128)S(1)}, u32[]{:S(2)}, u32[]{:S(2)}) %collective-permute-start.13) | collective-permute-done | bytes 65568 | tf_op jit(solution)/shard_map/ppermute | solution.py:626
  228.7 3.7 %collective-permute-start.15 = (f32[8,40,128]{2,1,0:T(8,128)S(1)}, f32[8,40,128]{2,1,0:T(8,128)S(1)}, u32[]{:S(2)}, u32[]{:S(2)}) collective-permute-start(f32[8,40,128]{2,1,0:T(8,128)S(1)} %pad_maximum_fusion.5.centre), channel_id=1, source_target_pairs={{4,0},{36,32},{68,64},{100,96},{132,128},{164,160},{196,192},{228,... | collective-permute-start | bytes 491528 | tf_op jit(solution)/shard_map/ppermute | solution.py:631
  232.4 2.3 collective-permute-start.14
  234.8 1.1 collective-permute-done.15.refs_1_
  235.8 1.2 collective-permute-done.14.refs_0_
  237.0 3.5 image.6
  240.9 34.4 %all_to_all.50 = f32[256,1,640]{2,1,0:T(1,128)S(1)} all-to-all(f32[256,1,640]{2,1,0:T(1,128)S(1)} %broadcast_in_dim.29), channel_id=1, replica_groups=mesh['gx'=8,'gy_0'=4,'gy_1'=2,'gz'=4] {'gx','gy_0','gy_1','gz'}, dimensions={0} | all-to-all | bytes 1310720 | tf_op jit(solution)/shard_map/all_to_all | solution.py:650
  275.3 6.7 %step.5 = (f32[8,128]{1,0:T(8,128)S(1)}, f32[2,20,40,128]{3,2,1,0:T(8,128)S(1)}, f32[2,9,40,128]{3,2,1,0:T(8,128)S(1)}, f32[8,16,128]{2,1,0:T(8,128)S(1)}, f32[1,256]{1,0:T(1,128)}, /*index=5*/f32[256,256]{1,0:T(8,128)}) custom-call(s32[2]{0:T(128)S(1)} %pad_add_fusion.pos, f32[256,640]{1,0:T(8,128)S(1)} %bitcast.46, ...), custom_call_target="tpu_custom_call", output_to_operand_aliasing={{1}: (6, {}), {2}: (7, {})} | custom-call | tf_op jit(solution)/shard_map/step/pallas_call | solution.py:587
  282.0 1.9 collective-permute-start.19
  283.9 3.6 %collective-permute-start.18 = (f32[1,16,128]{2,1,0:T(8,128)S(1)}, f32[1,16,128]{2,1,0:T(8,128)S(1)}, u32[]{:S(2)}, u32[]{:S(2)}) collective-permute-start(f32[1,16,128]{2,1,0:T(8,128)S(1)} %slice.90), channel_id=1, source_target_pairs={{0,4},{32,36},{64,68},{96,100},{128,132},{160,164},{192,196},{224,... | collective-permute-start | bytes 24584 | tf_op jit(solution)/shard_map/ppermute | solution.py:631
  287.6 1.3 collective-permute-start.17
  288.9 4.0 %collective-permute-start.16 = (f32[8,8,128]{2,1,0:T(8,128)S(1)}, f32[8,8,128]{2,1,0:T(8,128)S(1)}, u32[]{:S(2)}, u32[]{:S(2)}) collective-permute-start(f32[8,8,128]{2,1,0:T(8,128)S(1)} %get-tuple-element.103), channel_id=1, source_target_pairs={{0,32},{32,64},{64,96},{96,128},{128,160},{160,192},{192,224},{224... | collective-permute-start | bytes 98312 | tf_op jit(solution)/shard_map/ppermute | solution.py:635
  293.1 0.8 collective-permute-done.16.refs_0_
  294.3 22.6 %all_to_all.51 = f32[256,1,128]{2,1,0:T(1,128)S(1)} all-to-all(f32[256,1,128]{2,1,0:T(1,128)S(1)} %broadcast_in_dim.30), channel_id=1, replica_groups=mesh['gx'=8,'gy_0'=4,'gy_1'=2,'gz'=4] {'gx','gy_0','gy_1','gz'}, dimensions={0} | all-to-all | bytes 262144 | tf_op jit(solution)/shard_map/all_to_all | solution.py:650
  317.0 2.8 finish.1
  320.1 0.8 broadcast_in_dim.31
  321.0 10.1 %all_to_all.52 = f32[8,8,512]{2,1,0:T(8,128)S(1)} all-to-all(f32[8,8,512]{2,1,0:T(8,128)S(1)} %bitcast.61), channel_id=1, replica_groups=mesh['gx'=8,'gy_0'=4,'gy_1'=2,'gz'=4] {'gx'}, dimensions={0} | all-to-all | bytes 262144 | tf_op jit(solution)/shard_map/all_to_all | solution.py:715
  331.1 7.3 %all-to-all-start.8 = ((f32[256,1,256]{2,1,0:T(1,128)}), f32[256,1,256]{2,1,0:T(1,128)S(1)}, u32[]{:S(2)}, u32[]{:S(2)}) async-start(f32[256,1,256]{2,1,0:T(1,128)} %broadcast_in_dim.31), calls=%async_computation.8 | async-start | bytes 524288 | tf_op jit(solution)/shard_map/all_to_all | solution.py:714
  339.2 0.8 squeeze.23
  340.3 0.8 squeeze.22
  341.2 12.6 %all-to-all-done.8 = f32[256,1,256]{2,1,0:T(1,128)S(1)} async-done(((f32[256,1,256]{2,1,0:T(1,128)}), f32[256,1,256]{2,1,0:T(1,128)S(1)}, u32[]{:S(2)}, u32[]{:S(2)}) %all-to-all-start.8) | async-done | bytes 262176 | tf_op jit(solution)/shard_map/all_to_all | solution.py:714
  (103 shorter events, 9.5 us)
Async XLA Ops:
  0.6 1.2 copy-start.17
  1.7 0.8 copy-start.18
  21.7 17.9 %copy-start.19 = (s32[4]{0:T(128)S(1)}, s32[4]{0:T(128)}, u32[]{:S(2)}) copy-start(s32[4]{0:T(128)} %param.7) | copy-start | bytes 52
  21.8 4.5 %collective-permute-start = (f32[3,8,16,128]{3,2,1,0:T(8,128)S(1)}, f32[3,8,16,128]{3,2,1,0:T(8,128)S(1)}, u32[]{:S(2)}, u32[]{:S(2)}) collective-permute-start(f32[3,8,16,128]{3,2,1,0:T(8,128)S(1)} %pad_maximum_fusion.2), channel_id=1, source_target_pairs={{0,32},{32,64},{64,96},{96,128},{128,160},{160,192},{192,224},{224... | collective-permute-start | bytes 589832 | tf_op jit(solution)/shard_map/ppermute | solution.py:625
  23.7 6.4 %collective-permute-start.1 = (f32[3,8,16,128]{3,2,1,0:T(8,128)S(1)}, f32[3,8,16,128]{3,2,1,0:T(8,128)S(1)}, u32[]{:S(2)}, u32[]{:S(2)}) collective-permute-start(f32[3,8,16,128]{3,2,1,0:T(8,128)S(1)} %pad_maximum_fusion.2), channel_id=1, source_target_pairs={{32,0},{64,32},{96,64},{128,96},{160,128},{192,160},{224,192},{1,2... | collective-permute-start | bytes 589832 | tf_op jit(solution)/shard_map/ppermute | solution.py:626
  30.3 13.8 %collective-permute-start.3 = (f32[3,8,40,128]{3,2,1,0:T(8,128)S(1)}, f32[3,8,40,128]{3,2,1,0:T(8,128)S(1)}, u32[]{:S(2)}, u32[]{:S(2)}) collective-permute-start(f32[3,8,40,128]{3,2,1,0:T(8,128)S(1)} %pad_maximum_fusion), channel_id=1, source_target_pairs={{4,0},{36,32},{68,64},{100,96},{132,128},{164,160},{196,192},{228,... | collective-permute-start | bytes 1474568 | tf_op jit(solution)/shard_map/ppermute | solution.py:631
  36.4 8.9 %collective-permute-start.2 = (f32[3,8,40,128]{3,2,1,0:T(8,128)S(1)}, f32[3,8,40,128]{3,2,1,0:T(8,128)S(1)}, u32[]{:S(2)}, u32[]{:S(2)}) collective-permute-start(f32[3,8,40,128]{3,2,1,0:T(8,128)S(1)} %pad_maximum_fusion), channel_id=1, source_target_pairs={{0,4},{32,36},{64,68},{96,100},{128,132},{160,164},{192,196},{224,... | collective-permute-start | bytes 1474568 | tf_op jit(solution)/shard_map/ppermute | solution.py:631
  52.4 0.9 copy-start
  53.3 0.9 copy-start.5
  54.2 0.8 copy-start.7
  55.0 0.8 copy-start.9
  98.8 1.1 copy-start.6
  98.8 1.2 copy-start.10
  100.1 19.0 %copy-start.1 = (f32[2,20,40,128]{3,2,1,0:T(8,128)S(1)}, f32[2,20,40,128]{3,2,1,0:T(8,128)}, u32[]{:S(2)}) copy-start(f32[2,20,40,128]{3,2,1,0:T(8,128)} %copy-done) | copy-start | bytes 2457604
  103.8 18.8 %copy-start.3 = (f32[5,256,256]{2,1,0:T(8,128)}, f32[5,256,256]{2,1,0:T(8,128)S(1)}, u32[]{:S(2)}) copy-start(f32[5,256,256]{2,1,0:T(8,128)S(1)} %get-tuple-element.63.refs_2_.refs_3_) | copy-start | bytes 3932164
  103.8 18.8 %copy-start.13 = (f32[256,256]{1,0:T(8,128)}, f32[256,256]{1,0:T(8,128)S(1)}, u32[]{:S(2)}) copy-start(f32[256,256]{1,0:T(8,128)S(1)} %get-tuple-element.62.b2_was) | copy-start | bytes 786436
  103.9 3.5 collective-permute-start.4
  106.1 5.0 %collective-permute-start.5 = (f32[8,16,128]{2,1,0:T(8,128)S(1)}, f32[8,16,128]{2,1,0:T(8,128)S(1)}, u32[]{:S(2)}, u32[]{:S(2)}) collective-permute-start(f32[8,16,128]{2,1,0:T(8,128)S(1)} %get-tuple-element.57), channel_id=1, source_target_pairs={{32,0},{64,32},{96,64},{128,96},{160,128},{192,160},{224,192},{1,2... | collective-permute-start | bytes 196616 | tf_op jit(solution)/shard_map/ppermute | solution.py:626
  111.1 6.8 %collective-permute-start.7 = (f32[8,40,128]{2,1,0:T(8,128)S(1)}, f32[8,40,128]{2,1,0:T(8,128)S(1)}, u32[]{:S(2)}, u32[]{:S(2)}) collective-permute-start(f32[8,40,128]{2,1,0:T(8,128)S(1)} %pad_maximum_fusion.3.centre), channel_id=1, source_target_pairs={{4,0},{36,32},{68,64},{100,96},{132,128},{164,160},{196,192},{228,... | collective-permute-start | bytes 491528 | tf_op jit(solution)/shard_map/ppermute | solution.py:631
  114.7 4.4 %collective-permute-start.6 = (f32[8,40,128]{2,1,0:T(8,128)S(1)}, f32[8,40,128]{2,1,0:T(8,128)S(1)}, u32[]{:S(2)}, u32[]{:S(2)}) collective-permute-start(f32[8,40,128]{2,1,0:T(8,128)S(1)} %pad_maximum_fusion.3.centre), channel_id=1, source_target_pairs={{0,4},{32,36},{64,68},{96,100},{128,132},{160,164},{192,196},{224,... | collective-permute-start | bytes 491528 | tf_op jit(solution)/shard_map/ppermute | solution.py:631
  122.7 0.8 copy-start.11
  123.4 0.7 copy-start.15
  124.1 29.1 %copy-start.2 = (f32[2,20,40,128]{3,2,1,0:T(8,128)S(1)}, f32[2,20,40,128]{3,2,1,0:T(8,128)}, u32[]{:S(2)}) copy-start(f32[2,20,40,128]{3,2,1,0:T(8,128)} %copy-done) | copy-start | bytes 2457604
  124.1 29.1 %copy-start.12 = (f32[20,40,128]{2,1,0:T(8,128)S(1)}, f32[20,40,128]{2,1,0:T(8,128)}, u32[]{:S(2)}) copy-start(f32[20,40,128]{2,1,0:T(8,128)} %copy-done.11) | copy-start | bytes 1228804
  124.1 29.1 %copy-start.14 = (f32[256,256]{1,0:T(8,128)S(1)}, f32[256,256]{1,0:T(8,128)}, u32[]{:S(2)}) copy-start(f32[256,256]{1,0:T(8,128)} %copy-done.13) | copy-start | bytes 786436
  124.1 29.1 %copy-start.16 = (f32[9,40,128]{2,1,0:T(8,128)S(1)}, f32[9,40,128]{2,1,0:T(8,128)}, u32[]{:S(2)}) copy-start(f32[9,40,128]{2,1,0:T(8,128)} %copy-done.15) | copy-start | bytes 552964
  153.2 1.3 copy-start.4
  160.4 3.9 %collective-permute-start.8 = (f32[8,16,128]{2,1,0:T(8,128)S(1)}, f32[8,16,128]{2,1,0:T(8,128)S(1)}, u32[]{:S(2)}, u32[]{:S(2)}) collective-permute-start(f32[8,16,128]{2,1,0:T(8,128)S(1)} %get-tuple-element.65), channel_id=1, source_target_pairs={{0,32},{32,64},{64,96},{96,128},{128,160},{160,192},{192,224},{224... | collective-permute-start | bytes 196616 | tf_op jit(solution)/shard_map/ppermute | solution.py:625
  163.0 5.0 %collective-permute-start.9 = (f32[8,16,128]{2,1,0:T(8,128)S(1)}, f32[8,16,128]{2,1,0:T(8,128)S(1)}, u32[]{:S(2)}, u32[]{:S(2)}) collective-permute-start(f32[8,16,128]{2,1,0:T(8,128)S(1)} %get-tuple-element.65), channel_id=1, source_target_pairs={{32,0},{64,32},{96,64},{128,96},{160,128},{192,160},{224,192},{1,2... | collective-permute-start | bytes 196616 | tf_op jit(solution)/shard_map/ppermute | solution.py:626
  168.0 7.2 %collective-permute-start.11 = (f32[8,40,128]{2,1,0:T(8,128)S(1)}, f32[8,40,128]{2,1,0:T(8,128)S(1)}, u32[]{:S(2)}, u32[]{:S(2)}) collective-permute-start(f32[8,40,128]{2,1,0:T(8,128)S(1)} %pad_maximum_fusion.4.centre), channel_id=1, source_target_pairs={{4,0},{36,32},{68,64},{100,96},{132,128},{164,160},{196,192},{228,... | collective-permute-start | bytes 491528 | tf_op jit(solution)/shard_map/ppermute | solution.py:631
  172.2 4.2 %collective-permute-start.10 = (f32[8,40,128]{2,1,0:T(8,128)S(1)}, f32[8,40,128]{2,1,0:T(8,128)S(1)}, u32[]{:S(2)}, u32[]{:S(2)}) collective-permute-start(f32[8,40,128]{2,1,0:T(8,128)S(1)} %pad_maximum_fusion.4.centre), channel_id=1, source_target_pairs={{0,4},{32,36},{64,68},{96,100},{128,132},{160,164},{192,196},{224,... | collective-permute-start | bytes 491528 | tf_op jit(solution)/shard_map/ppermute | solution.py:631
  220.8 4.2 %collective-permute-start.12 = (f32[8,16,128]{2,1,0:T(8,128)S(1)}, f32[8,16,128]{2,1,0:T(8,128)S(1)}, u32[]{:S(2)}, u32[]{:S(2)}) collective-permute-start(f32[8,16,128]{2,1,0:T(8,128)S(1)} %get-tuple-element.74), channel_id=1, source_target_pairs={{0,32},{32,64},{64,96},{96,128},{128,160},{160,192},{192,224},{224... | collective-permute-start | bytes 196616 | tf_op jit(solution)/shard_map/ppermute | solution.py:625
  223.7 5.0 %collective-permute-start.13 = (f32[8,16,128]{2,1,0:T(8,128)S(1)}, f32[8,16,128]{2,1,0:T(8,128)S(1)}, u32[]{:S(2)}, u32[]{:S(2)}) collective-permute-start(f32[8,16,128]{2,1,0:T(8,128)S(1)} %get-tuple-element.74), channel_id=1, source_target_pairs={{32,0},{64,32},{96,64},{128,96},{160,128},{192,160},{224,192},{1,2... | collective-permute-start | bytes 196616 | tf_op jit(solution)/shard_map/ppermute | solution.py:626
  228.7 7.1 %collective-permute-start.15 = (f32[8,40,128]{2,1,0:T(8,128)S(1)}, f32[8,40,128]{2,1,0:T(8,128)S(1)}, u32[]{:S(2)}, u32[]{:S(2)}) collective-permute-start(f32[8,40,128]{2,1,0:T(8,128)S(1)} %pad_maximum_fusion.5.centre), channel_id=1, source_target_pairs={{4,0},{36,32},{68,64},{100,96},{132,128},{164,160},{196,192},{228,... | collective-permute-start | bytes 491528 | tf_op jit(solution)/shard_map/ppermute | solution.py:631
  232.4 4.6 %collective-permute-start.14 = (f32[8,40,128]{2,1,0:T(8,128)S(1)}, f32[8,40,128]{2,1,0:T(8,128)S(1)}, u32[]{:S(2)}, u32[]{:S(2)}) collective-permute-start(f32[8,40,128]{2,1,0:T(8,128)S(1)} %pad_maximum_fusion.5.centre), channel_id=1, source_target_pairs={{0,4},{32,36},{64,68},{96,100},{128,132},{160,164},{192,196},{224,... | collective-permute-start | bytes 491528 | tf_op jit(solution)/shard_map/ppermute | solution.py:631
  282.0 11.0 %collective-permute-start.19 = (f32[1,16,128]{2,1,0:T(8,128)S(1)}, f32[1,16,128]{2,1,0:T(8,128)S(1)}, u32[]{:S(2)}, u32[]{:S(2)}) collective-permute-start(f32[1,16,128]{2,1,0:T(8,128)S(1)} %slice.90), channel_id=1, source_target_pairs={{4,0},{36,32},{68,64},{100,96},{132,128},{164,160},{196,192},{228,... | collective-permute-start | bytes 24584 | tf_op jit(solution)/shard_map/ppermute | solution.py:631
  283.9 9.0 %collective-permute-start.18 = (f32[1,16,128]{2,1,0:T(8,128)S(1)}, f32[1,16,128]{2,1,0:T(8,128)S(1)}, u32[]{:S(2)}, u32[]{:S(2)}) collective-permute-start(f32[1,16,128]{2,1,0:T(8,128)S(1)} %slice.90), channel_id=1, source_target_pairs={{0,4},{32,36},{64,68},{96,100},{128,132},{160,164},{192,196},{224,... | collective-permute-start | bytes 24584 | tf_op jit(solution)/shard_map/ppermute | solution.py:631
  287.6 5.5 %collective-permute-start.17 = (f32[8,8,128]{2,1,0:T(8,128)S(1)}, f32[8,8,128]{2,1,0:T(8,128)S(1)}, u32[]{:S(2)}, u32[]{:S(2)}) collective-permute-start(f32[8,8,128]{2,1,0:T(8,128)S(1)} %get-tuple-element.102), channel_id=1, source_target_pairs={{32,0},{64,32},{96,64},{128,96},{160,128},{192,160},{224,192},{1,2... | collective-permute-start | bytes 98312 | tf_op jit(solution)/shard_map/ppermute | solution.py:636
  288.9 5.0 %collective-permute-start.16 = (f32[8,8,128]{2,1,0:T(8,128)S(1)}, f32[8,8,128]{2,1,0:T(8,128)S(1)}, u32[]{:S(2)}, u32[]{:S(2)}) collective-permute-start(f32[8,8,128]{2,1,0:T(8,128)S(1)} %get-tuple-element.103), channel_id=1, source_target_pairs={{0,32},{32,64},{64,96},{96,128},{128,160},{160,192},{192,224},{224... | collective-permute-start | bytes 98312 | tf_op jit(solution)/shard_map/ppermute | solution.py:635
  293.9 23.1 %copy-start.8 = (f32[3,9,40,128]{3,2,1,0:T(8,128)S(1)}, f32[3,9,40,128]{3,2,1,0:T(8,128)}, u32[]{:S(2)}) copy-start(f32[3,9,40,128]{3,2,1,0:T(8,128)} %copy-done.7) | copy-start | bytes 1658884
  331.1 22.7 %all-to-all-start.8 = ((f32[256,1,256]{2,1,0:T(1,128)}), f32[256,1,256]{2,1,0:T(1,128)S(1)}, u32[]{:S(2)}, u32[]{:S(2)}) async-start(f32[256,1,256]{2,1,0:T(1,128)} %broadcast_in_dim.31), calls=%async_computation.8 | async-start | bytes 524288 | tf_op jit(solution)/shard_map/all_to_all | solution.py:714

commit v3 on v2

--- a/solution.py
+++ b/solution.py
@@ -273,12 +273,17 @@
 
 
 def next_z(v):
-    return jnp.where(lane_ids() < 224, roll(v, -32, 1), roll(v, 223, 1))
+    lanes = lane_ids()
+    ahead = jnp.where(lanes < 224, roll(v, -32, 1), roll(v, -1, 1))
+    back = jnp.where(lanes >= 32, roll(v, 32, 1), roll(v, -1, 1))
+    return jnp.where(lanes % 2 == 0, ahead, back)
 
 
 def prev_z(v):
     lanes = lane_ids()
-    return jnp.where(lanes >= 32, roll(v, 32, 1), jnp.where(lanes == 0, 0.0, roll(v, -223, 1)))
+    back = jnp.where(lanes >= 32, roll(v, 32, 1), jnp.where(lanes == 0, 0.0, roll(v, 1, 1)))
+    ahead = jnp.where(lanes < 224, roll(v, -32, 1), roll(v, 1, 1))
+    return jnp.where(lanes % 2 == 0, back, ahead)
 
 
 def next_y(v):
@@ -413,7 +418,8 @@
         for dz in (-1, 0, 1):
             at_y = jnp.clip(gy + dy, 0, NGY - 1)
             at_z = jnp.clip(zb + dz, 0, NZB - 1)
-            picked[dy, dz] = lanes == ((at_z % NGX) * NGY + at_y) * NGZ + at_z // NGX
+            gz, k = at_z // NGX, at_z % NGX
+            picked[dy, dz] = lanes == (jnp.where(gz % 2 == 0, k, NGX - 1 - k) * NGY + at_y) * NGZ + gz
     lane = lax.broadcasted_iota(jnp.int32, (16, 128), 1)
     spread = lane % NX // 4 == lax.broadcasted_iota(jnp.int32, (16, 128), 0)
     rows_z = ziota() // 4
@@ -609,15 +615,18 @@
 PLANES = (256, NDEV)
 
 
+def device_of(gy, zb):
+    gz, k = zb // NGX, zb % NGX
+    return ((k if gz % 2 == 0 else NGX - 1 - k) * NGY + gy) * NGZ + gz
+
+
 def shift_pairs(dy, dz):
     pairs = []
     for gy in range(NGY):
         for zb in range(NZB):
             ty, tz = gy + dy, zb + dz
             if 0 <= ty < NGY and 0 <= tz < NZB:
-                source = ((zb % NGX) * NGY + gy) * NGZ + zb // NGX
-                target = ((tz % NGX) * NGY + ty) * NGZ + tz // NGX
-                pairs.append((source, target))
+                pairs.append((device_of(gy, zb), device_of(ty, tz)))
     return pairs
 
 
@@ -662,11 +671,14 @@
 def on_device(iterate, source, reaction, trial_powers):
     gx = lax.axis_index("gx")
     gy = lax.axis_index(GY)
-    zb = lax.axis_index("gz") * NGX + gx
+    gz = lax.axis_index("gz")
+    down_gx = gz % 2 == 1
+    zb = gz * NGX + jnp.where(down_gx, NGX - 1 - gx, gx)
     pos = jnp.stack([gy, zb]).astype(jnp.int32)
     pos, steps = lax.optimization_barrier((pos, jnp.exp2(-trial_powers.astype(F32))))
     fields = jnp.stack([iterate, source, reaction])
     fields = fields.reshape(3, 8, 16, 8, 16).transpose(3, 1, 0, 2, 4).reshape(8, 8, 3, 256)
+    fields = jnp.where(down_gx, fields[::-1], fields)
     fields = lax.all_to_all(fields, "gx", split_axis=0, concat_axis=0, tiled=True)
     fields = fields.reshape(NX, 3 * 256).T.reshape(3, 16, 16, NX)
     fields = jnp.concatenate([fields[:, :8], fields[:, :7:-1]], axis=-1)
@@ -713,6 +725,7 @@
     copies, both = lax.optimization_barrier((copies, both.reshape(8, 8, 512)))
     layers = lax.all_to_all(copies, ALL, split_axis=0, concat_axis=0, tiled=True)
     both = lax.all_to_all(both, "gx", split_axis=0, concat_axis=0, tiled=True)
+    both = jnp.where(down_gx, both[::-1], both)
     both = both.reshape(8, 8, 2, 16, 16).transpose(2, 1, 3, 0, 4).reshape(2, 8, 16, 128)
     layers = layers.sum(axis=0).reshape(TRIALS, NX) / (NY * NZ)
     energies = jnp.sum(layers, axis=1) / NX

time: 357 us -> 350 us (0.980)
  blocking collectives: 191 us -> 183 us
    all_to_all x4, blocking collectives: 120 us -> 115 us  [to_everyone(): return lax.all_to_all(copies, ALL, split_axis=0, concat_axis=0, tiled=True)]
    all_to_all x1, blocking collectives: 13.5 us -> 9.85 us  [to_everyone_by_axes(): got = lax.all_to_all(copies, 'gx', split_axis=0, concat_axis=0, tiled=True)]
where the time goes in v3:
time: 350 us; the launch traced here: 349 us
  blocking collectives  183 us (52%)
  starting transfers between devices  59.9 us (17%)
  Pallas kernels  43.2 us (12%)
  waiting for transfers between devices  42 us (12%)
  local copies, waits for them, and re-layouts  16.6 us (5%)
    all_to_all x4, blocking collectives, to_everyone(): return lax.all_to_all(copies, ALL, split_axis=0, concat_axis=0, tiled=True)  115 us
    pallas_call x10, Pallas kernels, run(): pl.pallas_call(kernel, in_specs=[SM] * n_scalar + [VM] * (len(args) - n_s...  43.2 us
    all_to_all x1, blocking collectives, to_everyone_by_axes(): lax.all_to_all(copies, (*GY, 'gz'), split_axis=0, concat_axis=0, tiled=True)  31.1 us
    ppermute x5, starting transfers between devices, exchange_y(): lax.ppermute(own, ALL, shift_pairs(-1, 0))  19.5 us
    all_to_all x1, blocking collectives, on_device(): lax.all_to_all(fields, 'gx', split_axis=0, concat_axis=0, tiled=True)  17.8 us
    ppermute x4, waiting for transfers between devices, exchange_z(): high = lax.ppermute(own, ALL, shift_pairs(0, -1))  14.9 us
    ppermute x5, starting transfers between devices, exchange_y(): lax.ppermute(own, ALL, shift_pairs(1, 0))  13.2 us
    all_to_all x1, waiting for transfers between devices, on_device(): lax.all_to_all(copies, ALL, split_axis=0, concat_axis=0, tiled=True)  12.6 us
  transfers between devices with their start and end apart: 21, of which 15 were waited for; matrix products, arithmetic and copies ran while one was open for 1% of the time, Pallas kernels for 0%

profile of v3, /device:TPU:1, one launch (start us, length us, event | category | flops | bytes accessed | tf_op | source)
XLA Modules:
  0.0 348.6 jit_solution(3076960349544298897)
XLA Ops:
  0.7 1.1 stack.33
  3.7 17.8 %all_to_all.45 = f32[8,8,3,256]{3,1,2,0:T(8,128)S(1)} all-to-all(f32[8,8,3,256]{3,1,2,0:T(8,128)S(1)} %reverse_select_fusion), channel_id=1, replica_groups=mesh['gx'=8,'gy_0'=4,'gy_1'=2,'gz'=4] {'gx'}, dimensions={0} | all-to-all | bytes 393216 | tf_op jit(solution)/shard_map/all_to_all | solution.py:682
  21.9 1.9 collective-permute-start
  23.8 1.3 collective-permute-start.1
  25.1 1.3 collective-permute-done
  26.4 3.8 %collective-permute-done.1 = f32[3,8,16,128]{3,2,1,0:T(8,128)S(1)} collective-permute-done((f32[3,8,16,128]{3,2,1,0:T(8,128)S(1)}, f32[3,8,16,128]{3,2,1,0:T(8,128)S(1)}, u32[]{:S(2)}, u32[]{:S(2)}) %collective-permute-start.1) | collective-permute-done | bytes 196640 | tf_op jit(solution)/shard_map/ppermute | solution.py:635
  30.3 6.1 %collective-permute-start.3 = (f32[3,8,40,128]{3,2,1,0:T(8,128)S(1)}, f32[3,8,40,128]{3,2,1,0:T(8,128)S(1)}, u32[]{:S(2)}, u32[]{:S(2)}) collective-permute-start(f32[3,8,40,128]{3,2,1,0:T(8,128)S(1)} %pad_maximum_fusion), channel_id=1, source_target_pairs={{4,0},{36,32},{68,64},{100,96},{132,128},{164,160},{196,192},{228,... | collective-permute-start | bytes 1474568 | tf_op jit(solution)/shard_map/ppermute | solution.py:640
  36.4 3.1 collective-permute-start.2
  39.7 4.5 %collective-permute-done.3 = f32[3,8,40,128]{3,2,1,0:T(8,128)S(1)} collective-permute-done((f32[3,8,40,128]{3,2,1,0:T(8,128)S(1)}, f32[3,8,40,128]{3,2,1,0:T(8,128)S(1)}, u32[]{:S(2)}, u32[]{:S(2)}) %collective-permute-start.3) | collective-permute-done | bytes 491552 | tf_op jit(solution)/shard_map/ppermute | solution.py:640
  44.2 1.1 collective-permute-done.2
  46.0 6.4 %setup.1 = (f32[5,20,40,128]{3,2,1,0:T(8,128)S(1)}, f32[5,10,40,128]{3,2,1,0:T(8,128)S(1)}, f32[2,20,40,128]{3,2,1,0:T(8,128)S(1)}, f32[2,20,40,128]{3,2,1,0:T(8...) custom-call(s32[2]{0:T(128)S(1)} %pad_add_fusion.pos, ...), custom_call_target="tpu_custom_call" | custom-call | tf_op jit(solution)/shard_map/setup/pallas_call | solution.py:593
  52.4 0.9 copy-done
  53.3 0.9 copy-done.5
  54.2 0.8 copy-done.7
  55.0 0.8 copy-done.9
  55.8 9.9 %all_to_all.46 = f32[8,1,1280]{2,1,0:T(1,128)S(1)} all-to-all(f32[8,1,1280]{2,1,0:T(1,128)S(1)} %broadcast_in_dim.24), channel_id=1, replica_groups=mesh['gx'=8,'gy_0'=4,'gy_1'=2,'gz'=4] {'gx'}, dimensions={0} | all-to-all | bytes 81920 | tf_op jit(solution)/shard_map/all_to_all | solution.py:665
  65.8 31.1 %all_to_all.47 = f32[32,8,1280]{2,1,0:T(8,128)S(1)} all-to-all(f32[32,8,1280]{2,1,0:T(8,128)S(1)} %broadcast_in_dim.25), channel_id=1, replica_groups=mesh['gx'=8,'gy_0'=4,'gy_1'=2,'gz'=4] {'gy_0','gy_1','gz'}, dimensions={0} | all-to-all | bytes 2621440 | tf_op jit(solution)/shard_map/all_to_all | solution.py:667
  97.3 0.7 copy-done.6
  98.1 3.8 %first.1 = (f32[8,16,128]{2,1,0:T(8,128)S(1)}, f32[5,256,256]{2,1,0:T(8,128)S(1)}, f32[5,64,256]{2,1,0:T(8,128)S(1)}, f32[256,256]{1,0:T(8,128)S(1)}) custom-call(s32[2]{0:T(128)S(1)} %pad_add_fusion.pos, f32[256,1280]{1,0:T(8,128)S(1)} %bitcast.45, f32[5,20,40,128]{3,2,1,0:T(8,128)S(1)} %get-tuple-element.53.coef.refs_3_.refs_0_.refs_1_.refs_4_, ...), custom_call_target="tpu_custom_call" | custom-call | tf_op jit(solution)/shard_map/first/pallas_call | solution.py:593
  101.9 2.2 collective-permute-start.4
  104.1 1.3 collective-permute-start.5
  105.4 3.7 %collective-permute-done.5 = f32[8,16,128]{2,1,0:T(8,128)S(1)} collective-permute-done((f32[8,16,128]{2,1,0:T(8,128)S(1)}, f32[8,16,128]{2,1,0:T(8,128)S(1)}, u32[]{:S(2)}, u32[]{:S(2)}) %collective-permute-start.5) | collective-permute-done | bytes 65568 | tf_op jit(solution)/shard_map/ppermute | solution.py:635
  109.2 3.6 %collective-permute-start.7 = (f32[8,40,128]{2,1,0:T(8,128)S(1)}, f32[8,40,128]{2,1,0:T(8,128)S(1)}, u32[]{:S(2)}, u32[]{:S(2)}) collective-permute-start(f32[8,40,128]{2,1,0:T(8,128)S(1)} %pad_maximum_fusion.3.centre), channel_id=1, source_target_pairs={{4,0},{36,32},{68,64},{100,96},{132,128},{164,160},{196,192},{228,... | collective-permute-start | bytes 491528 | tf_op jit(solution)/shard_map/ppermute | solution.py:640
  112.7 2.2 collective-permute-start.6
  114.9 1.1 collective-permute-done.7.refs_1_
  116.0 1.2 collective-permute-done.6.refs_0_
  117.2 3.5 %image.4 = (f32[9,40,128]{2,1,0:T(8,128)S(1)}, f32[20,40,128]{2,1,0:T(8,128)S(1)}, f32[1,384]{1,0:T(1,128)S(1)}) custom-call(f32[8,40,128]{2,1,0:T(8,128)S(1)} %pad_maximum_fusion.3.centre, f32[8,40,128]{2,1,0:T(8,128)S(1)} %collective-permute-done.6.refs_0_, f32[8,40,128]{2,1,0:T(8,128)S(1)} %collective-permute-done.7.refs_1_, ...), custom_call_target="tpu_custom_call" | custom-call | tf_op jit(solution)/shard_map/image/pallas_call | solution.py:593
  120.7 0.7 copy-done.11
  122.4 27.0 %all_to_all.48 = f32[256,1,384]{2,1,0:T(1,128)S(1)} all-to-all(f32[256,1,384]{2,1,0:T(1,128)S(1)} %broadcast_in_dim.26), channel_id=1, replica_groups=mesh['gx'=8,'gy_0'=4,'gy_1'=2,'gz'=4] {'gx','gy_0','gy_1','gz'}, dimensions={0} | all-to-all | bytes 786432 | tf_op jit(solution)/shard_map/all_to_all | solution.py:659
  149.5 1.3 copy-done.4
  150.8 6.0 %step.3 = (f32[8,128]{1,0:T(8,128)S(1)}, f32[2,20,40,128]{3,2,1,0:T(8,128)S(1)}, f32[2,9,40,128]{3,2,1,0:T(8,128)S(1)}, f32[8,16,128]{2,1,0:T(8,128)S(1)}, f32[1,256]{1,0:T(1,128)S(1)}, /*index=5*/f32[256,256]{1,0:T(8,128)S(1)}) custom-call(s32[2]{0:T(128)S(1)} %pad_add_fusion.pos, f32[256,384]{1,0:T(8,128)S(1)} %bitcast.48, ...), custom_call_target="tpu_custom_call", output_to_operand_aliasing={{1}: (6, {})} | custom-call | tf_op jit(solution)/shard_map/step/pallas_call | solution.py:593
  156.8 2.6 collective-permute-start.8
  159.4 1.3 collective-permute-start.9
  160.7 3.7 %collective-permute-done.9 = f32[8,16,128]{2,1,0:T(8,128)S(1)} collective-permute-done((f32[8,16,128]{2,1,0:T(8,128)S(1)}, f32[8,16,128]{2,1,0:T(8,128)S(1)}, u32[]{:S(2)}, u32[]{:S(2)}) %collective-permute-start.9) | collective-permute-done | bytes 65568 | tf_op jit(solution)/shard_map/ppermute | solution.py:635
  164.4 4.1 %collective-permute-start.11 = (f32[8,40,128]{2,1,0:T(8,128)S(1)}, f32[8,40,128]{2,1,0:T(8,128)S(1)}, u32[]{:S(2)}, u32[]{:S(2)}) collective-permute-start(f32[8,40,128]{2,1,0:T(8,128)S(1)} %pad_maximum_fusion.4.centre), channel_id=1, source_target_pairs={{4,0},{36,32},{68,64},{100,96},{132,128},{164,160},{196,192},{228,... | collective-permute-start | bytes 491528 | tf_op jit(solution)/shard_map/ppermute | solution.py:640
  168.6 2.0 collective-permute-start.10
  170.6 1.1 collective-permute-done.11.refs_1_
  171.6 1.2 collective-permute-done.10.refs_0_
  172.8 3.5 %image.5 = (f32[9,40,128]{2,1,0:T(8,128)S(1)}, f32[20,40,128]{2,1,0:T(8,128)S(1)}, f32[1,384]{1,0:T(1,128)S(1)}) custom-call(f32[8,40,128]{2,1,0:T(8,128)S(1)} %pad_maximum_fusion.4.centre, f32[8,40,128]{2,1,0:T(8,128)S(1)} %collective-permute-done.10.refs_0_, f32[8,40,128]{2,1,0:T(8,128)S(1)} %collective-permute-done.11.refs_1_, ...), custom_call_target="tpu_custom_call" | custom-call | tf_op jit(solution)/shard_map/image/pallas_call | solution.py:593
  176.7 32.5 %all_to_all.49 = f32[256,1,640]{2,1,0:T(1,128)S(1)} all-to-all(f32[256,1,640]{2,1,0:T(1,128)S(1)} %broadcast_in_dim.28), channel_id=1, replica_groups=mesh['gx'=8,'gy_0'=4,'gy_1'=2,'gz'=4] {'gx','gy_0','gy_1','gz'}, dimensions={0} | all-to-all | bytes 1310720 | tf_op jit(solution)/shard_map/all_to_all | solution.py:659
  209.3 6.3 %step.4 = (f32[8,128]{1,0:T(8,128)S(1)}, f32[2,20,40,128]{3,2,1,0:T(8,128)S(1)}, f32[2,9,40,128]{3,2,1,0:T(8,128)S(1)}, f32[8,16,128]{2,1,0:T(8,128)S(1)}, f32[1,256]{1,0:T(1,128)S(1)}, /*index=5*/f32[256,256]{1,0:T(8,128)S(1)}) custom-call(s32[2]{0:T(128)S(1)} %pad_add_fusion.pos, ...), custom_call_target="tpu_custom_call", output_to_operand_aliasing={{1}: (6, {}), {2}: (7, {})} | custom-call | tf_op jit(solution)/shard_map/step/pallas_call | solution.py:593
  215.5 2.9 collective-permute-start.12
  218.4 1.3 collective-permute-start.13
  219.7 3.7 %collective-permute-done.13 = f32[8,16,128]{2,1,0:T(8,128)S(1)} collective-permute-done((f32[8,16,128]{2,1,0:T(8,128)S(1)}, f32[8,16,128]{2,1,0:T(8,128)S(1)}, u32[]{:S(2)}, u32[]{:S(2)}) %collective-permute-start.13) | collective-permute-done | bytes 65568 | tf_op jit(solution)/shard_map/ppermute | solution.py:635
  223.5 3.7 %collective-permute-start.15 = (f32[8,40,128]{2,1,0:T(8,128)S(1)}, f32[8,40,128]{2,1,0:T(8,128)S(1)}, u32[]{:S(2)}, u32[]{:S(2)}) collective-permute-start(f32[8,40,128]{2,1,0:T(8,128)S(1)} %pad_maximum_fusion.5.centre), channel_id=1, source_target_pairs={{4,0},{36,32},{68,64},{100,96},{132,128},{164,160},{196,192},{228,... | collective-permute-start | bytes 491528 | tf_op jit(solution)/shard_map/ppermute | solution.py:640
  227.2 2.3 collective-permute-start.14
  229.5 1.1 collective-permute-done.15.refs_1_
  230.6 1.2 collective-permute-done.14.refs_0_
  231.8 3.5 %image.6 = (f32[9,40,128]{2,1,0:T(8,128)S(1)}, f32[20,40,128]{2,1,0:T(8,128)S(1)}, f32[1,384]{1,0:T(1,128)S(1)}) custom-call(f32[8,40,128]{2,1,0:T(8,128)S(1)} %pad_maximum_fusion.5.centre, f32[8,40,128]{2,1,0:T(8,128)S(1)} %collective-permute-done.14.refs_0_, f32[8,40,128]{2,1,0:T(8,128)S(1)} %collective-permute-done.15.refs_1_, ...), custom_call_target="tpu_custom_call" | custom-call | tf_op jit(solution)/shard_map/image/pallas_call | solution.py:593
  235.7 32.6 %all_to_all.50 = f32[256,1,640]{2,1,0:T(1,128)S(1)} all-to-all(f32[256,1,640]{2,1,0:T(1,128)S(1)} %broadcast_in_dim.29), channel_id=1, replica_groups=mesh['gx'=8,'gy_0'=4,'gy_1'=2,'gz'=4] {'gx','gy_0','gy_1','gz'}, dimensions={0} | all-to-all | bytes 1310720 | tf_op jit(solution)/shard_map/all_to_all | solution.py:659
  268.3 7.0 %step.5 = (f32[8,128]{1,0:T(8,128)S(1)}, f32[2,20,40,128]{3,2,1,0:T(8,128)S(1)}, f32[2,9,40,128]{3,2,1,0:T(8,128)S(1)}, f32[8,16,128]{2,1,0:T(8,128)S(1)}, f32[1,256]{1,0:T(1,128)}, /*index=5*/f32[256,256]{1,0:T(8,128)}) custom-call(s32[2]{0:T(128)S(1)} %pad_add_fusion.pos, f32[256,640]{1,0:T(8,128)S(1)} %bitcast.46, ...), custom_call_target="tpu_custom_call", output_to_operand_aliasing={{1}: (6, {}), {2}: (7, {})} | custom-call | tf_op jit(solution)/shard_map/step/pallas_call | solution.py:593
  275.3 1.9 collective-permute-start.19
  277.2 3.6 %collective-permute-start.18 = (f32[1,16,128]{2,1,0:T(8,128)S(1)}, f32[1,16,128]{2,1,0:T(8,128)S(1)}, u32[]{:S(2)}, u32[]{:S(2)}) collective-permute-start(f32[1,16,128]{2,1,0:T(8,128)S(1)} %slice.90), channel_id=1, source_target_pairs={{0,4},{32,36},{64,68},{96,100},{128,132},{160,164},{192,196},{224,... | collective-permute-start | bytes 24584 | tf_op jit(solution)/shard_map/ppermute | solution.py:640
  280.9 1.3 collective-permute-start.17
  282.2 4.0 %collective-permute-start.16 = (f32[8,8,128]{2,1,0:T(8,128)S(1)}, f32[8,8,128]{2,1,0:T(8,128)S(1)}, u32[]{:S(2)}, u32[]{:S(2)}) collective-permute-start(f32[8,8,128]{2,1,0:T(8,128)S(1)} %get-tuple-element.103), channel_id=1, source_target_pairs={{0,32},{32,64},{64,96},{96,128},{128,160},{160,192},{192,224},{224... | collective-permute-start | bytes 98312 | tf_op jit(solution)/shard_map/ppermute | solution.py:644
  286.4 0.8 collective-permute-done.16.refs_0_
  287.7 22.5 %all_to_all.51 = f32[256,1,128]{2,1,0:T(1,128)S(1)} all-to-all(f32[256,1,128]{2,1,0:T(1,128)S(1)} %broadcast_in_dim.30), channel_id=1, replica_groups=mesh['gx'=8,'gy_0'=4,'gy_1'=2,'gz'=4] {'gx','gy_0','gy_1','gz'}, dimensions={0} | all-to-all | bytes 262144 | tf_op jit(solution)/shard_map/all_to_all | solution.py:659
  310.2 2.8 finish.1
  313.3 0.8 broadcast_in_dim.31
  314.1 10.1 %all_to_all.52 = f32[8,8,512]{2,1,0:T(8,128)S(1)} all-to-all(f32[8,8,512]{2,1,0:T(8,128)S(1)} %bitcast.61), channel_id=1, replica_groups=mesh['gx'=8,'gy_0'=4,'gy_1'=2,'gz'=4] {'gx'}, dimensions={0} | all-to-all | bytes 262144 | tf_op jit(solution)/shard_map/all_to_all | solution.py:727
  324.3 7.3 %all-to-all-start.8 = ((f32[256,1,256]{2,1,0:T(1,128)}), f32[256,1,256]{2,1,0:T(1,128)S(1)}, u32[]{:S(2)}, u32[]{:S(2)}) async-start(f32[256,1,256]{2,1,0:T(1,128)} %broadcast_in_dim.31), calls=%async_computation.8 | async-start | bytes 524288 | tf_op jit(solution)/shard_map/all_to_all | solution.py:726
  332.4 0.8 squeeze.23
  333.5 0.8 squeeze.22
  334.3 12.6 %all-to-all-done.8 = f32[256,1,256]{2,1,0:T(1,128)S(1)} async-done(((f32[256,1,256]{2,1,0:T(1,128)}), f32[256,1,256]{2,1,0:T(1,128)S(1)}, u32[]{:S(2)}, u32[]{:S(2)}) %all-to-all-start.8) | async-done | bytes 262176 | tf_op jit(solution)/shard_map/all_to_all | solution.py:726
  (105 shorter events, 9.5 us)
Async XLA Ops:
  0.6 1.2 copy-start.17
  1.7 0.8 copy-start.18
  21.7 17.9 %copy-start.19 = (s32[4]{0:T(128)S(1)}, s32[4]{0:T(128)}, u32[]{:S(2)}) copy-start(s32[4]{0:T(128)} %param.7) | copy-start | bytes 52
  21.9 4.5 %collective-permute-start = (f32[3,8,16,128]{3,2,1,0:T(8,128)S(1)}, f32[3,8,16,128]{3,2,1,0:T(8,128)S(1)}, u32[]{:S(2)}, u32[]{:S(2)}) collective-permute-start(f32[3,8,16,128]{3,2,1,0:T(8,128)S(1)} %pad_maximum_fusion.2), channel_id=1, source_target_pairs={{0,32},{32,64},{64,96},{96,128},{128,160},{160,192},{192,224},{224... | collective-permute-start | bytes 589832 | tf_op jit(solution)/shard_map/ppermute | solution.py:634
  23.8 6.4 %collective-permute-start.1 = (f32[3,8,16,128]{3,2,1,0:T(8,128)S(1)}, f32[3,8,16,128]{3,2,1,0:T(8,128)S(1)}, u32[]{:S(2)}, u32[]{:S(2)}) collective-permute-start(f32[3,8,16,128]{3,2,1,0:T(8,128)S(1)} %pad_maximum_fusion.2), channel_id=1, source_target_pairs={{32,0},{64,32},{96,64},{128,96},{160,128},{192,160},{224,192},{225... | collective-permute-start | bytes 589832 | tf_op jit(solution)/shard_map/ppermute | solution.py:635
  30.3 13.8 %collective-permute-start.3 = (f32[3,8,40,128]{3,2,1,0:T(8,128)S(1)}, f32[3,8,40,128]{3,2,1,0:T(8,128)S(1)}, u32[]{:S(2)}, u32[]{:S(2)}) collective-permute-start(f32[3,8,40,128]{3,2,1,0:T(8,128)S(1)} %pad_maximum_fusion), channel_id=1, source_target_pairs={{4,0},{36,32},{68,64},{100,96},{132,128},{164,160},{196,192},{228,... | collective-permute-start | bytes 1474568 | tf_op jit(solution)/shard_map/ppermute | solution.py:640
  36.4 8.9 %collective-permute-start.2 = (f32[3,8,40,128]{3,2,1,0:T(8,128)S(1)}, f32[3,8,40,128]{3,2,1,0:T(8,128)S(1)}, u32[]{:S(2)}, u32[]{:S(2)}) collective-permute-start(f32[3,8,40,128]{3,2,1,0:T(8,128)S(1)} %pad_maximum_fusion), channel_id=1, source_target_pairs={{0,4},{32,36},{64,68},{96,100},{128,132},{160,164},{192,196},{224,... | collective-permute-start | bytes 1474568 | tf_op jit(solution)/shard_map/ppermute | solution.py:640
  52.4 0.9 copy-start
  53.3 0.9 copy-start.5
  54.2 0.8 copy-start.7
  55.0 0.8 copy-start.9
  96.9 1.1 copy-start.6
  96.9 1.2 copy-start.10
  98.1 19.0 %copy-start.1 = (f32[2,20,40,128]{3,2,1,0:T(8,128)S(1)}, f32[2,20,40,128]{3,2,1,0:T(8,128)}, u32[]{:S(2)}) copy-start(f32[2,20,40,128]{3,2,1,0:T(8,128)} %copy-done) | copy-start | bytes 2457604
  101.9 18.8 %copy-start.3 = (f32[5,256,256]{2,1,0:T(8,128)}, f32[5,256,256]{2,1,0:T(8,128)S(1)}, u32[]{:S(2)}) copy-start(f32[5,256,256]{2,1,0:T(8,128)S(1)} %get-tuple-element.63.refs_2_.refs_3_) | copy-start | bytes 3932164
  101.9 18.8 %copy-start.13 = (f32[256,256]{1,0:T(8,128)}, f32[256,256]{1,0:T(8,128)S(1)}, u32[]{:S(2)}) copy-start(f32[256,256]{1,0:T(8,128)S(1)} %get-tuple-element.62.b2_was) | copy-start | bytes 786436
  101.9 3.5 %collective-permute-start.4 = (f32[8,16,128]{2,1,0:T(8,128)S(1)}, f32[8,16,128]{2,1,0:T(8,128)S(1)}, u32[]{:S(2)}, u32[]{:S(2)}) collective-permute-start(f32[8,16,128]{2,1,0:T(8,128)S(1)} %get-tuple-element.57), channel_id=1, source_target_pairs={{0,32},{32,64},{64,96},{96,128},{128,160},{160,192},{192,224},{224... | collective-permute-start | bytes 196616 | tf_op jit(solution)/shard_map/ppermute | solution.py:634
  104.1 5.0 %collective-permute-start.5 = (f32[8,16,128]{2,1,0:T(8,128)S(1)}, f32[8,16,128]{2,1,0:T(8,128)S(1)}, u32[]{:S(2)}, u32[]{:S(2)}) collective-permute-start(f32[8,16,128]{2,1,0:T(8,128)S(1)} %get-tuple-element.57), channel_id=1, source_target_pairs={{32,0},{64,32},{96,64},{128,96},{160,128},{192,160},{224,192},{225... | collective-permute-start | bytes 196616 | tf_op jit(solution)/shard_map/ppermute | solution.py:635
  109.2 6.8 %collective-permute-start.7 = (f32[8,40,128]{2,1,0:T(8,128)S(1)}, f32[8,40,128]{2,1,0:T(8,128)S(1)}, u32[]{:S(2)}, u32[]{:S(2)}) collective-permute-start(f32[8,40,128]{2,1,0:T(8,128)S(1)} %pad_maximum_fusion.3.centre), channel_id=1, source_target_pairs={{4,0},{36,32},{68,64},{100,96},{132,128},{164,160},{196,192},{228,... | collective-permute-start | bytes 491528 | tf_op jit(solution)/shard_map/ppermute | solution.py:640
  112.7 4.4 %collective-permute-start.6 = (f32[8,40,128]{2,1,0:T(8,128)S(1)}, f32[8,40,128]{2,1,0:T(8,128)S(1)}, u32[]{:S(2)}, u32[]{:S(2)}) collective-permute-start(f32[8,40,128]{2,1,0:T(8,128)S(1)} %pad_maximum_fusion.3.centre), channel_id=1, source_target_pairs={{0,4},{32,36},{64,68},{96,100},{128,132},{160,164},{192,196},{224,... | collective-permute-start | bytes 491528 | tf_op jit(solution)/shard_map/ppermute | solution.py:640
  120.7 0.8 copy-start.11
  121.5 0.7 copy-start.15
  122.2 27.2 %copy-start.2 = (f32[2,20,40,128]{3,2,1,0:T(8,128)S(1)}, f32[2,20,40,128]{3,2,1,0:T(8,128)}, u32[]{:S(2)}) copy-start(f32[2,20,40,128]{3,2,1,0:T(8,128)} %copy-done) | copy-start | bytes 2457604
  122.2 27.2 %copy-start.12 = (f32[20,40,128]{2,1,0:T(8,128)S(1)}, f32[20,40,128]{2,1,0:T(8,128)}, u32[]{:S(2)}) copy-start(f32[20,40,128]{2,1,0:T(8,128)} %copy-done.11) | copy-start | bytes 1228804
  122.2 27.2 %copy-start.14 = (f32[256,256]{1,0:T(8,128)S(1)}, f32[256,256]{1,0:T(8,128)}, u32[]{:S(2)}) copy-start(f32[256,256]{1,0:T(8,128)} %copy-done.13) | copy-start | bytes 786436
  122.2 27.2 %copy-start.16 = (f32[9,40,128]{2,1,0:T(8,128)S(1)}, f32[9,40,128]{2,1,0:T(8,128)}, u32[]{:S(2)}) copy-start(f32[9,40,128]{2,1,0:T(8,128)} %copy-done.15) | copy-start | bytes 552964
  149.4 1.3 copy-start.4
  156.8 3.9 %collective-permute-start.8 = (f32[8,16,128]{2,1,0:T(8,128)S(1)}, f32[8,16,128]{2,1,0:T(8,128)S(1)}, u32[]{:S(2)}, u32[]{:S(2)}) collective-permute-start(f32[8,16,128]{2,1,0:T(8,128)S(1)} %get-tuple-element.65), channel_id=1, source_target_pairs={{0,32},{32,64},{64,96},{96,128},{128,160},{160,192},{192,224},{224... | collective-permute-start | bytes 196616 | tf_op jit(solution)/shard_map/ppermute | solution.py:634
  159.4 5.0 %collective-permute-start.9 = (f32[8,16,128]{2,1,0:T(8,128)S(1)}, f32[8,16,128]{2,1,0:T(8,128)S(1)}, u32[]{:S(2)}, u32[]{:S(2)}) collective-permute-start(f32[8,16,128]{2,1,0:T(8,128)S(1)} %get-tuple-element.65), channel_id=1, source_target_pairs={{32,0},{64,32},{96,64},{128,96},{160,128},{192,160},{224,192},{225... | collective-permute-start | bytes 196616 | tf_op jit(solution)/shard_map/ppermute | solution.py:635
  164.4 7.2 %collective-permute-start.11 = (f32[8,40,128]{2,1,0:T(8,128)S(1)}, f32[8,40,128]{2,1,0:T(8,128)S(1)}, u32[]{:S(2)}, u32[]{:S(2)}) collective-permute-start(f32[8,40,128]{2,1,0:T(8,128)S(1)} %pad_maximum_fusion.4.centre), channel_id=1, source_target_pairs={{4,0},{36,32},{68,64},{100,96},{132,128},{164,160},{196,192},{228,... | collective-permute-start | bytes 491528 | tf_op jit(solution)/shard_map/ppermute | solution.py:640
  168.6 4.2 %collective-permute-start.10 = (f32[8,40,128]{2,1,0:T(8,128)S(1)}, f32[8,40,128]{2,1,0:T(8,128)S(1)}, u32[]{:S(2)}, u32[]{:S(2)}) collective-permute-start(f32[8,40,128]{2,1,0:T(8,128)S(1)} %pad_maximum_fusion.4.centre), channel_id=1, source_target_pairs={{0,4},{32,36},{64,68},{96,100},{128,132},{160,164},{192,196},{224,... | collective-permute-start | bytes 491528 | tf_op jit(solution)/shard_map/ppermute | solution.py:640
  215.5 4.2 %collective-permute-start.12 = (f32[8,16,128]{2,1,0:T(8,128)S(1)}, f32[8,16,128]{2,1,0:T(8,128)S(1)}, u32[]{:S(2)}, u32[]{:S(2)}) collective-permute-start(f32[8,16,128]{2,1,0:T(8,128)S(1)} %get-tuple-element.74), channel_id=1, source_target_pairs={{0,32},{32,64},{64,96},{96,128},{128,160},{160,192},{192,224},{224... | collective-permute-start | bytes 196616 | tf_op jit(solution)/shard_map/ppermute | solution.py:634
  218.4 5.0 %collective-permute-start.13 = (f32[8,16,128]{2,1,0:T(8,128)S(1)}, f32[8,16,128]{2,1,0:T(8,128)S(1)}, u32[]{:S(2)}, u32[]{:S(2)}) collective-permute-start(f32[8,16,128]{2,1,0:T(8,128)S(1)} %get-tuple-element.74), channel_id=1, source_target_pairs={{32,0},{64,32},{96,64},{128,96},{160,128},{192,160},{224,192},{225... | collective-permute-start | bytes 196616 | tf_op jit(solution)/shard_map/ppermute | solution.py:635
  223.5 7.1 %collective-permute-start.15 = (f32[8,40,128]{2,1,0:T(8,128)S(1)}, f32[8,40,128]{2,1,0:T(8,128)S(1)}, u32[]{:S(2)}, u32[]{:S(2)}) collective-permute-start(f32[8,40,128]{2,1,0:T(8,128)S(1)} %pad_maximum_fusion.5.centre), channel_id=1, source_target_pairs={{4,0},{36,32},{68,64},{100,96},{132,128},{164,160},{196,192},{228,... | collective-permute-start | bytes 491528 | tf_op jit(solution)/shard_map/ppermute | solution.py:640
  227.2 4.6 %collective-permute-start.14 = (f32[8,40,128]{2,1,0:T(8,128)S(1)}, f32[8,40,128]{2,1,0:T(8,128)S(1)}, u32[]{:S(2)}, u32[]{:S(2)}) collective-permute-start(f32[8,40,128]{2,1,0:T(8,128)S(1)} %pad_maximum_fusion.5.centre), channel_id=1, source_target_pairs={{0,4},{32,36},{64,68},{96,100},{128,132},{160,164},{192,196},{224,... | collective-permute-start | bytes 491528 | tf_op jit(solution)/shard_map/ppermute | solution.py:640
  275.3 11.0 %collective-permute-start.19 = (f32[1,16,128]{2,1,0:T(8,128)S(1)}, f32[1,16,128]{2,1,0:T(8,128)S(1)}, u32[]{:S(2)}, u32[]{:S(2)}) collective-permute-start(f32[1,16,128]{2,1,0:T(8,128)S(1)} %slice.90), channel_id=1, source_target_pairs={{4,0},{36,32},{68,64},{100,96},{132,128},{164,160},{196,192},{228,... | collective-permute-start | bytes 24584 | tf_op jit(solution)/shard_map/ppermute | solution.py:640
  277.2 9.0 %collective-permute-start.18 = (f32[1,16,128]{2,1,0:T(8,128)S(1)}, f32[1,16,128]{2,1,0:T(8,128)S(1)}, u32[]{:S(2)}, u32[]{:S(2)}) collective-permute-start(f32[1,16,128]{2,1,0:T(8,128)S(1)} %slice.90), channel_id=1, source_target_pairs={{0,4},{32,36},{64,68},{96,100},{128,132},{160,164},{192,196},{224,... | collective-permute-start | bytes 24584 | tf_op jit(solution)/shard_map/ppermute | solution.py:640
  280.9 5.5 %collective-permute-start.17 = (f32[8,8,128]{2,1,0:T(8,128)S(1)}, f32[8,8,128]{2,1,0:T(8,128)S(1)}, u32[]{:S(2)}, u32[]{:S(2)}) collective-permute-start(f32[8,8,128]{2,1,0:T(8,128)S(1)} %get-tuple-element.102), channel_id=1, source_target_pairs={{32,0},{64,32},{96,64},{128,96},{160,128},{192,160},{224,192},{225... | collective-permute-start | bytes 98312 | tf_op jit(solution)/shard_map/ppermute | solution.py:645
  282.2 5.0 %collective-permute-start.16 = (f32[8,8,128]{2,1,0:T(8,128)S(1)}, f32[8,8,128]{2,1,0:T(8,128)S(1)}, u32[]{:S(2)}, u32[]{:S(2)}) collective-permute-start(f32[8,8,128]{2,1,0:T(8,128)S(1)} %get-tuple-element.103), channel_id=1, source_target_pairs={{0,32},{32,64},{64,96},{96,128},{128,160},{160,192},{192,224},{224... | collective-permute-start | bytes 98312 | tf_op jit(solution)/shard_map/ppermute | solution.py:644
  287.2 23.0 %copy-start.8 = (f32[3,9,40,128]{3,2,1,0:T(8,128)S(1)}, f32[3,9,40,128]{3,2,1,0:T(8,128)}, u32[]{:S(2)}) copy-start(f32[3,9,40,128]{3,2,1,0:T(8,128)} %copy-done.7) | copy-start | bytes 1658884
  324.3 22.7 %all-to-all-start.8 = ((f32[256,1,256]{2,1,0:T(1,128)}), f32[256,1,256]{2,1,0:T(1,128)S(1)}, u32[]{:S(2)}, u32[]{:S(2)}) async-start(f32[256,1,256]{2,1,0:T(1,128)} %broadcast_in_dim.31), calls=%async_computation.8 | async-start | bytes 524288 | tf_op jit(solution)/shard_map/all_to_all | solution.py:726

commit v4 on v3

--- a/solution.py
+++ b/solution.py
@@ -172,7 +172,7 @@
     smooth_down(fine, 3, H, r, r1, u1, x, r2)
     rows(2, H // 2, lambda y, c: (c, [(b1, y, sum_x(sum_z(r2[2 * y] + r2[2 * y + 1], 1), 1))]), 0)
     smooth_down(mid, 3, H // 2, b1, r1m, u1m, xm, r2m)
-    return to_line([sum_x(sum_z(r2m[2 * k + 6] + r2m[2 * k + 7], 2), 2) for k in range(2)])
+    return [sum_x(sum_z(r2m[2 * k + 6] + r2m[2 * k + 7], 2), 2) for k in range(2)]
 
 
 def to_line(folded):
@@ -259,7 +259,7 @@
 
     rows(0, H // 2, row1, zero, 2)
 
-    pay[:, 0:256] = down(fine, mid, r, *cycle_of(cycle, cycle1), *scratch)
+    pay[:, 0:256] = to_line(down(fine, mid, r, *cycle_of(cycle, cycle1), *scratch))
     pair = [(2 * k + 6, 2 * k + 7) for k in range(2)]
     pay[:, 256:512] = to_line([sum_z(odd_x(wx1[a] + wx1[b], 2), 2) for a, b in pair])
     half = lane < NX
@@ -485,7 +485,7 @@
     pay[:, 0:128] = jnp.where(lane == 0, jnp.sum(a), jnp.where(lane == 1, jnp.sum(b), 0.0))
     if not last:
         cycle, cycle1 = scratch[:2]
-        pay[:, 128:384] = down(fine, mid, w, *cycle_of(cycle, cycle1), *scratch[2:])
+        pay[:, 128:384] = to_line(down(fine, mid, w, *cycle_of(cycle, cycle1), *scratch[2:]))
 
 
 def step_sizes(got, old, scal, first):
@@ -510,9 +510,12 @@
     return alpha, beta
 
 
-def step_kernel(first, pos, got, old, z, w, b2_was, rq, *refs):
+def step_kernel(first, again, pos, got, old, z, w, b2_was, rq, *refs):
     pd, refs = (None, refs) if first else (refs[0], refs[1:])
-    coef, coef1, k2, k3, scal, rq_o, pd_o, out, pay, b2q, b2t, cycle, cycle1, e2, *scratch = refs
+    coef, coef1, k2, k3, scal, rq_o, pd_o, out, b2, *refs = refs
+    (pay, refs) = (refs[0], refs[1:]) if first else (None, refs)
+    cycle, cycle1, e2, *scratch = refs
+    b2q, b2t = b2.at[0], b2.at[1]
     fine, mid = levels_of(coef, coef1)
     alpha, beta = step_sizes(got, old, scal, first)
 
@@ -528,15 +531,17 @@
 
     rows(0, 9, row_d, 0)
     x, r2, xm, r2m = cycle_of(cycle, cycle1)
-    pay[...] = down(fine, mid, rq_o.at[0], x, r2, xm, r2m, *scratch)
+    folded = down(fine, mid, rq_o.at[0], x, r2, xm, r2m, *scratch)
+    if first:
+        pay[...] = to_line(folded)
     alpha2 = jnp.concatenate([alpha, alpha], axis=1)
     if first:
         b2q[...] = got[:, 128:384].T
         b2t[...] = b2_was[...] - alpha2 * b2q[...]
     else:
         beta2 = jnp.concatenate([beta, beta], axis=1)
-        b2q[...] = got[:, 128:384].T + beta2 * b2_was[...]
-        b2t[...] = got[:, 384:640].T - alpha2 * b2q[...]
+        b2q[...] = got[:, 128:384].T + beta2 * b2_was[0]
+        b2t[...] = (got[:, 384:640].T if again else b2_was[1]) - alpha2 * b2q[...]
     up(pos, k2, k3, b2t, fine, mid, x, r2, xm, r2m, out, e2, *scratch)
 
 
@@ -706,15 +711,19 @@
         )(*around, rq, coef, coef1)
         if last:
             break
-        if not first:
+        if i == 1:
             line = jnp.concatenate([line, pay], axis=1)
+        else:
+            line = jnp.pad(line, ((0, 0), (0, 128)))
         got = to_everyone(line)[:, 0]
         state = (rq,) if first else (rq, pd)
-        scal, rq, pd, z, pay, b2 = call(
-            functools.partial(step_kernel, first), 1,
-            [(8, 128), (2, *FINE), (2, *KEPT), own, (1, 256), PLANES], [PLANES] + CYCLE + [COARSE] + SCRATCH, "step",
-            {6: 1} if first else {6: 1, 7: 2},
+        scal, rq, pd, z, b2, *rest = call(
+            functools.partial(step_kernel, first, i == 1), 1,
+            [(8, 128), (2, *FINE), (2, *KEPT), own, (2, *PLANES)] + ([(1, 256)] if first else []),
+            CYCLE + [COARSE] + SCRATCH, "step", {6: 1} if first else {6: 1, 7: 2},
         )(pos, got, scal, z, w, b2, *state, coef, coef1, k2, k3)
+        if first:
+            (pay,) = rest
     dots = to_everyone(line)[:, 0]
     d_own, r_own, layers = call(finish_kernel, 2, [own, own, (TRIALS, 8, 128)], [KEPT], "finish")(
         pos, steps, dots, scal, z, w, rq, pd, kept

time: 350 us -> 346 us (0.989)
  local copies, waits for them, and re-layouts: 16.6 us -> 13 us
    unnamed x44 -> x22, local copies, waits for them, and re-layouts: 7.51 us -> 3.9 us
where the time goes in v4:
time: 346 us; the launch traced here: 345 us
  blocking collectives  183 us (53%)
  starting transfers between devices  60.1 us (17%)
  Pallas kernels  43 us (12%)
  waiting for transfers between devices  42 us (12%)
  local copies, waits for them, and re-layouts  13 us (4%)
    all_to_all x4, blocking collectives, to_everyone(): return lax.all_to_all(copies, ALL, split_axis=0, concat_axis=0, tiled=True)  115 us
    pallas_call x10, Pallas kernels, run(): pl.pallas_call(kernel, in_specs=[SM] * n_scalar + [VM] * (len(args) - n_s...  43 us
    all_to_all x1, blocking collectives, to_everyone_by_axes(): lax.all_to_all(copies, (*GY, 'gz'), split_axis=0, concat_axis=0, tiled=True)  31.1 us
    ppermute x5, starting transfers between devices, exchange_y(): lax.ppermute(own, ALL, shift_pairs(-1, 0))  19.1 us
    all_to_all x1, blocking collectives, on_device(): lax.all_to_all(fields, 'gx', split_axis=0, concat_axis=0, tiled=True)  17.8 us
    ppermute x4, waiting for transfers between devices, exchange_z(): high = lax.ppermute(own, ALL, shift_pairs(0, -1))  14.9 us
    ppermute x5, starting transfers between devices, exchange_y(): lax.ppermute(own, ALL, shift_pairs(1, 0))  13.4 us
    all_to_all x1, waiting for transfers between devices, on_device(): lax.all_to_all(copies, ALL, split_axis=0, concat_axis=0, tiled=True)  12.6 us
  transfers between devices with their start and end apart: 21, of which 15 were waited for; matrix products, arithmetic and copies ran while one was open for 1% of the time, Pallas kernels for 0%

profile of v4, /device:TPU:1, one launch (start us, length us, event | category | flops | bytes accessed | tf_op | source)
XLA Modules:
  0.0 345.0 jit_solution(14691341367629253228)
XLA Ops:
  0.7 1.1 stack.33
  3.0 0.7 reshape.56
  3.7 17.8 %all_to_all.45 = f32[8,8,3,256]{3,1,2,0:T(8,128)S(1)} all-to-all(f32[8,8,3,256]{3,1,2,0:T(8,128)S(1)} %reverse_select_fusion), channel_id=1, replica_groups=mesh['gx'=8,'gy_0'=4,'gy_1'=2,'gz'=4] {'gx'}, dimensions={0} | all-to-all | bytes 393216 | tf_op jit(solution)/shard_map/all_to_all | solution.py:687
  21.9 1.9 collective-permute-start
  23.8 1.3 collective-permute-start.1
  25.1 1.3 collective-permute-done
  26.4 3.8 %collective-permute-done.1 = f32[3,8,16,128]{3,2,1,0:T(8,128)S(1)} collective-permute-done((f32[3,8,16,128]{3,2,1,0:T(8,128)S(1)}, f32[3,8,16,128]{3,2,1,0:T(8,128)S(1)}, u32[]{:S(2)}, u32[]{:S(2)}) %collective-permute-start.1) | collective-permute-done | bytes 196640 | tf_op jit(solution)/shard_map/ppermute | solution.py:640
  30.3 6.1 %collective-permute-start.3 = (f32[3,8,40,128]{3,2,1,0:T(8,128)S(1)}, f32[3,8,40,128]{3,2,1,0:T(8,128)S(1)}, u32[]{:S(2)}, u32[]{:S(2)}) collective-permute-start(f32[3,8,40,128]{3,2,1,0:T(8,128)S(1)} %pad_maximum_fusion), channel_id=1, source_target_pairs={{4,0},{36,32},{68,64},{100,96},{132,128},{164,160},{196,192},{228,... | collective-permute-start | bytes 1474568 | tf_op jit(solution)/shard_map/ppermute | solution.py:645
  36.4 3.1 collective-permute-start.2
  39.7 4.5 %collective-permute-done.3 = f32[3,8,40,128]{3,2,1,0:T(8,128)S(1)} collective-permute-done((f32[3,8,40,128]{3,2,1,0:T(8,128)S(1)}, f32[3,8,40,128]{3,2,1,0:T(8,128)S(1)}, u32[]{:S(2)}, u32[]{:S(2)}) %collective-permute-start.3) | collective-permute-done | bytes 491552 | tf_op jit(solution)/shard_map/ppermute | solution.py:645
  44.2 1.1 collective-permute-done.2
  46.0 6.4 %setup.1 = (f32[5,20,40,128]{3,2,1,0:T(8,128)S(1)}, f32[5,10,40,128]{3,2,1,0:T(8,128)S(1)}, f32[2,20,40,128]{3,2,1,0:T(8,128)S(1)}, f32[2,20,40,128]{3,2,1,0:T(8...) custom-call(s32[2]{0:T(128)S(1)} %pad_add_fusion.pos, ...), custom_call_target="tpu_custom_call" | custom-call | tf_op jit(solution)/shard_map/setup/pallas_call | solution.py:598
  52.4 0.9 copy-done
  53.3 0.9 copy-done.2
  54.2 0.8 copy-done.4
  55.1 9.9 %all_to_all.46 = f32[8,1,1280]{2,1,0:T(1,128)S(1)} all-to-all(f32[8,1,1280]{2,1,0:T(1,128)S(1)} %broadcast_in_dim.24), channel_id=1, replica_groups=mesh['gx'=8,'gy_0'=4,'gy_1'=2,'gz'=4] {'gx'}, dimensions={0} | all-to-all | bytes 81920 | tf_op jit(solution)/shard_map/all_to_all | solution.py:670
  65.0 31.1 %all_to_all.47 = f32[32,8,1280]{2,1,0:T(8,128)S(1)} all-to-all(f32[32,8,1280]{2,1,0:T(8,128)S(1)} %broadcast_in_dim.25), channel_id=1, replica_groups=mesh['gx'=8,'gy_0'=4,'gy_1'=2,'gz'=4] {'gy_0','gy_1','gz'}, dimensions={0} | all-to-all | bytes 2621440 | tf_op jit(solution)/shard_map/all_to_all | solution.py:672
  96.6 0.7 copy-done.3
  97.3 3.9 %first.1 = (f32[8,16,128]{2,1,0:T(8,128)S(1)}, f32[5,256,256]{2,1,0:T(8,128)S(1)}, f32[5,64,256]{2,1,0:T(8,128)S(1)}, f32[256,256]{1,0:T(8,128)S(1)}) custom-call(s32[2]{0:T(128)S(1)} %pad_add_fusion.pos, f32[256,1280]{1,0:T(8,128)S(1)} %bitcast.47, f32[5,20,40,128]{3,2,1,0:T(8,128)S(1)} %get-tuple-element.52.coef.refs_3_.refs_0_.refs_1_.refs_4_, ...), custom_call_target="tpu_custom_call" | custom-call | tf_op jit(solution)/shard_map/first/pallas_call | solution.py:598
  101.2 2.2 collective-permute-start.4
  103.4 1.3 collective-permute-start.5
  104.7 3.7 %collective-permute-done.5 = f32[8,16,128]{2,1,0:T(8,128)S(1)} collective-permute-done((f32[8,16,128]{2,1,0:T(8,128)S(1)}, f32[8,16,128]{2,1,0:T(8,128)S(1)}, u32[]{:S(2)}, u32[]{:S(2)}) %collective-permute-start.5) | collective-permute-done | bytes 65568 | tf_op jit(solution)/shard_map/ppermute | solution.py:640
  108.4 3.6 %collective-permute-start.7 = (f32[8,40,128]{2,1,0:T(8,128)S(1)}, f32[8,40,128]{2,1,0:T(8,128)S(1)}, u32[]{:S(2)}, u32[]{:S(2)}) collective-permute-start(f32[8,40,128]{2,1,0:T(8,128)S(1)} %pad_maximum_fusion.3.centre), channel_id=1, source_target_pairs={{4,0},{36,32},{68,64},{100,96},{132,128},{164,160},{196,192},{228,... | collective-permute-start | bytes 491528 | tf_op jit(solution)/shard_map/ppermute | solution.py:645
  112.0 2.2 collective-permute-start.6
  114.2 1.1 collective-permute-done.7.refs_1_
  115.2 1.2 collective-permute-done.6.refs_0_
  116.4 3.5 %image.4 = (f32[9,40,128]{2,1,0:T(8,128)S(1)}, f32[20,40,128]{2,1,0:T(8,128)S(1)}, f32[1,384]{1,0:T(1,128)S(1)}) custom-call(f32[8,40,128]{2,1,0:T(8,128)S(1)} %pad_maximum_fusion.3.centre, f32[8,40,128]{2,1,0:T(8,128)S(1)} %collective-permute-done.6.refs_0_, f32[8,40,128]{2,1,0:T(8,128)S(1)} %collective-permute-done.7.refs_1_, ...), custom_call_target="tpu_custom_call" | custom-call | tf_op jit(solution)/shard_map/image/pallas_call | solution.py:598
  120.2 29.5 %all_to_all.48 = f32[256,1,512]{2,1,0:T(1,128)S(1)} all-to-all(f32[256,1,512]{2,1,0:T(1,128)S(1)} %broadcast_in_dim.26), channel_id=1, replica_groups=mesh['gx'=8,'gy_0'=4,'gy_1'=2,'gz'=4] {'gx','gy_0','gy_1','gz'}, dimensions={0} | all-to-all | bytes 1048576 | tf_op jit(solution)/shard_map/all_to_all | solution.py:664
  149.8 6.1 %step.3 = (f32[8,128]{1,0:T(8,128)S(1)}, f32[2,20,40,128]{3,2,1,0:T(8,128)S(1)}, f32[2,9,40,128]{3,2,1,0:T(8,128)S(1)}, f32[8,16,128]{2,1,0:T(8,128)S(1)}, f32[2...) custom-call(s32[2]{0:T(128)S(1)} %pad_add_fusion.pos, f32[256,512]{1,0:T(8,128)S(1)} %bitcast.50, ...), custom_call_target="tpu_custom_call", output_to_operand_aliasing={{1}: (6, {})} | custom-call | tf_op jit(solution)/shard_map/step/pallas_call | solution.py:598
  155.8 2.9 collective-permute-start.8
  158.8 1.3 collective-permute-start.9
  160.1 3.7 %collective-permute-done.9 = f32[8,16,128]{2,1,0:T(8,128)S(1)} collective-permute-done((f32[8,16,128]{2,1,0:T(8,128)S(1)}, f32[8,16,128]{2,1,0:T(8,128)S(1)}, u32[]{:S(2)}, u32[]{:S(2)}) %collective-permute-start.9) | collective-permute-done | bytes 65568 | tf_op jit(solution)/shard_map/ppermute | solution.py:640
  163.8 3.8 %collective-permute-start.11 = (f32[8,40,128]{2,1,0:T(8,128)S(1)}, f32[8,40,128]{2,1,0:T(8,128)S(1)}, u32[]{:S(2)}, u32[]{:S(2)}) collective-permute-start(f32[8,40,128]{2,1,0:T(8,128)S(1)} %pad_maximum_fusion.4.centre), channel_id=1, source_target_pairs={{4,0},{36,32},{68,64},{100,96},{132,128},{164,160},{196,192},{228,... | collective-permute-start | bytes 491528 | tf_op jit(solution)/shard_map/ppermute | solution.py:645
  167.7 2.2 collective-permute-start.10
  169.8 1.1 collective-permute-done.11.refs_1_
  170.9 1.2 collective-permute-done.10.refs_0_
  172.1 3.5 %image.5 = (f32[9,40,128]{2,1,0:T(8,128)S(1)}, f32[20,40,128]{2,1,0:T(8,128)S(1)}, f32[1,384]{1,0:T(1,128)S(1)}) custom-call(f32[8,40,128]{2,1,0:T(8,128)S(1)} %pad_maximum_fusion.4.centre, f32[8,40,128]{2,1,0:T(8,128)S(1)} %collective-permute-done.10.refs_0_, f32[8,40,128]{2,1,0:T(8,128)S(1)} %collective-permute-done.11.refs_1_, ...), custom_call_target="tpu_custom_call" | custom-call | tf_op jit(solution)/shard_map/image/pallas_call | solution.py:598
  176.0 32.6 %all_to_all.49 = f32[256,1,640]{2,1,0:T(1,128)S(1)} all-to-all(f32[256,1,640]{2,1,0:T(1,128)S(1)} %broadcast_in_dim.28), channel_id=1, replica_groups=mesh['gx'=8,'gy_0'=4,'gy_1'=2,'gz'=4] {'gx','gy_0','gy_1','gz'}, dimensions={0} | all-to-all | bytes 1310720 | tf_op jit(solution)/shard_map/all_to_all | solution.py:664
  208.6 6.2 %step.4 = (f32[8,128]{1,0:T(8,128)S(1)}, f32[2,20,40,128]{3,2,1,0:T(8,128)S(1)}, f32[2,9,40,128]{3,2,1,0:T(8,128)S(1)}, f32[8,16,128]{2,1,0:T(8,128)S(1)}, f32[2,256,256]{2,1,0:T(8,128)S(1)}) custom-call(s32[2]{0:T(128)S(1)} %pad_add_fusion.pos, f32[256,640]{1,0:T(8,128)S(1)} %bitcast.48, ...), custom_call_target="tpu_custom_call", output_to_operand_aliasing={{1}: (6, {}), {2}: (7, {})} | custom-call | tf_op jit(solution)/shard_map/step/pallas_call | solution.py:598
  214.8 2.9 collective-permute-start.12
  217.6 1.3 collective-permute-start.13
  219.0 3.7 %collective-permute-done.13 = f32[8,16,128]{2,1,0:T(8,128)S(1)} collective-permute-done((f32[8,16,128]{2,1,0:T(8,128)S(1)}, f32[8,16,128]{2,1,0:T(8,128)S(1)}, u32[]{:S(2)}, u32[]{:S(2)}) %collective-permute-start.13) | collective-permute-done | bytes 65568 | tf_op jit(solution)/shard_map/ppermute | solution.py:640
  222.7 3.7 %collective-permute-start.15 = (f32[8,40,128]{2,1,0:T(8,128)S(1)}, f32[8,40,128]{2,1,0:T(8,128)S(1)}, u32[]{:S(2)}, u32[]{:S(2)}) collective-permute-start(f32[8,40,128]{2,1,0:T(8,128)S(1)} %pad_maximum_fusion.5.centre), channel_id=1, source_target_pairs={{4,0},{36,32},{68,64},{100,96},{132,128},{164,160},{196,192},{228,... | collective-permute-start | bytes 491528 | tf_op jit(solution)/shard_map/ppermute | solution.py:645
  226.4 2.3 collective-permute-start.14
  228.8 1.1 collective-permute-done.15.refs_1_
  229.8 1.2 collective-permute-done.14.refs_0_
  231.0 3.5 %image.6 = (f32[9,40,128]{2,1,0:T(8,128)S(1)}, f32[20,40,128]{2,1,0:T(8,128)S(1)}, f32[1,384]{1,0:T(1,128)S(1)}) custom-call(f32[8,40,128]{2,1,0:T(8,128)S(1)} %pad_maximum_fusion.5.centre, f32[8,40,128]{2,1,0:T(8,128)S(1)} %collective-permute-done.14.refs_0_, f32[8,40,128]{2,1,0:T(8,128)S(1)} %collective-permute-done.15.refs_1_, ...), custom_call_target="tpu_custom_call" | custom-call | tf_op jit(solution)/shard_map/image/pallas_call | solution.py:598
  234.8 29.8 %all_to_all.50 = f32[256,1,512]{2,1,0:T(1,128)S(1)} all-to-all(f32[256,1,512]{2,1,0:T(1,128)S(1)} %broadcast_in_dim.29), channel_id=1, replica_groups=mesh['gx'=8,'gy_0'=4,'gy_1'=2,'gz'=4] {'gx','gy_0','gy_1','gz'}, dimensions={0} | all-to-all | bytes 1048576 | tf_op jit(solution)/shard_map/all_to_all | solution.py:664
  264.6 6.8 %step.5 = (f32[8,128]{1,0:T(8,128)S(1)}, f32[2,20,40,128]{3,2,1,0:T(8,128)S(1)}, f32[2,9,40,128]{3,2,1,0:T(8,128)S(1)}, f32[8,16,128]{2,1,0:T(8,128)S(1)}, f32[2,256,256]{2,1,0:T(8,128)}) custom-call(s32[2]{0:T(128)S(1)} %pad_add_fusion.pos, f32[256,512]{1,0:T(8,128)S(1)} %bitcast.49, ...), custom_call_target="tpu_custom_call", output_to_operand_aliasing={{1}: (6, {}), {2}: (7, {})} | custom-call | tf_op jit(solution)/shard_map/step/pallas_call | solution.py:598
  271.4 1.9 collective-permute-start.19
  273.3 3.6 %collective-permute-start.18 = (f32[1,16,128]{2,1,0:T(8,128)S(1)}, f32[1,16,128]{2,1,0:T(8,128)S(1)}, u32[]{:S(2)}, u32[]{:S(2)}) collective-permute-start(f32[1,16,128]{2,1,0:T(8,128)S(1)} %slice.90), channel_id=1, source_target_pairs={{0,4},{32,36},{64,68},{96,100},{128,132},{160,164},{192,196},{224,... | collective-permute-start | bytes 24584 | tf_op jit(solution)/shard_map/ppermute | solution.py:645
  277.0 1.3 collective-permute-start.17
  278.3 4.0 %collective-permute-start.16 = (f32[8,8,128]{2,1,0:T(8,128)S(1)}, f32[8,8,128]{2,1,0:T(8,128)S(1)}, u32[]{:S(2)}, u32[]{:S(2)}) collective-permute-start(f32[8,8,128]{2,1,0:T(8,128)S(1)} %get-tuple-element.101), channel_id=1, source_target_pairs={{0,32},{32,64},{64,96},{96,128},{128,160},{160,192},{192,224},{224... | collective-permute-start | bytes 98312 | tf_op jit(solution)/shard_map/ppermute | solution.py:649
  282.5 0.8 collective-permute-done.16.refs_0_
  283.8 22.8 %all_to_all.51 = f32[256,1,128]{2,1,0:T(1,128)S(1)} all-to-all(f32[256,1,128]{2,1,0:T(1,128)S(1)} %broadcast_in_dim.30), channel_id=1, replica_groups=mesh['gx'=8,'gy_0'=4,'gy_1'=2,'gz'=4] {'gx','gy_0','gy_1','gz'}, dimensions={0} | all-to-all | bytes 262144 | tf_op jit(solution)/shard_map/all_to_all | solution.py:664
  306.5 2.8 finish.1
  309.7 0.8 broadcast_in_dim.31
  310.5 10.1 %all_to_all.52 = f32[8,8,512]{2,1,0:T(8,128)S(1)} all-to-all(f32[8,8,512]{2,1,0:T(8,128)S(1)} %bitcast.63), channel_id=1, replica_groups=mesh['gx'=8,'gy_0'=4,'gy_1'=2,'gz'=4] {'gx'}, dimensions={0} | all-to-all | bytes 262144 | tf_op jit(solution)/shard_map/all_to_all | solution.py:736
  320.6 7.3 %all-to-all-start.8 = ((f32[256,1,256]{2,1,0:T(1,128)}), f32[256,1,256]{2,1,0:T(1,128)S(1)}, u32[]{:S(2)}, u32[]{:S(2)}) async-start(f32[256,1,256]{2,1,0:T(1,128)} %broadcast_in_dim.31), calls=%async_computation.8 | async-start | bytes 524288 | tf_op jit(solution)/shard_map/all_to_all | solution.py:735
  328.7 0.8 squeeze.23
  329.9 0.8 squeeze.22
  330.7 12.6 %all-to-all-done.8 = f32[256,1,256]{2,1,0:T(1,128)S(1)} async-done(((f32[256,1,256]{2,1,0:T(1,128)}), f32[256,1,256]{2,1,0:T(1,128)S(1)}, u32[]{:S(2)}, u32[]{:S(2)}) %all-to-all-start.8) | async-done | bytes 262176 | tf_op jit(solution)/shard_map/all_to_all | solution.py:735
  343.8 0.6 constant_dynamic-slice_fusion
  344.4 0.5 broadcast_multiply_fusion.1
  (83 shorter events, 6.9 us)
Async XLA Ops:
  0.6 1.2 copy-start.6
  1.7 0.8 copy-start.7
  21.7 17.9 %copy-start.8 = (s32[4]{0:T(128)S(1)}, s32[4]{0:T(128)}, u32[]{:S(2)}) copy-start(s32[4]{0:T(128)} %param.7) | copy-start | bytes 52
  21.9 4.5 %collective-permute-start = (f32[3,8,16,128]{3,2,1,0:T(8,128)S(1)}, f32[3,8,16,128]{3,2,1,0:T(8,128)S(1)}, u32[]{:S(2)}, u32[]{:S(2)}) collective-permute-start(f32[3,8,16,128]{3,2,1,0:T(8,128)S(1)} %pad_maximum_fusion.2), channel_id=1, source_target_pairs={{0,32},{32,64},{64,96},{96,128},{128,160},{160,192},{192,224},{224... | collective-permute-start | bytes 589832 | tf_op jit(solution)/shard_map/ppermute | solution.py:639
  23.8 6.4 %collective-permute-start.1 = (f32[3,8,16,128]{3,2,1,0:T(8,128)S(1)}, f32[3,8,16,128]{3,2,1,0:T(8,128)S(1)}, u32[]{:S(2)}, u32[]{:S(2)}) collective-permute-start(f32[3,8,16,128]{3,2,1,0:T(8,128)S(1)} %pad_maximum_fusion.2), channel_id=1, source_target_pairs={{32,0},{64,32},{96,64},{128,96},{160,128},{192,160},{224,192},{225... | collective-permute-start | bytes 589832 | tf_op jit(solution)/shard_map/ppermute | solution.py:640
  30.3 13.8 %collective-permute-start.3 = (f32[3,8,40,128]{3,2,1,0:T(8,128)S(1)}, f32[3,8,40,128]{3,2,1,0:T(8,128)S(1)}, u32[]{:S(2)}, u32[]{:S(2)}) collective-permute-start(f32[3,8,40,128]{3,2,1,0:T(8,128)S(1)} %pad_maximum_fusion), channel_id=1, source_target_pairs={{4,0},{36,32},{68,64},{100,96},{132,128},{164,160},{196,192},{228,... | collective-permute-start | bytes 1474568 | tf_op jit(solution)/shard_map/ppermute | solution.py:645
  36.4 8.9 %collective-permute-start.2 = (f32[3,8,40,128]{3,2,1,0:T(8,128)S(1)}, f32[3,8,40,128]{3,2,1,0:T(8,128)S(1)}, u32[]{:S(2)}, u32[]{:S(2)}) collective-permute-start(f32[3,8,40,128]{3,2,1,0:T(8,128)S(1)} %pad_maximum_fusion), channel_id=1, source_target_pairs={{0,4},{32,36},{64,68},{96,100},{128,132},{160,164},{192,196},{224,... | collective-permute-start | bytes 1474568 | tf_op jit(solution)/shard_map/ppermute | solution.py:645
  52.4 0.9 copy-start
  53.3 0.9 copy-start.2
  54.2 0.8 copy-start.4
  96.1 1.1 copy-start.3
  97.3 19.1 %copy-start.1 = (f32[2,20,40,128]{3,2,1,0:T(8,128)S(1)}, f32[2,20,40,128]{3,2,1,0:T(8,128)}, u32[]{:S(2)}) copy-start(f32[2,20,40,128]{3,2,1,0:T(8,128)} %copy-done) | copy-start | bytes 2457604
  101.2 3.5 %collective-permute-start.4 = (f32[8,16,128]{2,1,0:T(8,128)S(1)}, f32[8,16,128]{2,1,0:T(8,128)S(1)}, u32[]{:S(2)}, u32[]{:S(2)}) collective-permute-start(f32[8,16,128]{2,1,0:T(8,128)S(1)} %get-tuple-element.56), channel_id=1, source_target_pairs={{0,32},{32,64},{64,96},{96,128},{128,160},{160,192},{192,224},{224... | collective-permute-start | bytes 196616 | tf_op jit(solution)/shard_map/ppermute | solution.py:639
  103.4 5.0 %collective-permute-start.5 = (f32[8,16,128]{2,1,0:T(8,128)S(1)}, f32[8,16,128]{2,1,0:T(8,128)S(1)}, u32[]{:S(2)}, u32[]{:S(2)}) collective-permute-start(f32[8,16,128]{2,1,0:T(8,128)S(1)} %get-tuple-element.56), channel_id=1, source_target_pairs={{32,0},{64,32},{96,64},{128,96},{160,128},{192,160},{224,192},{225... | collective-permute-start | bytes 196616 | tf_op jit(solution)/shard_map/ppermute | solution.py:640
  108.4 6.8 %collective-permute-start.7 = (f32[8,40,128]{2,1,0:T(8,128)S(1)}, f32[8,40,128]{2,1,0:T(8,128)S(1)}, u32[]{:S(2)}, u32[]{:S(2)}) collective-permute-start(f32[8,40,128]{2,1,0:T(8,128)S(1)} %pad_maximum_fusion.3.centre), channel_id=1, source_target_pairs={{4,0},{36,32},{68,64},{100,96},{132,128},{164,160},{196,192},{228,... | collective-permute-start | bytes 491528 | tf_op jit(solution)/shard_map/ppermute | solution.py:645
  112.0 4.4 %collective-permute-start.6 = (f32[8,40,128]{2,1,0:T(8,128)S(1)}, f32[8,40,128]{2,1,0:T(8,128)S(1)}, u32[]{:S(2)}, u32[]{:S(2)}) collective-permute-start(f32[8,40,128]{2,1,0:T(8,128)S(1)} %pad_maximum_fusion.3.centre), channel_id=1, source_target_pairs={{0,4},{32,36},{64,68},{96,100},{128,132},{160,164},{192,196},{224,... | collective-permute-start | bytes 491528 | tf_op jit(solution)/shard_map/ppermute | solution.py:645
  155.8 4.3 %collective-permute-start.8 = (f32[8,16,128]{2,1,0:T(8,128)S(1)}, f32[8,16,128]{2,1,0:T(8,128)S(1)}, u32[]{:S(2)}, u32[]{:S(2)}) collective-permute-start(f32[8,16,128]{2,1,0:T(8,128)S(1)} %get-tuple-element.64), channel_id=1, source_target_pairs={{0,32},{32,64},{64,96},{96,128},{128,160},{160,192},{192,224},{224... | collective-permute-start | bytes 196616 | tf_op jit(solution)/shard_map/ppermute | solution.py:639
  158.8 5.0 %collective-permute-start.9 = (f32[8,16,128]{2,1,0:T(8,128)S(1)}, f32[8,16,128]{2,1,0:T(8,128)S(1)}, u32[]{:S(2)}, u32[]{:S(2)}) collective-permute-start(f32[8,16,128]{2,1,0:T(8,128)S(1)} %get-tuple-element.64), channel_id=1, source_target_pairs={{32,0},{64,32},{96,64},{128,96},{160,128},{192,160},{224,192},{225... | collective-permute-start | bytes 196616 | tf_op jit(solution)/shard_map/ppermute | solution.py:640
  163.8 7.0 %collective-permute-start.11 = (f32[8,40,128]{2,1,0:T(8,128)S(1)}, f32[8,40,128]{2,1,0:T(8,128)S(1)}, u32[]{:S(2)}, u32[]{:S(2)}) collective-permute-start(f32[8,40,128]{2,1,0:T(8,128)S(1)} %pad_maximum_fusion.4.centre), channel_id=1, source_target_pairs={{4,0},{36,32},{68,64},{100,96},{132,128},{164,160},{196,192},{228,... | collective-permute-start | bytes 491528 | tf_op jit(solution)/shard_map/ppermute | solution.py:645
  167.7 4.4 %collective-permute-start.10 = (f32[8,40,128]{2,1,0:T(8,128)S(1)}, f32[8,40,128]{2,1,0:T(8,128)S(1)}, u32[]{:S(2)}, u32[]{:S(2)}) collective-permute-start(f32[8,40,128]{2,1,0:T(8,128)S(1)} %pad_maximum_fusion.4.centre), channel_id=1, source_target_pairs={{0,4},{32,36},{64,68},{96,100},{128,132},{160,164},{192,196},{224,... | collective-permute-start | bytes 491528 | tf_op jit(solution)/shard_map/ppermute | solution.py:645
  214.8 4.2 %collective-permute-start.12 = (f32[8,16,128]{2,1,0:T(8,128)S(1)}, f32[8,16,128]{2,1,0:T(8,128)S(1)}, u32[]{:S(2)}, u32[]{:S(2)}) collective-permute-start(f32[8,16,128]{2,1,0:T(8,128)S(1)} %get-tuple-element.73), channel_id=1, source_target_pairs={{0,32},{32,64},{64,96},{96,128},{128,160},{160,192},{192,224},{224... | collective-permute-start | bytes 196616 | tf_op jit(solution)/shard_map/ppermute | solution.py:639
  217.6 5.0 %collective-permute-start.13 = (f32[8,16,128]{2,1,0:T(8,128)S(1)}, f32[8,16,128]{2,1,0:T(8,128)S(1)}, u32[]{:S(2)}, u32[]{:S(2)}) collective-permute-start(f32[8,16,128]{2,1,0:T(8,128)S(1)} %get-tuple-element.73), channel_id=1, source_target_pairs={{32,0},{64,32},{96,64},{128,96},{160,128},{192,160},{224,192},{225... | collective-permute-start | bytes 196616 | tf_op jit(solution)/shard_map/ppermute | solution.py:640
  222.7 7.1 %collective-permute-start.15 = (f32[8,40,128]{2,1,0:T(8,128)S(1)}, f32[8,40,128]{2,1,0:T(8,128)S(1)}, u32[]{:S(2)}, u32[]{:S(2)}) collective-permute-start(f32[8,40,128]{2,1,0:T(8,128)S(1)} %pad_maximum_fusion.5.centre), channel_id=1, source_target_pairs={{4,0},{36,32},{68,64},{100,96},{132,128},{164,160},{196,192},{228,... | collective-permute-start | bytes 491528 | tf_op jit(solution)/shard_map/ppermute | solution.py:645
  226.4 4.6 %collective-permute-start.14 = (f32[8,40,128]{2,1,0:T(8,128)S(1)}, f32[8,40,128]{2,1,0:T(8,128)S(1)}, u32[]{:S(2)}, u32[]{:S(2)}) collective-permute-start(f32[8,40,128]{2,1,0:T(8,128)S(1)} %pad_maximum_fusion.5.centre), channel_id=1, source_target_pairs={{0,4},{32,36},{64,68},{96,100},{128,132},{160,164},{192,196},{224,... | collective-permute-start | bytes 491528 | tf_op jit(solution)/shard_map/ppermute | solution.py:645
  271.4 11.0 %collective-permute-start.19 = (f32[1,16,128]{2,1,0:T(8,128)S(1)}, f32[1,16,128]{2,1,0:T(8,128)S(1)}, u32[]{:S(2)}, u32[]{:S(2)}) collective-permute-start(f32[1,16,128]{2,1,0:T(8,128)S(1)} %slice.90), channel_id=1, source_target_pairs={{4,0},{36,32},{68,64},{100,96},{132,128},{164,160},{196,192},{228,... | collective-permute-start | bytes 24584 | tf_op jit(solution)/shard_map/ppermute | solution.py:645
  273.3 9.0 %collective-permute-start.18 = (f32[1,16,128]{2,1,0:T(8,128)S(1)}, f32[1,16,128]{2,1,0:T(8,128)S(1)}, u32[]{:S(2)}, u32[]{:S(2)}) collective-permute-start(f32[1,16,128]{2,1,0:T(8,128)S(1)} %slice.90), channel_id=1, source_target_pairs={{0,4},{32,36},{64,68},{96,100},{128,132},{160,164},{192,196},{224,... | collective-permute-start | bytes 24584 | tf_op jit(solution)/shard_map/ppermute | solution.py:645
  277.0 5.5 %collective-permute-start.17 = (f32[8,8,128]{2,1,0:T(8,128)S(1)}, f32[8,8,128]{2,1,0:T(8,128)S(1)}, u32[]{:S(2)}, u32[]{:S(2)}) collective-permute-start(f32[8,8,128]{2,1,0:T(8,128)S(1)} %get-tuple-element.100), channel_id=1, source_target_pairs={{32,0},{64,32},{96,64},{128,96},{160,128},{192,160},{224,192},{225... | collective-permute-start | bytes 98312 | tf_op jit(solution)/shard_map/ppermute | solution.py:650
  278.3 5.0 %collective-permute-start.16 = (f32[8,8,128]{2,1,0:T(8,128)S(1)}, f32[8,8,128]{2,1,0:T(8,128)S(1)}, u32[]{:S(2)}, u32[]{:S(2)}) collective-permute-start(f32[8,8,128]{2,1,0:T(8,128)S(1)} %get-tuple-element.101), channel_id=1, source_target_pairs={{0,32},{32,64},{64,96},{96,128},{128,160},{160,192},{192,224},{224... | collective-permute-start | bytes 98312 | tf_op jit(solution)/shard_map/ppermute | solution.py:649
  283.3 23.2 %copy-start.5 = (f32[3,9,40,128]{3,2,1,0:T(8,128)S(1)}, f32[3,9,40,128]{3,2,1,0:T(8,128)}, u32[]{:S(2)}) copy-start(f32[3,9,40,128]{3,2,1,0:T(8,128)} %copy-done.4) | copy-start | bytes 1658884
  320.6 22.7 %all-to-all-start.8 = ((f32[256,1,256]{2,1,0:T(1,128)}), f32[256,1,256]{2,1,0:T(1,128)S(1)}, u32[]{:S(2)}, u32[]{:S(2)}) async-start(f32[256,1,256]{2,1,0:T(1,128)} %broadcast_in_dim.31), calls=%async_computation.8 | async-start | bytes 524288 | tf_op jit(solution)/shard_map/all_to_all | solution.py:735
